TPU v7x, 8 devices: a whole 2x2x1 slice. The times are simulated.
8 devices in a mesh: ep: 8 (over z, y, x, core).
Axes of the slice: x: 2, y: 2, z: 1, core: 2. Of those that a mesh axis runs over, the one named last changes fastest.
Arguments:
- x_tokens: bfloat16 [65536, 768], P('ep')
- w_router: float32 [768, 16], replicated
- expert_idx: int32 [65536], P('ep')
- w_in: bfloat16 [16, 768, 3072], P('ep')
- w_out: bfloat16 [16, 3072, 768], P('ep')
- grad_y: bfloat16 [65536, 768], P('ep')
Outputs:
- output 1: bfloat16 [65536, 768], P('ep')
- output 2: float32 [16, 768, 3072], P('ep')
- output 3: float32 [16, 3072, 768], P('ep')
- output 4: float32 [768, 16], replicated
- output 5: float32 [], replicated
- output 6: float32 [], replicated
All inputs are finite; a program needn't handle non-finite values.
Results may differ from a plain program's by a relative error of at most 0.0122261.
Values are sent between devices in bfloat16 or wider.
A program may use at most 1 GiB of HBM per device.

v0:
```python
import jax
import jax.numpy as jnp
from jax import lax
from jax.sharding import PartitionSpec as P

AUX_WEIGHT = 0.01
Z_WEIGHT = 0.001


def route_slots(idx_group, num_experts, capacity):
    tokens = idx_group.shape[0]
    n_slots = num_experts * capacity
    onehot = (idx_group[:, None] == jnp.arange(num_experts, dtype=jnp.int32)[None, :]).astype(jnp.int32)
    position = jnp.sum(jnp.cumsum(onehot, axis=0) * onehot, axis=1) - 1
    tok_slot = jnp.where(position < capacity, idx_group * capacity + position, n_slots)
    slot_tok = jnp.full((n_slots,), tokens, jnp.int32).at[tok_slot].set(jnp.arange(tokens, dtype=jnp.int32), mode='drop')
    return onehot.astype(jnp.float32), tok_slot, slot_tok


def gather_rows(source, row_index):
    return jnp.take(source, row_index, axis=0, mode='fill', fill_value=0)


def router_grad(router_prob, onehot, gate_val, d_gate, log_norm, aux_vec, z_coef):
    spread = jnp.sum(router_prob * aux_vec, axis=-1, keepdims=True)
    return ((gate_val * d_gate)[..., None] * (onehot - router_prob)
            + router_prob * (aux_vec - spread)
            + (z_coef * log_norm)[..., None] * router_prob)


def solution(mesh):
    n_dev = mesh.shape['ep']

    def expert_layer(x_tokens, w_router, expert_idx, w_in, w_out, grad_y):
        tokens, d_model = x_tokens.shape
        n_local = w_in.shape[0]
        num_experts = n_local * n_dev
        capacity = (5 * tokens + 4 * num_experts - 1) // (4 * num_experts)
        total_tok = tokens * n_dev
        onehot, tok_slot, slot_tok = route_slots(expert_idx, num_experts, capacity)
        logits = jnp.dot(x_tokens, w_router, preferred_element_type=jnp.float32)
        router_prob = jax.nn.softmax(logits, axis=-1)
        log_norm = jax.nn.logsumexp(logits, axis=-1)
        gate_val = jnp.sum(router_prob * onehot, axis=-1)
        route_stats = jnp.concatenate([jnp.sum(onehot, axis=0), jnp.sum(router_prob, axis=0), jnp.sum(log_norm * log_norm)[None]])
        route_stats = lax.psum(route_stats, 'ep')

        sent_rows = gather_rows(x_tokens, slot_tok).reshape(n_dev, n_local, capacity, d_model)
        recv_rows = lax.all_to_all(sent_rows, 'ep', 0, 0, tiled=True)
        pre_act = jnp.einsum('pecd,edf->pecf', recv_rows, w_in, preferred_element_type=jnp.float32)
        hidden = jnp.maximum(pre_act, 0.0).astype(jnp.bfloat16)
        expert_out = jnp.einsum('pecf,efd->pecd', hidden, w_out, preferred_element_type=jnp.float32).astype(jnp.bfloat16)
        back_out = lax.all_to_all(expert_out, 'ep', 0, 0, tiled=True).reshape(num_experts * capacity, d_model)
        out_tok = gather_rows(back_out, tok_slot)
        gy_f32 = grad_y.astype(jnp.float32)
        d_gate = jnp.sum(out_tok.astype(jnp.float32) * gy_f32, axis=-1)

        scaled = (gate_val[:, None] * gy_f32).astype(jnp.bfloat16)
        sent_grad = gather_rows(scaled, slot_tok).reshape(n_dev, n_local, capacity, d_model)
        recv_grad = lax.all_to_all(sent_grad, 'ep', 0, 0, tiled=True)
        d_hidden = jnp.einsum('pecd,efd->pecf', recv_grad, w_out, preferred_element_type=jnp.float32)
        d_pre = jnp.where(hidden > 0, d_hidden, 0.0).astype(jnp.bfloat16)
        grad_w_out = jnp.einsum('pecf,pecd->efd', hidden, recv_grad, preferred_element_type=jnp.float32)
        grad_w_in = jnp.einsum('pecd,pecf->edf', recv_rows, d_pre, preferred_element_type=jnp.float32)
        d_rows = jnp.einsum('pecf,edf->pecd', d_pre, w_in, preferred_element_type=jnp.float32).astype(jnp.bfloat16)
        back_grad = lax.all_to_all(d_rows, 'ep', 0, 0, tiled=True).reshape(num_experts * capacity, d_model)
        dx_expert = gather_rows(back_grad, tok_slot)

        load_frac = route_stats[:num_experts] / total_tok
        mean_prob = route_stats[num_experts:2 * num_experts] / total_tok
        aux_loss = AUX_WEIGHT * num_experts * jnp.sum(load_frac * mean_prob)
        z_loss = Z_WEIGHT * route_stats[2 * num_experts] / total_tok
        aux_vec = AUX_WEIGHT * num_experts * load_frac / total_tok
        d_logits = router_grad(router_prob, onehot, gate_val, d_gate, log_norm, aux_vec, 2.0 * Z_WEIGHT / total_tok)
        dx_router = jnp.einsum('se,de->sd', d_logits, w_router)
        grad_x = (dx_expert.astype(jnp.float32) + dx_router).astype(jnp.bfloat16)
        grad_w_router = lax.psum(jnp.einsum('sd,se->de', x_tokens, d_logits, preferred_element_type=jnp.float32), 'ep')
        return grad_x, grad_w_in, grad_w_out, grad_w_router, aux_loss, z_loss

    return jax.shard_map(expert_layer, mesh=mesh,
                         in_specs=(P('ep', None), P(None, None), P('ep'), P('ep', None, None), P('ep', None, None), P('ep', None)),
                         out_specs=(P('ep', None), P('ep', None, None), P('ep', None, None), P(None, None), P(), P()),
                         check_vma=False)
```

profile of v0, /device:TPU:1, one launch (start us, length us, event | category | flops | bytes accessed | tf_op | source)
XLA Modules:
  0.0 1283.7 jit_solution(9847303963493053287)
XLA Ops:
  0.6 0.8 fusion.22
  1.5 4.8 reduce-window.6
  7.2 1.1 fusion.21
  8.3 1.4 compare_and_fusion.1
  9.7 30.5 %scatter_custom_fusion = s32[10240]{0:T(1024)S(1)} fusion(s32[8192]{0:T(1024)S(1)} %get-tuple-element.13, s32[8192]{0:T(1024)S(1)} %iota.11, s32[]{:T(128)} %constant.17.clone.1), kind=kCustom, calls=%fused_computation.65 | custom fusion | bytes 40964 | tf_op jit(solution)/shard_map/scatter | solution.py:16
  40.3 52.2 %gather_fusion = bf16[10240,768]{1,0:T(8,128)(2,1)} fusion(bf16[8192,768]{1,0:T(8,128)(2,1)} %param.10, s32[10240]{0:T(1024)S(1)} %fusion.35), kind=kCustom, calls=%fused_computation.clone | custom fusion | bytes 31498240 | tf_op jit(solution)/shard_map/jit(_take)/gather | solution.py:21
  92.5 10.0 broadcast_select_fusion.1
  102.5 175.3 %all_to_all.20 = bf16[8,2,640,768]{3,2,1,0:T(8,128)(2,1)} all-to-all(bf16[8,2,640,768]{3,2,1,0:T(8,128)(2,1)S(1)} %bitcast.62), channel_id=1, replica_groups=mesh['ep'=8] {'ep'}, dimensions={0} | all-to-all | bytes 31457280 | tf_op jit(solution)/shard_map/all_to_all | solution.py:49
  277.8 58.8 %fusion.1 = bf16[8,2,640,3072]{3,2,0,1:T(8,128)(2,1)} fusion(bf16[8,2,640,768]{3,2,1,0:T(8,128)(2,1)} %all_to_all.20, bf16[2,768,3072]{2,1,0:T(8,128)(2,1)} %param.13), kind=kOutput, calls=%fused_computation.8 | convolution fusion | flops 48381296640 | bytes 88080384 | tf_op jit(solution)/shard_map/pecd,edf->pecf/dot_general | solution.py:50
  336.6 56.0 %convert_bitcast_fusion = bf16[8,2,640,768]{3,2,0,1:T(8,128)(2,1)S(1)} fusion(bf16[8,2,640,3072]{3,2,0,1:T(8,128)(2,1)} %fusion.1, bf16[2,3072,768]{2,1,0:T(8,128)(2,1)} %param.14), kind=kOutput, calls=%fused_computation.17 | convolution fusion | flops 48326246400 | bytes 88080384 | tf_op jit(solution)/shard_map/pecf,efd->pecd/dot_general | solution.py:52
  392.6 6.3 copy.23
  398.9 6.0 all-to-all-start.3
  404.9 8.0 fusion.41
  414.1 0.7 pad_maximum_fusion
  414.8 177.9 %psum.14 = f32[33]{0:T(128)S(1)} all-reduce(f32[33]{0:T(128)S(1)} %pad_maximum_fusion), channel_id=1, replica_groups=mesh['ep'=8] {'ep'}, use_global_device_ids=true, to_apply=%region_12.15 | all-reduce | flops 33 | bytes 264 | tf_op jit(solution)/shard_map/psum | solution.py:46
  592.7 0.7 multiply_reduce_fusion.3
  593.8 44.5 %gather_fusion.3 = bf16[8192,768]{1,0:T(8,128)(2,1)} fusion(bf16[10240,768]{1,0:T(8,128)(2,1)} %bitcast.14, s32[8192]{0:T(1024)S(1)} %broadcast_clamp_fusion), kind=kCustom, calls=%fused_computation.3.clone | custom fusion | bytes 25198592 | tf_op jit(solution)/shard_map/jit(_take)/gather | solution.py:21
  638.3 17.3 %fusion.5 = (f32[8192]{0:T(1024)S(1)}, bf16[8192,768]{1,0:T(8,128)(2,1)}) fusion(bf16[8192,768]{1,0:T(8,128)(2,1)} %param.15, bf16[8192,768]{1,0:T(8,128)(2,1)} %gather_fusion.3, pred[8192]{0:T(1024)(128)(4,1)S(1)} %copy-done.23, f32[8192]{0:T(1024)S(1)} %get-tuple-element.9), kind=kLoop, calls=%fused_computation.14 | loop fusion | flops 44032000 | bytes 37822464 | tf_op jit(solution)/shard_map/reduce_sum | solution.py:56
  655.6 52.2 %gather_fusion.1 = bf16[10240,768]{1,0:T(8,128)(2,1)} fusion(bf16[8192,768]{1,0:T(8,128)(2,1)} %get-tuple-element.15, s32[10240]{0:T(1024)S(1)} %copy-done.10), kind=kCustom, calls=%fused_computation.2.clone | custom fusion | bytes 31498240 | tf_op jit(solution)/shard_map/jit(_take)/gather | solution.py:21
  707.8 15.0 %broadcast_select_fusion = bf16[10240,768]{1,0:T(8,128)(2,1)} fusion(bf16[10240,768]{1,0:T(8,128)(2,1)} %gather_fusion.1, pred[10240]{0:T(1024)(128)(4,1)S(1)} %copy-done.22), kind=kLoop, calls=%fused_computation.19 | loop fusion | flops 7864320 | bytes 31467520 | tf_op jit(solution)/shard_map/jit(_take)/select_n | solution.py:21
  722.9 5.8 all-to-all-start.1
  730.6 6.4 convolution_bitcast_fusion
  737.0 180.2 %psum.15 = f32[768,16]{0,1:T(8,128)} all-reduce(f32[768,16]{0,1:T(8,128)S(1)} %convolution_bitcast_fusion), channel_id=1, replica_groups=mesh['ep'=8] {'ep'}, use_global_device_ids=true, to_apply=%region_14.17 | all-reduce | flops 12288 | bytes 98304 | tf_op jit(solution)/shard_map/psum | solution.py:77
  917.2 62.5 %fusion = bf16[8,2,640,3072]{3,2,0,1:T(8,128)(2,1)} fusion(bf16[8,2,640,3072]{3,2,0,1:T(8,128)(2,1)} %fusion.1, bf16[8,2,640,768]{3,2,1,0:T(8,128)(2,1)} %all-to-all-done.1, bf16[2,3072,768]{2,1,0:T(8,128)(2,1)} %param.14), kind=kOutput, calls=%fused_computation.6 | convolution fusion | flops 48412753920 | bytes 150994944 | tf_op jit(solution)/shard_map/pecd,efd->pecf/dot_general | solution.py:61
  979.7 57.5 %convert_bitcast_fusion.1 = bf16[8,2,640,768]{3,2,0,1:T(8,128)(2,1)} fusion(bf16[8,2,640,3072]{3,2,0,1:T(8,128)(2,1)} %fusion, bf16[2,768,3072]{2,1,0:T(8,128)(2,1)} %param.13), kind=kOutput, calls=%fused_computation.18 | convolution fusion | flops 48326246400 | bytes 88080384 | tf_op jit(solution)/shard_map/pecf,edf->pecd/dot_general | solution.py:65
  1037.2 13.2 %copy.22 = bf16[8,2,640,768]{3,2,1,0:T(8,128)(2,1)} copy(bf16[8,2,640,768]{3,2,0,1:T(8,128)(2,1)} %convert_bitcast_fusion.1) | data formatting | bytes 31457280 | tf_op jit(solution)/shard_map/convert_element_type | solution.py:65
  1050.4 5.7 all-to-all-start.2
  1056.1 58.3 %fusion.17 = f32[2,768,3072]{2,1,0:T(8,128)} fusion(bf16[8,2,640,768]{3,2,1,0:T(8,128)(2,1)} %all_to_all.20, bf16[8,2,640,3072]{3,2,0,1:T(8,128)(2,1)} %fusion), kind=kOutput, calls=%fused_computation.29 | convolution fusion | flops 48318382080 | bytes 97517568 | tf_op jit(solution)/shard_map/pecd,pecf->edf/dot_general | solution.py:64
  1114.5 58.5 %fusion.14 = f32[2,3072,768]{2,1,0:T(8,128)} fusion(bf16[8,2,640,3072]{3,2,0,1:T(8,128)(2,1)} %fusion.1, bf16[8,2,640,768]{3,2,1,0:T(8,128)(2,1)} %all-to-all-done.1), kind=kOutput, calls=%fused_computation.28 | convolution fusion | flops 48318382080 | bytes 97517568 | tf_op jit(solution)/shard_map/pecf,pecd->efd/dot_general | solution.py:63
  1173.0 52.2 %all-to-all-done.2 = bf16[8,2,640,768]{3,2,1,0:T(8,128)(2,1)} async-done(((bf16[8,2,640,768]{3,2,1,0:T(8,128)(2,1)}), bf16[8,2,640,768]{3,2,1,0:T(8,128)(2,1)}, u32[]{:S(2)}, u32[]{:S(2)}) %all-to-all-start.2) | async-done | bytes 15728672 | tf_op jit(solution)/shard_map/all_to_all | solution.py:66
  1225.3 44.6 %gather_fusion.2 = bf16[8192,768]{1,0:T(8,128)(2,1)} fusion(bf16[10240,768]{1,0:T(8,128)(2,1)} %bitcast.11, s32[8192]{0:T(1024)S(1)} %copy-done.12), kind=kCustom, calls=%fused_computation.1.clone | custom fusion | bytes 25198592 | tf_op jit(solution)/shard_map/jit(_take)/gather | solution.py:21
  1269.9 11.3 add_convert_fusion
  (70 shorter events, 3.1 us)
Async XLA Ops:
  0.6 404.2 %copy-start = (f32[768,16]{0,1:T(8,128)S(1)}, f32[768,16]{0,1:T(8,128)}, u32[]{:S(2)}) copy-start(f32[768,16]{0,1:T(8,128)} %param.11) | copy-start | bytes 147460
  9.7 30.5 %copy-start.19 = (s32[8192]{0:T(1024)}, s32[8192]{0:T(1024)S(1)}, u32[]{:S(2)}) copy-start(s32[8192]{0:T(1024)S(1)} %get-tuple-element.13) | copy-start | bytes 98308
  40.2 52.3 %copy-start.21 = (pred[10240]{0:T(1024)(128)(4,1)}, pred[10240]{0:T(1024)(128)(4,1)S(1)}, u32[]{:S(2)}) copy-start(pred[10240]{0:T(1024)(128)(4,1)S(1)} %compare_and_fusion) | copy-start | bytes 30724
  40.3 52.3 %copy-start.9 = (s32[10240]{0:T(1024)}, s32[10240]{0:T(1024)S(1)}, u32[]{:S(2)}) copy-start(s32[10240]{0:T(1024)S(1)} %fusion.35) | copy-start | bytes 122884
  398.9 194.9 %all-to-all-start.3 = ((bf16[8,2,640,768]{3,2,1,0:T(8,128)(2,1)}), bf16[8,2,640,768]{3,2,1,0:T(8,128)(2,1)}, u32[]{:S(2)}, u32[]{:S(2)}) async-start(bf16[8,2,640,768]{3,2,1,0:T(8,128)(2,1)} %copy.23), calls=%async_computation.3 | async-start | bytes 31457280 | tf_op jit(solution)/shard_map/all_to_all | solution.py:53
  404.9 8.2 copy-start.5
  404.9 188.8 %copy-start.20 = (s32[8192]{0:T(1024)S(1)}, s32[8192]{0:T(1024)}, u32[]{:S(2)}) copy-start(s32[8192]{0:T(1024)} %copy-done.19) | copy-start | bytes 98308
  412.9 317.7 %copy-start.1 = (f32[8192,16]{0,1:T(8,128)}, f32[8192,16]{0,1:T(8,128)S(1)}, u32[]{:S(2)}) copy-start(f32[8192,16]{0,1:T(8,128)S(1)} %get-tuple-element.21) | copy-start | bytes 1572868
  412.9 317.7 %copy-start.3 = (f32[8192]{0:T(1024)}, f32[8192]{0:T(1024)S(1)}, u32[]{:S(2)}) copy-start(f32[8192]{0:T(1024)S(1)} %get-tuple-element.20) | copy-start | bytes 98308
  413.0 317.5 %copy-start.7 = (f32[8192]{0:T(1024)}, f32[8192]{0:T(1024)S(1)}, u32[]{:S(2)}) copy-start(f32[8192]{0:T(1024)S(1)} %fusion.24) | copy-start | bytes 98308
  414.1 316.5 %copy-start.13 = (f32[8192]{0:T(1024)}, f32[8192]{0:T(1024)S(1)}, u32[]{:S(2)}) copy-start(f32[8192]{0:T(1024)S(1)} %get-tuple-element.16) | copy-start | bytes 98308
  593.4 137.2 %copy-start.25 = (f32[16]{0:T(128)}, f32[16]{0:T(128)S(1)}, u32[]{:S(2)}) copy-start(f32[16]{0:T(128)S(1)} %get-tuple-element.19) | copy-start | bytes 196
  593.7 136.9 %copy-start.15 = (f32[8192]{0:T(1024)}, f32[8192]{0:T(1024)S(1)}, u32[]{:S(2)}) copy-start(f32[8192]{0:T(1024)S(1)} %get-tuple-element.8) | copy-start | bytes 98308
  593.8 44.6 %copy-start.11 = (s32[8192]{0:T(1024)}, s32[8192]{0:T(1024)S(1)}, u32[]{:S(2)}) copy-start(s32[8192]{0:T(1024)S(1)} %broadcast_clamp_fusion) | copy-start | bytes 98308
  593.8 44.6 %copy-start.23 = (pred[8192]{0:T(1024)(128)(4,1)S(1)}, pred[8192]{0:T(1024)(128)(4,1)}, u32[]{:S(2)}) copy-start(pred[8192]{0:T(1024)(128)(4,1)} %get-tuple-element.12) | copy-start | bytes 24580
  638.3 17.3 %copy-start.10 = (s32[10240]{0:T(1024)S(1)}, s32[10240]{0:T(1024)}, u32[]{:S(2)}) copy-start(s32[10240]{0:T(1024)} %copy-done.9) | copy-start | bytes 122884
  655.6 52.2 %copy-start.22 = (pred[10240]{0:T(1024)(128)(4,1)S(1)}, pred[10240]{0:T(1024)(128)(4,1)}, u32[]{:S(2)}) copy-start(pred[10240]{0:T(1024)(128)(4,1)} %copy-done.21) | copy-start | bytes 30724
  722.9 194.3 %all-to-all-start.1 = ((bf16[8,2,640,768]{3,2,1,0:T(8,128)(2,1)}), bf16[8,2,640,768]{3,2,1,0:T(8,128)(2,1)}, u32[]{:S(2)}, u32[]{:S(2)}) async-start(bf16[8,2,640,768]{3,2,1,0:T(8,128)(2,1)} %bitcast.61), calls=%async_computation.1 | async-start | bytes 31457280 | tf_op jit(solution)/shard_map/all_to_all | solution.py:60
  730.5 249.1 %copy-start.17 = (f32[8192]{0:T(1024)}, f32[8192]{0:T(1024)S(1)}, u32[]{:S(2)}) copy-start(f32[8192]{0:T(1024)S(1)} %mul.78) | copy-start | bytes 98308
  1050.4 174.8 %all-to-all-start.2 = ((bf16[8,2,640,768]{3,2,1,0:T(8,128)(2,1)}), bf16[8,2,640,768]{3,2,1,0:T(8,128)(2,1)}, u32[]{:S(2)}, u32[]{:S(2)}) async-start(bf16[8,2,640,768]{3,2,1,0:T(8,128)(2,1)} %copy.22), calls=%async_computation.2 | async-start | bytes 31457280 | tf_op jit(solution)/shard_map/all_to_all | solution.py:66
  1114.5 110.7 %copy-start.12 = (s32[8192]{0:T(1024)S(1)}, s32[8192]{0:T(1024)}, u32[]{:S(2)}) copy-start(s32[8192]{0:T(1024)} %copy-done.11) | copy-start | bytes 98308
  1225.2 44.7 %copy-start.2 = (f32[8192,16]{0,1:T(8,128)S(1)}, f32[8192,16]{0,1:T(8,128)}, u32[]{:S(2)}) copy-start(f32[8192,16]{0,1:T(8,128)} %copy-done.1) | copy-start | bytes 1572868
  1225.2 44.7 %copy-start.4 = (f32[8192]{0:T(1024)S(1)}, f32[8192]{0:T(1024)}, u32[]{:S(2)}) copy-start(f32[8192]{0:T(1024)} %copy-done.3) | copy-start | bytes 98308
  1225.2 44.7 %copy-start.6 = (s32[8192]{0:T(1024)S(1)}, s32[8192]{0:T(1024)}, u32[]{:S(2)}) copy-start(s32[8192]{0:T(1024)} %param.12) | copy-start | bytes 98308
  1225.2 44.7 %copy-start.8 = (f32[8192]{0:T(1024)S(1)}, f32[8192]{0:T(1024)}, u32[]{:S(2)}) copy-start(f32[8192]{0:T(1024)} %copy-done.7) | copy-start | bytes 98308
  1225.2 44.7 %copy-start.14 = (f32[8192]{0:T(1024)S(1)}, f32[8192]{0:T(1024)}, u32[]{:S(2)}) copy-start(f32[8192]{0:T(1024)} %copy-done.13) | copy-start | bytes 98308
  1225.3 44.7 %copy-start.16 = (f32[8192]{0:T(1024)S(1)}, f32[8192]{0:T(1024)}, u32[]{:S(2)}) copy-start(f32[8192]{0:T(1024)} %copy-done.15) | copy-start | bytes 98308
  1225.3 44.7 %copy-start.18 = (f32[8192]{0:T(1024)S(1)}, f32[8192]{0:T(1024)}, u32[]{:S(2)}) copy-start(f32[8192]{0:T(1024)} %copy-done.17) | copy-start | bytes 98308
  1225.3 44.7 %copy-start.24 = (pred[8192]{0:T(1024)(128)(4,1)S(1)}, pred[8192]{0:T(1024)(128)(4,1)}, u32[]{:S(2)}) copy-start(pred[8192]{0:T(1024)(128)(4,1)} %get-tuple-element.12) | copy-start | bytes 24580
  1225.3 44.7 %copy-start.26 = (f32[16]{0:T(128)S(1)}, f32[16]{0:T(128)}, u32[]{:S(2)}) copy-start(f32[16]{0:T(128)} %copy-done.25) | copy-start | bytes 196
where the time goes:
time: 1290 us; the launch traced here: 1280 us
  blocking collectives  533 us (41%)
  matrix products  377 us (29%)
  local copies, waits for them, and re-layouts  245 us (19%)
  other arithmetic  53.6 us (4%)
  waiting for transfers between devices  52.2 us (4%)
  starting transfers between devices  17.5 us (1%)
    gather x4, local copies, waits for them, and re-layouts, gather_rows(): return jnp.take(source, row_index, axis=0, mode='fill', fill_value=0)  194 us
    psum x1, blocking collectives, expert_layer(): lax.psum(jnp.einsum('sd,se->de', x_tokens, d_logits, preferred_element_ty...  180 us
    psum x1, blocking collectives, expert_layer(): route_stats = lax.psum(route_stats, 'ep')  178 us
    all_to_all x1, blocking collectives, expert_layer(): recv_rows = lax.all_to_all(sent_rows, 'ep', 0, 0, tiled=True)  175 us
    dot_general x1, matrix products, expert_layer(): jnp.einsum('pecd,efd->pecf', recv_grad, w_out, preferred_element_type=jnp...  62.5 us
    dot_general x1, matrix products, expert_layer(): jnp.einsum('pecd,edf->pecf', recv_rows, w_in, preferred_element_type=jnp....  58.8 us
    dot_general x1, matrix products, expert_layer(): jnp.einsum('pecf,pecd->efd', hidden, recv_grad, preferred_element_type=jn...  58.5 us
    dot_general x1, matrix products, expert_layer(): jnp.einsum('pecd,pecf->edf', recv_rows, d_pre, preferred_element_type=jnp...  58.3 us
  transfers between devices with their start and end apart: 3, of which 1 were waited for; matrix products, arithmetic and copies ran while one was open for 10% of the time, Pallas kernels for 0%

commit v1 on v0

--- a/solution.py
+++ b/solution.py
@@ -1,10 +1,16 @@
 import jax
 import jax.numpy as jnp
 from jax import lax
+from jax.experimental import pallas as pl
+from jax.experimental.pallas import tpu as pltpu
 from jax.sharding import PartitionSpec as P
 
 AUX_WEIGHT = 0.01
 Z_WEIGHT = 0.001
+MESH = pl.DeviceIdType.MESH
+F32 = jnp.float32
+BF16 = jnp.bfloat16
+LANES = 128
 
 
 def route_slots(idx_group, num_experts, capacity):
@@ -28,6 +34,249 @@
             + (z_coef * log_norm)[..., None] * router_prob)
 
 
+def split3(w):
+    hi = lax.reduce_precision(w, 8, 7)
+    mid = lax.reduce_precision(w - hi, 8, 7)
+    return hi.astype(BF16), mid.astype(BF16), (w - hi - mid).astype(BF16)
+
+
+def nt(a, b):
+    return lax.dot_general(a, b, (((1,), (1,)), ((), ())), preferred_element_type=F32)
+
+
+def nn(a, b):
+    return jnp.dot(a, b, preferred_element_type=F32)
+
+
+def expert_kernel(n_dev, n_local, num_experts, blk, xs, dys, wr, w_in, w_out,
+                  xr, dyr, dsend, dback, gback, gwin, gwout_t,
+                  xv, dyv, gv, x_t, g_t, win_v, wout_v, acc_in, acc_out, o_acc, r_acc, r_out, g_all,
+                  x_send, x_recv, dy_send, dy_recv, r_send, r_recv, s_send, s_recv, ld_sem, st_sem, w_sem, flush_sem, own_sem):
+    me = lax.axis_index('ep')
+    n_blk = w_in.shape[2] // blk
+    n_chunk = n_local * n_dev
+
+    def peer_of(k):
+        out = 0
+        bit = 1
+        while bit < n_dev:
+            out = out + bit * (((me // bit) + (k // bit)) % 2)
+            bit *= 2
+        return out
+
+    barrier = pltpu.get_barrier_semaphore()
+    for k in range(1, n_dev):
+        pl.semaphore_signal(barrier, inc=1, device_id=(peer_of(k),), device_id_type=MESH)
+    pl.semaphore_wait(barrier, n_dev - 1)
+
+    def x_copy(k, e):
+        p = peer_of(k)
+        return pltpu.make_async_remote_copy(xs.at[p, e], xr.at[me, e], x_send.at[e, k], x_recv.at[e, k], device_id=(p,), device_id_type=MESH)
+
+    def dy_copy(k, e):
+        p = peer_of(k)
+        return pltpu.make_async_remote_copy(dys.at[p, e], dyr.at[me, e], dy_send.at[e, k], dy_recv.at[e, k], device_id=(p,), device_id_type=MESH)
+
+    def r_copy(k, e):
+        p = peer_of(k)
+        return pltpu.make_async_remote_copy(dsend.at[p, e], dback.at[me, e], r_send.at[e, k], r_recv.at[e, k], device_id=(p,), device_id_type=MESH)
+
+    def s_copy(k, e):
+        p = peer_of(k)
+        return pltpu.make_async_remote_copy(g_all.at[e, k], gback.at[me, e], s_send.at[e, k], s_recv.at[e, k], device_id=(p,), device_id_type=MESH)
+
+    for e in range(n_local):
+        for k in (1, 2, 4, 6, 3, 5, 7):
+            x_copy(k, e).start()
+            dy_copy(k, e).start()
+
+    order = (0, 1, 2, 4, 6, 3, 5, 7)
+
+    def offset_of(i):
+        k = i * 0
+        for at, val in enumerate(order):
+            k = k + jnp.where(i == at, val, 0)
+        return k
+
+    def load(e, i, slot, do):
+        k = offset_of(i)
+        p = peer_of(k)
+
+        @pl.when(i == 0)
+        def _():
+            do(pltpu.make_async_copy(xs.at[me, e], xv.at[slot], ld_sem.at[slot, 0]))
+            do(pltpu.make_async_copy(dys.at[me, e], dyv.at[slot], ld_sem.at[slot, 1]))
+
+        @pl.when(i > 0)
+        def _():
+            do(pltpu.make_async_copy(xr.at[p, e], xv.at[slot], ld_sem.at[slot, 0]))
+            do(pltpu.make_async_copy(dyr.at[p, e], dyv.at[slot], ld_sem.at[slot, 1]))
+
+    def arrive(e, i):
+        @pl.when(i > 0)
+        def _():
+            k = offset_of(i)
+            x_copy(k, e).wait_recv()
+            dy_copy(k, e).wait_recv()
+
+    def store(c, do):
+        e, i = c // n_dev, c % n_dev
+        k = offset_of(i)
+        p = peer_of(k)
+
+        @pl.when(i == 0)
+        def _():
+            do(pltpu.make_async_copy(r_out.at[c % 2], dback.at[me, e], st_sem.at[c % 2]))
+
+        @pl.when(i > 0)
+        def _():
+            do(pltpu.make_async_copy(r_out.at[c % 2], dsend.at[p, e], st_sem.at[c % 2]))
+
+    def own_g(e):
+        return pltpu.make_async_copy(g_all.at[e, 0], gback.at[me, e], own_sem.at[e])
+
+    def send_back(c):
+        e, i = c // n_dev, c % n_dev
+        k = offset_of(i)
+        store(c, lambda cp: cp.wait())
+
+        @pl.when(i == 0)
+        def _():
+            own_g(e).start()
+
+        @pl.when(i > 0)
+        def _():
+            r_copy(k, e).start()
+            s_copy(k, e).start()
+
+    def weights(e):
+        return (pltpu.make_async_copy(w_in.at[e], win_v, w_sem.at[0]), pltpu.make_async_copy(w_out.at[e], wout_v, w_sem.at[1]))
+
+    def flush(e):
+        return (pltpu.make_async_copy(acc_in, gwin.at[e], flush_sem.at[0]), pltpu.make_async_copy(acc_out, gwout_t.at[e], flush_sem.at[1]))
+
+    for cp in weights(0):
+        cp.start()
+    load(0, 0, 0, lambda cp: cp.start())
+
+    def chunk(c, _):
+        e, i = c // n_dev, c % n_dev
+        k = offset_of(i)
+        slot = c % 2
+
+        @pl.when(i == 0)
+        def _():
+            @pl.when(c > 0)
+            def _():
+                for cp in weights(e):
+                    cp.start()
+                for cp in flush(e - 1):
+                    cp.wait()
+            acc_in[...] = jnp.zeros_like(acc_in)
+            acc_out[...] = jnp.zeros_like(acc_out)
+            for cp in weights(e):
+                cp.wait()
+
+        load(e, i, slot, lambda cp: cp.wait())
+        x = xv[slot]
+        logits = nn(x, wr[0]) + nn(x, wr[1]) + nn(x, wr[2])
+        lane = lax.broadcasted_iota(jnp.int32, logits.shape, 1)
+        logits = jnp.where(lane < num_experts, logits, -1e30)
+        prob = jnp.exp(logits - jnp.max(logits, axis=1, keepdims=True))
+        mine = jnp.sum(jnp.where(lane == me * n_local + e, prob, 0.0), axis=1, keepdims=True)
+        gate = mine / jnp.sum(prob, axis=1, keepdims=True)
+        grad = (gate * dyv[slot].astype(F32)).astype(BF16)
+        gv[...] = grad
+        x_t[...] = x.T
+        g_t[...] = grad.T
+        o_acc[...] = jnp.zeros_like(o_acc)
+        r_acc[...] = jnp.zeros_like(r_acc)
+
+        def block(f, _):
+            @pl.when(f == n_blk - 1)
+            def _():
+                @pl.when(c + 1 < n_chunk)
+                def _():
+                    ne, ni = (c + 1) // n_dev, (c + 1) % n_dev
+                    arrive(ne, ni)
+                    load(ne, ni, 1 - slot, lambda cp: cp.start())
+
+            @pl.when(f == 1)
+            def _():
+                @pl.when(c > 0)
+                def _():
+                    send_back(c - 1)
+
+            cols = pl.ds(pl.multiple_of(f * blk, LANES), blk)
+            win = win_v[:, cols]
+            wout = wout_v[cols, :]
+            hidden = jnp.maximum(nn(xv[slot], win), 0.0).astype(BF16)
+            d_hidden = nt(gv[...], wout)
+            d_pre = jnp.where(hidden > 0, d_hidden, 0.0).astype(BF16)
+            o_acc[...] += nn(hidden, wout)
+            r_acc[...] += nt(d_pre, win)
+            acc_out[:, cols] += nn(g_t[...], hidden)
+            acc_in[:, cols] += nn(x_t[...], d_pre)
+            return 0
+
+        lax.fori_loop(0, n_blk, block, 0)
+        r_out[slot] = r_acc[...].astype(BF16)
+        store(c, lambda cp: cp.start())
+        g_val = jnp.sum(o_acc[...].astype(BF16).astype(F32) * dyv[slot].astype(F32), axis=1, keepdims=True)
+        g_row = jnp.broadcast_to(g_val, (g_val.shape[0], LANES)).T
+        g_all[e, k] = g_row[0:1, :]
+
+        @pl.when(i == n_dev - 1)
+        def _():
+            for cp in flush(e):
+                cp.start()
+        return 0
+
+    lax.fori_loop(0, n_chunk, chunk, 0)
+    send_back(n_chunk - 1)
+    for cp in flush(n_local - 1):
+        cp.wait()
+    for e in range(n_local):
+        own_g(e).wait()
+        for k in range(1, n_dev):
+            x_copy(k, e).wait_send()
+            dy_copy(k, e).wait_send()
+            r_copy(k, e).wait()
+            s_copy(k, e).wait()
+
+
+def expert_exchange(n_dev, xs, dys, wr, w_in, w_out):
+    n_local, d_model, d_ff = w_in.shape
+    cap = xs.shape[2]
+    num_experts = n_dev * n_local
+    blk = d_ff // 4
+    hbm = pl.BlockSpec(memory_space=pl.ANY)
+    vmem = pl.BlockSpec(memory_space=pltpu.VMEM)
+    rows = jax.ShapeDtypeStruct(xs.shape, BF16)
+    g_shape = jax.ShapeDtypeStruct((n_dev, n_local, 1, cap), F32)
+    w_shape = jax.ShapeDtypeStruct((n_local, d_model, d_ff), F32)
+    dma = pltpu.SemaphoreType.DMA
+    pair = (n_local, n_dev)
+    return pl.pallas_call(
+        lambda *refs: expert_kernel(n_dev, n_local, num_experts, blk, *refs),
+        out_shape=(rows, rows, rows, rows, g_shape, w_shape, w_shape),
+        in_specs=[hbm, hbm, vmem, hbm, hbm],
+        out_specs=[hbm] * 7,
+        scratch_shapes=[
+            pltpu.VMEM((2, cap, d_model), BF16), pltpu.VMEM((2, cap, d_model), BF16), pltpu.VMEM((cap, d_model), BF16),
+            pltpu.VMEM((d_model, cap), BF16), pltpu.VMEM((d_model, cap), BF16),
+            pltpu.VMEM((d_model, d_ff), BF16), pltpu.VMEM((d_ff, d_model), BF16),
+            pltpu.VMEM((d_model, d_ff), F32), pltpu.VMEM((d_model, d_ff), F32),
+            pltpu.VMEM((cap, d_model), F32), pltpu.VMEM((cap, d_model), F32),
+            pltpu.VMEM((2, cap, d_model), BF16), pltpu.VMEM((n_local, n_dev, 1, cap), F32),
+            dma(pair), dma(pair), dma(pair), dma(pair), dma(pair), dma(pair), dma(pair), dma(pair),
+            dma((2, 2)), dma((2,)), dma((2,)), dma((2,)), dma((n_local,)),
+        ],
+        compiler_params=pltpu.CompilerParams(collective_id=0, has_side_effects=True, vmem_limit_bytes=63 * 2 ** 20),
+        name='expert_exchange',
+    )(xs, dys, wr, w_in, w_out)
+
+
 def solution(mesh):
     n_dev = mesh.shape['ep']
 
@@ -38,6 +287,10 @@
         capacity = (5 * tokens + 4 * num_experts - 1) // (4 * num_experts)
         total_tok = tokens * n_dev
         onehot, tok_slot, slot_tok = route_slots(expert_idx, num_experts, capacity)
+        xs = gather_rows(x_tokens, slot_tok).reshape(n_dev, n_local, capacity, d_model)
+        dys = gather_rows(grad_y, slot_tok).reshape(n_dev, n_local, capacity, d_model)
+        wr = jnp.pad(jnp.stack(split3(w_router)), ((0, 0), (0, 0), (0, LANES - num_experts)))
+
         logits = jnp.dot(x_tokens, w_router, preferred_element_type=jnp.float32)
         router_prob = jax.nn.softmax(logits, axis=-1)
         log_norm = jax.nn.logsumexp(logits, axis=-1)
@@ -45,26 +298,10 @@
         route_stats = jnp.concatenate([jnp.sum(onehot, axis=0), jnp.sum(router_prob, axis=0), jnp.sum(log_norm * log_norm)[None]])
         route_stats = lax.psum(route_stats, 'ep')
 
-        sent_rows = gather_rows(x_tokens, slot_tok).reshape(n_dev, n_local, capacity, d_model)
-        recv_rows = lax.all_to_all(sent_rows, 'ep', 0, 0, tiled=True)
-        pre_act = jnp.einsum('pecd,edf->pecf', recv_rows, w_in, preferred_element_type=jnp.float32)
-        hidden = jnp.maximum(pre_act, 0.0).astype(jnp.bfloat16)
-        expert_out = jnp.einsum('pecf,efd->pecd', hidden, w_out, preferred_element_type=jnp.float32).astype(jnp.bfloat16)
-        back_out = lax.all_to_all(expert_out, 'ep', 0, 0, tiled=True).reshape(num_experts * capacity, d_model)
-        out_tok = gather_rows(back_out, tok_slot)
-        gy_f32 = grad_y.astype(jnp.float32)
-        d_gate = jnp.sum(out_tok.astype(jnp.float32) * gy_f32, axis=-1)
-
-        scaled = (gate_val[:, None] * gy_f32).astype(jnp.bfloat16)
-        sent_grad = gather_rows(scaled, slot_tok).reshape(n_dev, n_local, capacity, d_model)
-        recv_grad = lax.all_to_all(sent_grad, 'ep', 0, 0, tiled=True)
-        d_hidden = jnp.einsum('pecd,efd->pecf', recv_grad, w_out, preferred_element_type=jnp.float32)
-        d_pre = jnp.where(hidden > 0, d_hidden, 0.0).astype(jnp.bfloat16)
-        grad_w_out = jnp.einsum('pecf,pecd->efd', hidden, recv_grad, preferred_element_type=jnp.float32)
-        grad_w_in = jnp.einsum('pecd,pecf->edf', recv_rows, d_pre, preferred_element_type=jnp.float32)
-        d_rows = jnp.einsum('pecf,edf->pecd', d_pre, w_in, preferred_element_type=jnp.float32).astype(jnp.bfloat16)
-        back_grad = lax.all_to_all(d_rows, 'ep', 0, 0, tiled=True).reshape(num_experts * capacity, d_model)
-        dx_expert = gather_rows(back_grad, tok_slot)
+        _, _, _, d_back, g_back, grad_w_in, gwout_t = expert_exchange(n_dev, xs, dys, wr, w_in, w_out)
+        grad_w_out = jnp.swapaxes(gwout_t, 1, 2)
+        d_gate = gather_rows(g_back.reshape(-1), tok_slot)
+        dx_expert = gather_rows(d_back.reshape(num_experts * capacity, d_model), tok_slot)
 
         load_frac = route_stats[:num_experts] / total_tok
         mean_prob = route_stats[num_experts:2 * num_experts] / total_tok

time: 1290 us -> 878 us (0.68)
  Pallas kernels: 0 us -> 514 us
  blocking collectives: 533 us -> 45.5 us
  matrix products: 377 us -> 25.6 us
  waiting for transfers between devices: 52.2 us -> 0 us
  other arithmetic: 53.6 us -> 34 us
  starting transfers between devices: 17.5 us -> 0 us
    pallas_call x0 -> x1, Pallas kernels: none -> 514 us  [expert_exchange(): pl.pallas_call(lambda *refs: expert_kernel(n_dev, n_local, num_experts, b...]
    dot_general x6 -> x0, matrix products: 352 us -> none  [the longest x1 62.5 us: expert_layer(): jnp.einsum('pecd,efd->pecf', recv_grad, w_out, preferred_element_type=jnp...]
    all_to_all x1 -> x0, blocking collectives: 175 us -> none  [expert_layer(): recv_rows = lax.all_to_all(sent_rows, 'ep', 0, 0, tiled=True)]
    psum x1, blocking collectives: 178 us -> 21.5 us  [expert_layer(): route_stats = lax.psum(route_stats, 'ep')]
    psum x1, blocking collectives: 180 us -> 24 us  [expert_layer(): lax.psum(jnp.einsum('sd,se->de', x_tokens, d_logits, preferred_element_ty...]
    all_to_all x3 -> x0, waiting for transfers between devices: 52.2 us -> none  [the longest x1 52.2 us: expert_layer(): lax.all_to_all(d_rows, 'ep', 0, 0, tiled=True)]
    unnamed x54 -> x6, local copies, waits for them, and re-layouts: 0.12 us -> 31.6 us
    convert_element_type x2 -> x0, local copies, waits for them, and re-layouts: 19.5 us -> none  [the longest x1 13.2 us: expert_layer(): jnp.einsum('pecf,edf->pecd', d_pre, w_in, preferred_element_type=jnp.floa...]
  transfers between devices with their start and end apart: 3 -> 0, of which waited for: 1 -> 0; matrix products, arithmetic and copies ran while one was open for 10% -> 0% of each run, Pallas kernels for 0% -> 0%
where the time goes in v1:
time: 878 us; the launch traced here: 875 us
  Pallas kernels  514 us (59%)
  local copies, waits for them, and re-layouts  251 us (29%)
  blocking collectives  45.5 us (5%)
  other arithmetic  34 us (4%)
  matrix products  25.6 us (3%)
    pallas_call x1, Pallas kernels, expert_exchange(): pl.pallas_call(lambda *refs: expert_kernel(n_dev, n_local, num_experts, b...  514 us
    gather x4, local copies, waits for them, and re-layouts, gather_rows(): return jnp.take(source, row_index, axis=0, mode='fill', fill_value=0)  187 us
    unnamed x6, local copies, waits for them, and re-layouts  31.6 us
    scatter x1, local copies, waits for them, and re-layouts, route_slots(): jnp.full((n_slots,), tokens, jnp.int32).at[tok_slot]  30.5 us
    psum x1, blocking collectives, expert_layer(): lax.psum(jnp.einsum('sd,se->de', x_tokens, d_logits, preferred_element_ty...  24 us
    select_n x1, other arithmetic, gather_rows(): return jnp.take(source, row_index, axis=0, mode='fill', fill_value=0)  23.2 us
    psum x1, blocking collectives, expert_layer(): route_stats = lax.psum(route_stats, 'ep')  21.5 us

profile of v1, /device:TPU:1, one launch (start us, length us, event | category | flops | bytes accessed | tf_op | source)
XLA Modules:
  0.0 874.9 jit_solution(9859306671621527394)
XLA Ops:
  0.6 0.8 fusion.2
  1.4 4.8 reduce-window.6
  6.2 0.5 slice_reduce_fusion
  6.7 0.2 reduce-window.9
  7.0 0.2 broadcast_add_fusion
  7.2 1.1 fusion.1
  8.3 0.8 broadcast_clamp_fusion
  9.1 30.5 %scatter_custom_fusion = s32[10240]{0:T(1024)S(1)} fusion(s32[8192]{0:T(1024)S(1)} %get-tuple-element.40, s32[8192]{0:T(1024)S(1)} %iota.11, s32[]{:T(128)} %constant.47.clone.1), kind=kCustom, calls=%fused_computation.53 | custom fusion | bytes 40964 | tf_op jit(solution)/shard_map/scatter | solution.py:22
  39.6 52.4 %gather_fusion.2 = bf16[10240,768]{1,0:T(8,128)(2,1)} fusion(bf16[8192,768]{1,0:T(8,128)(2,1)} %param.8, s32[10240]{0:T(1024)S(1)} %fusion.16), kind=kCustom, calls=%fused_computation.clone | custom fusion | bytes 31498240 | tf_op jit(solution)/shard_map/jit(_take)/gather | solution.py:27
  92.0 52.2 %gather_fusion.3 = bf16[10240,768]{1,0:T(8,128)(2,1)} fusion(bf16[8192,768]{1,0:T(8,128)(2,1)} %param.13, s32[10240]{0:T(1024)S(1)} %fusion.16), kind=kCustom, calls=%fused_computation.1.clone | custom fusion | bytes 31498240 | tf_op jit(solution)/shard_map/jit(_take)/gather | solution.py:27
  144.3 0.0 copy-start.1
  144.3 23.2 %broadcast_select_fusion = (bf16[10240,768]{1,0:T(8,128)(2,1)}, bf16[10240,768]{1,0:T(8,128)(2,1)}) fusion(bf16[10240,768]{1,0:T(8,128)(2,1)} %gather_fusion.3, pred[10240]{0:T(1024)(128)(4,1)S(1)} %compare_and_fusion, bf16[10240,768]{1,0:T(8,128)(2,1)} %gather_fusion.2), kind=kLoop, calls=%fused_computation.6 | loop fusion | flops 15728640 | bytes 62924800 | tf_op jit(solution)/shard_map/jit(_take)/select_n | solution.py:27
  167.5 0.3 copy.18
  167.8 0.9 pad.4.refs_2_
  168.8 514.2 %expert_exchange.1 = (bf16[8,2,640,768]{3,2,1,0:T(8,128)(2,1)}, bf16[8,2,640,768]{3,2,1,0:T(8,128)(2,1)}, bf16[8,2,640,768]{3,2,1,0:T(8,128)(2,1)}, bf16[8,2,640...) custom-call(bf16[8,2,640,768]{3,2,1,0:T(8,128)(2,1)} %bitcast.37, ...), custom_call_target="tpu_custom_call" | custom-call | tf_op jit(solution)/shard_map/expert_exchange/pallas_call | solution.py:260
  683.0 37.6 %gather_fusion.1 = f32[8192]{0:T(1024)S(1)} fusion(f32[10240]{0:T(1024)} %bitcast.34, s32[8192]{0:T(1024)S(1)} %get-tuple-element.39), kind=kCustom, calls=%fused_computation.3 | custom fusion | bytes 98304 | tf_op jit(solution)/shard_map/jit(_take)/gather | solution.py:27
  720.6 0.0 copy-start
  720.6 8.0 fusion.25
  728.6 0.1 fusion.4
  728.7 0.5 multiply_reduce_fusion.1
  729.3 0.6 multiply_reduce_fusion.2
  729.9 0.7 pad_maximum_fusion.1
  730.6 21.5 %psum.14 = f32[33]{0:T(128)S(1)} all-reduce(f32[33]{0:T(128)S(1)} %pad_maximum_fusion.1), channel_id=1, replica_groups=mesh['ep'=8] {'ep'}, use_global_device_ids=true, to_apply=%region_11.13 | all-reduce | flops 33 | bytes 264 | tf_op jit(solution)/shard_map/psum | solution.py:299
  752.1 0.7 multiply_reduce_fusion.3
  752.8 0.2 multiply_reduce_fusion
  753.0 6.4 convolution_bitcast_fusion
  759.4 24.0 %psum.15 = f32[768,16]{0,1:T(8,128)} all-reduce(f32[768,16]{0,1:T(8,128)S(1)} %convolution_bitcast_fusion), channel_id=1, replica_groups=mesh['ep'=8] {'ep'}, use_global_device_ids=true, to_apply=%region_13.15 | all-reduce | flops 12288 | bytes 98304 | tf_op jit(solution)/shard_map/psum | solution.py:314
  783.4 44.5 %gather_fusion = bf16[8192,768]{1,0:T(8,128)(2,1)} fusion(bf16[10240,768]{1,0:T(8,128)(2,1)} %bitcast.35, s32[8192]{0:T(1024)S(1)} %get-tuple-element.39), kind=kCustom, calls=%fused_computation.2 | custom fusion | bytes 25198592 | tf_op jit(solution)/shard_map/jit(_take)/gather | solution.py:27
  827.9 11.3 %add_convert_fusion = bf16[8192,768]{1,0:T(8,128)(2,1)} fusion(bf16[8192,768]{1,0:T(8,128)(2,1)} %gather_fusion, pred[8192]{0:T(1024)(128)(4,1)S(1)} %get-tuple-element.38, f32[768,16]{0,1:T(8,128)S(1)} %copy-done.1, f32[8192]{0:T(1024)S(1)} %get-tuple-element.42, f32[8192]{0:T(1024)S(1)} %multiply_reduce_fusion, f32[16]{0:T(128)S(1)} %get-tuple-element.49, ...), kind=kOutput, calls=%fused_computation.5 | convolution fusion | flops 228065280 | bytes 25944128 | tf_op jit(solution)/shard_map/se,de->sd/dot_general | solution.py:312
  839.8 0.6 slice.19
  841.1 18.6 %copy.19 = f32[2,3072,768]{2,1,0:T(8,128)} copy(f32[2,3072,768]{1,2,0:T(8,128)} %bitcast.38) | data formatting | bytes 37748736
  859.7 12.9 %copy.23 = f32[2,768,3072]{2,1,0:T(8,128)} copy(f32[2,768,3072]{2,1,0:T(8,128)} %get-tuple-element.59) | data formatting | bytes 37748736
  (9 shorter events, 0.1 us)
Async XLA Ops:
  144.3 23.2 %copy-start.1 = (f32[768,16]{0,1:T(8,128)S(1)}, f32[768,16]{0,1:T(8,128)}, u32[]{:S(2)}) copy-start(f32[768,16]{0,1:T(8,128)} %param.9) | copy-start | bytes 147460
  720.6 8.1 copy-start

commit v2 on v1

--- a/solution.py
+++ b/solution.py
@@ -14,24 +14,10 @@
 
 
 def route_slots(idx_group, num_experts, capacity):
-    tokens = idx_group.shape[0]
-    n_slots = num_experts * capacity
     onehot = (idx_group[:, None] == jnp.arange(num_experts, dtype=jnp.int32)[None, :]).astype(jnp.int32)
     position = jnp.sum(jnp.cumsum(onehot, axis=0) * onehot, axis=1) - 1
-    tok_slot = jnp.where(position < capacity, idx_group * capacity + position, n_slots)
-    slot_tok = jnp.full((n_slots,), tokens, jnp.int32).at[tok_slot].set(jnp.arange(tokens, dtype=jnp.int32), mode='drop')
-    return onehot.astype(jnp.float32), tok_slot, slot_tok
-
-
-def gather_rows(source, row_index):
-    return jnp.take(source, row_index, axis=0, mode='fill', fill_value=0)
-
-
-def router_grad(router_prob, onehot, gate_val, d_gate, log_norm, aux_vec, z_coef):
-    spread = jnp.sum(router_prob * aux_vec, axis=-1, keepdims=True)
-    return ((gate_val * d_gate)[..., None] * (onehot - router_prob)
-            + router_prob * (aux_vec - spread)
-            + (z_coef * log_norm)[..., None] * router_prob)
+    tok_slot = jnp.where(position < capacity, idx_group * capacity + position, num_experts * capacity)
+    return tok_slot, jnp.sum(onehot, axis=0)
 
 
 def split3(w):
@@ -48,10 +34,10 @@
     return jnp.dot(a, b, preferred_element_type=F32)
 
 
-def expert_kernel(n_dev, n_local, num_experts, blk, xs, dys, wr, w_in, w_out,
-                  xr, dyr, dsend, dback, gback, gwin, gwout_t,
+def expert_kernel(n_dev, n_local, num_experts, blk, xs, dys, wr, cnt, w_in, w_out,
+                  xr, dyr, dsend, dback, gback, gwin, gwout_t, cnt_all,
                   xv, dyv, gv, x_t, g_t, win_v, wout_v, acc_in, acc_out, o_acc, r_acc, r_out, g_all,
-                  x_send, x_recv, dy_send, dy_recv, r_send, r_recv, s_send, s_recv, ld_sem, st_sem, w_sem, flush_sem, own_sem):
+                  x_send, x_recv, dy_send, dy_recv, r_send, r_recv, s_send, s_recv, c_send, c_recv, ld_sem, st_sem, w_sem, flush_sem, own_sem):
     me = lax.axis_index('ep')
     n_blk = w_in.shape[2] // blk
     n_chunk = n_local * n_dev
@@ -85,6 +71,14 @@
         p = peer_of(k)
         return pltpu.make_async_remote_copy(g_all.at[e, k], gback.at[me, e], s_send.at[e, k], s_recv.at[e, k], device_id=(p,), device_id_type=MESH)
 
+    def c_copy(k):
+        p = peer_of(k)
+        return pltpu.make_async_remote_copy(cnt, cnt_all.at[me], c_send.at[k], c_recv.at[k], device_id=(p,), device_id_type=MESH)
+
+    own_cnt = pltpu.make_async_copy(cnt, cnt_all.at[me], own_sem.at[n_local])
+    own_cnt.start()
+    for k in range(1, n_dev):
+        c_copy(k).start()
     for e in range(n_local):
         for k in (1, 2, 4, 6, 3, 5, 7):
             x_copy(k, e).start()
@@ -236,6 +230,9 @@
     send_back(n_chunk - 1)
     for cp in flush(n_local - 1):
         cp.wait()
+    own_cnt.wait()
+    for k in range(1, n_dev):
+        c_copy(k).wait()
     for e in range(n_local):
         own_g(e).wait()
         for k in range(1, n_dev):
@@ -245,7 +242,7 @@
             s_copy(k, e).wait()
 
 
-def expert_exchange(n_dev, xs, dys, wr, w_in, w_out):
+def expert_exchange(n_dev, xs, dys, wr, cnt, w_in, w_out):
     n_local, d_model, d_ff = w_in.shape
     cap = xs.shape[2]
     num_experts = n_dev * n_local
@@ -259,9 +256,9 @@
     pair = (n_local, n_dev)
     return pl.pallas_call(
         lambda *refs: expert_kernel(n_dev, n_local, num_experts, blk, *refs),
-        out_shape=(rows, rows, rows, rows, g_shape, w_shape, w_shape),
-        in_specs=[hbm, hbm, vmem, hbm, hbm],
-        out_specs=[hbm] * 7,
+        out_shape=(rows, rows, rows, rows, g_shape, w_shape, w_shape, jax.ShapeDtypeStruct((n_dev,) + cnt.shape, F32)),
+        in_specs=[hbm, hbm, vmem, vmem, hbm, hbm],
+        out_specs=[hbm] * 8,
         scratch_shapes=[
             pltpu.VMEM((2, cap, d_model), BF16), pltpu.VMEM((2, cap, d_model), BF16), pltpu.VMEM((cap, d_model), BF16),
             pltpu.VMEM((d_model, cap), BF16), pltpu.VMEM((d_model, cap), BF16),
@@ -269,12 +266,249 @@
             pltpu.VMEM((d_model, d_ff), F32), pltpu.VMEM((d_model, d_ff), F32),
             pltpu.VMEM((cap, d_model), F32), pltpu.VMEM((cap, d_model), F32),
             pltpu.VMEM((2, cap, d_model), BF16), pltpu.VMEM((n_local, n_dev, 1, cap), F32),
-            dma(pair), dma(pair), dma(pair), dma(pair), dma(pair), dma(pair), dma(pair), dma(pair),
-            dma((2, 2)), dma((2,)), dma((2,)), dma((2,)), dma((n_local,)),
+            dma(pair), dma(pair), dma(pair), dma(pair), dma(pair), dma(pair), dma(pair), dma(pair), dma((n_dev,)), dma((n_dev,)),
+            dma((2, 2)), dma((2,)), dma((2,)), dma((2,)), dma((n_local + 1,)),
         ],
         compiler_params=pltpu.CompilerParams(collective_id=0, has_side_effects=True, vmem_limit_bytes=63 * 2 ** 20),
         name='expert_exchange',
-    )(xs, dys, wr, w_in, w_out)
+    )(xs, dys, wr, cnt, w_in, w_out)
+
+
+PITCH = 7 * 8
+ROW_TILES = 6
+
+
+def row_address(slot):
+    return (slot // 8) * PITCH + slot % 8
+
+
+def row(addr, tiles):
+    return pl.ds(addr, tiles, stride=8)
+
+
+def permute_kernel(tb, addr, x_hbm, dy_hbm, xs, dys, inb, stage, table, outb, in_sem, out_sem):
+    tokens = x_hbm.shape[0]
+    n_out, n_local, cap, d_model = xs.shape
+    groups = cap // 8
+    tiled = table.reshape(table.shape[0] // PITCH, PITCH, LANES)
+    stage3 = stage.reshape(tb // 8, PITCH, LANES)
+    n_in = tokens // tb
+
+    def fetch(source, b):
+        return pltpu.make_async_copy(source.at[pl.ds(pl.multiple_of(b * tb, tb), tb), :], inb.at[b % 2], in_sem.at[b % 2])
+
+    def emit(sink, c):
+        return pltpu.make_async_copy(outb.at[c % 2], sink.at[c // n_local, c % n_local], out_sem.at[c % 2])
+
+    fetch(x_hbm, 0).start()
+    table[...] = jnp.zeros_like(table)
+    for source, sink, follow in ((x_hbm, xs, dy_hbm), (dy_hbm, dys, None)):
+        def scatter(b, _):
+            @pl.when(b + 1 < n_in)
+            def _():
+                fetch(source, b + 1).start()
+            if follow is not None:
+                @pl.when(b + 1 == n_in)
+                def _():
+                    fetch(follow, 0).start()
+            fetch(source, b).wait()
+            for j in range(ROW_TILES):
+                part = inb[b % 2, :, j * LANES:(j + 1) * LANES].astype(F32)
+                stage3[:, j * 8:(j + 1) * 8, :] = part.reshape(tb // 8, 8, LANES)
+
+            def move(i, _):
+                for r in range(32):
+                    at = addr[b * tb + i * 32 + r]
+                    table[row(at, ROW_TILES), :] = stage[row(i * (4 * PITCH) + (r // 8) * PITCH + r % 8, ROW_TILES), :]
+                return 0
+
+            lax.fori_loop(0, tb // 32, move, 0)
+            return 0
+
+        lax.fori_loop(0, n_in, scatter, 0)
+
+        def drain(c, _):
+            @pl.when(c >= 2)
+            def _():
+                emit(sink, c - 2).wait()
+            for j in range(ROW_TILES):
+                part = tiled[pl.ds(c * groups, groups), j * 8:(j + 1) * 8, :].reshape(cap, LANES)
+                outb[c % 2, :, j * LANES:(j + 1) * LANES] = part.astype(BF16)
+            emit(sink, c).start()
+            return 0
+
+        n_chunk = n_out * n_local
+        lax.fori_loop(0, n_chunk, drain, 0)
+        for c in (n_chunk - 2, n_chunk - 1):
+            emit(sink, c).wait()
+
+
+def permute(n_dev, n_local, capacity, addr, x, dy):
+    tokens, d_model = x.shape
+    tb = 512
+    hbm = pl.BlockSpec(memory_space=pl.ANY)
+    out = jax.ShapeDtypeStruct((n_dev, n_local, capacity, d_model), BF16)
+    n_groups = n_dev * n_local * capacity // 8 + 1
+    return pl.pallas_call(
+        lambda *refs: permute_kernel(tb, *refs),
+        out_shape=(out, out),
+        grid_spec=pltpu.PrefetchScalarGridSpec(
+            num_scalar_prefetch=1, grid=(), in_specs=[hbm, hbm], out_specs=[hbm, hbm],
+            scratch_shapes=[
+                pltpu.VMEM((2, tb, d_model), BF16), pltpu.VMEM((tb // 8 * PITCH, LANES), F32), pltpu.VMEM((n_groups * PITCH, LANES), F32),
+                pltpu.VMEM((2, capacity, d_model), BF16), pltpu.SemaphoreType.DMA((2,)), pltpu.SemaphoreType.DMA((2,))]),
+        compiler_params=pltpu.CompilerParams(vmem_limit_bytes=60 * 2 ** 20),
+        name='permute_rows',
+    )(addr, x, dy)
+
+
+def token_kernel(num_experts, z_coef, addr, x, idx, wr, wr_back, v_row, dback, gback, grad_x, partial, acc,
+                 stage, table, inb, pieces_t, p_acc, z_acc, in_sem):
+    b = pl.program_id(0)
+    tb = x.shape[0]
+    n_out, n_local, cap, d_model = dback.shape
+    groups = cap // 8
+    tiled = table.reshape(table.shape[0] // PITCH, PITCH, LANES)
+    stage3 = stage.reshape(tb // 8, PITCH, LANES)
+    n_chunk = n_out * n_local
+
+    @pl.when(b == 0)
+    def _():
+        def fetch(c):
+            return pltpu.make_async_copy(dback.at[c // n_local, c % n_local], inb.at[c % 2], in_sem.at[c % 2])
+
+        fetch(0).start()
+        acc[...] = jnp.zeros_like(acc)
+        p_acc[...] = jnp.zeros_like(p_acc)
+        z_acc[...] = jnp.zeros_like(z_acc)
+        tiled[n_chunk * groups] = jnp.zeros((PITCH, LANES), F32)
+
+        def fill(c, _):
+            @pl.when(c + 1 < n_chunk)
+            def _():
+                fetch(c + 1).start()
+            fetch(c).wait()
+            for j in range(ROW_TILES):
+                part = inb[c % 2, :, j * LANES:(j + 1) * LANES].astype(F32)
+                tiled[pl.ds(c * groups, groups), j * 8:(j + 1) * 8, :] = part.reshape(groups, 8, LANES)
+            g_col = jnp.broadcast_to(gback[pl.ds(c, 1), :], (LANES, cap)).T
+            tiled[pl.ds(c * groups, groups), 6 * 8:7 * 8, :] = g_col.reshape(groups, 8, LANES)
+            return 0
+
+        lax.fori_loop(0, n_chunk, fill, 0)
+
+    def move(i, _):
+        for r in range(32):
+            at = addr[b * tb + i * 32 + r]
+            stage[row(i * (4 * PITCH) + (r // 8) * PITCH + r % 8, 7), :] = table[row(at, 7), :]
+        return 0
+
+    lax.fori_loop(0, tb // 32, move, 0)
+
+    xv = x[...]
+    logits = nn(xv, wr[0]) + nn(xv, wr[1]) + nn(xv, wr[2])
+    lane = lax.broadcasted_iota(jnp.int32, logits.shape, 1)
+    real = lane < num_experts
+    top = jnp.max(jnp.where(real, logits, -1e30), axis=1, keepdims=True)
+    expd = jnp.where(real, jnp.exp(jnp.minimum(logits - top, 0.0)), 0.0)
+    total = jnp.sum(expd, axis=1, keepdims=True)
+    prob = expd / total
+    z = top + jnp.log(total)
+    mine = jnp.broadcast_to(idx[pl.ds(b, 1), :], (LANES, tb)).T == lane.astype(F32)
+    onehot = jnp.where(mine, 1.0, 0.0)
+    gate = jnp.sum(jnp.where(mine, prob, 0.0), axis=1, keepdims=True)
+    g = stage3[:, 6 * 8:7 * 8, :].reshape(tb, LANES)
+    v = v_row[0:1, :]
+    spread = jnp.sum(prob * v, axis=1, keepdims=True)
+    dlog = gate * g * (onehot - prob) + prob * (v - spread) + (z_coef * z) * prob
+    hi = dlog.astype(BF16).astype(F32)
+    mid = (dlog - hi).astype(BF16).astype(F32)
+    low = dlog - hi - mid
+    def at(piece, k):
+        return piece if k == 0 else pltpu.roll(piece, k * num_experts, 1)
+    pieces = at(hi, 0) + at(mid, 1) + at(low, 2) + at(hi, 3) + at(mid, 4) + at(hi, 5)
+    dx = nn(pieces.astype(BF16), wr_back[...])
+    pieces_t[...] = pieces.T.astype(BF16)
+    for j in range(ROW_TILES):
+        cols = slice(j * LANES, (j + 1) * LANES)
+        grad_x[:, cols] = (stage3[:, j * 8:(j + 1) * 8, :].reshape(tb, LANES) + dx[:, cols]).astype(BF16)
+    acc[...] += nn(pieces_t[...], xv)
+    p_acc[...] += jnp.sum(prob.reshape(tb // 8, 8, LANES), axis=0)
+    z_acc[...] += jnp.sum(jnp.broadcast_to(z * z, (tb, LANES)).reshape(tb // 8, 8, LANES), axis=0)
+
+    @pl.when(b == pl.num_programs(0) - 1)
+    def _():
+        n = num_experts
+        partial[...] = jnp.zeros_like(partial)
+        partial[0:n, :] = acc[0:n, :] + acc[n:2 * n, :] + acc[2 * n:3 * n, :]
+        partial[n:n + 1, 0:LANES] = jnp.sum(p_acc[...], axis=0, keepdims=True)
+        partial[n:n + 1, LANES:2 * LANES] = jnp.sum(z_acc[...], axis=0, keepdims=True)
+
+
+def token_side(num_experts, z_coef, addr, x, idx, wr, wr_back, v_row, dback, gback):
+    tokens, d_model = x.shape
+    n_dev, n_local, cap, _ = dback.shape
+    tb = 512
+    hbm = pl.BlockSpec(memory_space=pl.ANY)
+    idx = idx.astype(F32).reshape(tokens // tb, tb)
+    gback = gback.reshape(n_dev * n_local, cap)
+
+    def whole(a):
+        return pl.BlockSpec(a.shape, lambda b, addr: (0,) * a.ndim)
+
+    n_groups = n_dev * n_local * cap // 8 + 1
+    rows = num_experts + 8
+    return pl.pallas_call(
+        lambda *refs: token_kernel(num_experts, z_coef, *refs),
+        out_shape=(jax.ShapeDtypeStruct(x.shape, BF16), jax.ShapeDtypeStruct((rows, d_model), F32), jax.ShapeDtypeStruct((LANES, d_model), F32)),
+        grid_spec=pltpu.PrefetchScalarGridSpec(
+            num_scalar_prefetch=1, grid=(tokens // tb,),
+            in_specs=[pl.BlockSpec((tb, d_model), lambda b, addr: (b, 0)), whole(idx),
+                      whole(wr), whole(wr_back), whole(v_row), hbm, whole(gback)],
+            out_specs=[pl.BlockSpec((tb, d_model), lambda b, addr: (b, 0)), pl.BlockSpec((rows, d_model), lambda b, addr: (0, 0)),
+                       pl.BlockSpec((LANES, d_model), lambda b, addr: (0, 0))],
+            scratch_shapes=[
+                pltpu.VMEM((tb // 8 * PITCH, LANES), F32), pltpu.VMEM((n_groups * PITCH, LANES), F32),
+                pltpu.VMEM((2, cap, d_model), BF16),
+                pltpu.VMEM((LANES, tb), BF16), pltpu.VMEM((8, LANES), F32), pltpu.VMEM((8, LANES), F32),
+                pltpu.SemaphoreType.DMA((2,))]),
+        compiler_params=pltpu.CompilerParams(vmem_limit_bytes=60 * 2 ** 20),
+        name='token_side',
+    )(addr, x, idx, wr, wr_back, v_row, dback, gback)
+
+
+def total_kernel(n_dev, part, out, stats, parts, send_sem, recv_sem):
+    me = lax.axis_index('ep')
+    barrier = pltpu.get_barrier_semaphore()
+    peers = [(me + k) % n_dev for k in range(1, n_dev)]
+    for p in peers:
+        pl.semaphore_signal(barrier, inc=1, device_id=(p,), device_id_type=MESH)
+    pl.semaphore_wait(barrier, n_dev - 1)
+    copies = [pltpu.make_async_remote_copy(part, parts.at[me], send_sem.at[k], recv_sem.at[k], device_id=(p,), device_id_type=MESH)
+              for k, p in enumerate(peers)]
+    for copy in copies:
+        copy.start()
+    parts[me] = part[...]
+    for copy in copies:
+        copy.wait()
+    total = parts[0]
+    for d in range(1, n_dev):
+        total = total + parts[d]
+    n = out.shape[0]
+    out[...] = total[0:n]
+    stats[...] = total[n:]
+
+
+def total_over_devices(n_dev, n_grad, part):
+    vmem = pl.BlockSpec(memory_space=pltpu.VMEM)
+    return pl.pallas_call(
+        lambda *refs: total_kernel(n_dev, *refs),
+        out_shape=(jax.ShapeDtypeStruct((n_grad, part.shape[1]), F32), jax.ShapeDtypeStruct((part.shape[0] - n_grad, part.shape[1]), F32)),
+        in_specs=[vmem], out_specs=[vmem, vmem],
+        scratch_shapes=[pltpu.VMEM((n_dev,) + part.shape, F32), pltpu.SemaphoreType.DMA((n_dev - 1,)), pltpu.SemaphoreType.DMA((n_dev - 1,))],
+        compiler_params=pltpu.CompilerParams(collective_id=1, has_side_effects=True),
+        name='device_total',
+    )(part)
 
 
 def solution(mesh):
@@ -286,33 +520,26 @@
         num_experts = n_local * n_dev
         capacity = (5 * tokens + 4 * num_experts - 1) // (4 * num_experts)
         total_tok = tokens * n_dev
-        onehot, tok_slot, slot_tok = route_slots(expert_idx, num_experts, capacity)
-        xs = gather_rows(x_tokens, slot_tok).reshape(n_dev, n_local, capacity, d_model)
-        dys = gather_rows(grad_y, slot_tok).reshape(n_dev, n_local, capacity, d_model)
-        wr = jnp.pad(jnp.stack(split3(w_router)), ((0, 0), (0, 0), (0, LANES - num_experts)))
-
-        logits = jnp.dot(x_tokens, w_router, preferred_element_type=jnp.float32)
-        router_prob = jax.nn.softmax(logits, axis=-1)
-        log_norm = jax.nn.logsumexp(logits, axis=-1)
-        gate_val = jnp.sum(router_prob * onehot, axis=-1)
-        route_stats = jnp.concatenate([jnp.sum(onehot, axis=0), jnp.sum(router_prob, axis=0), jnp.sum(log_norm * log_norm)[None]])
-        route_stats = lax.psum(route_stats, 'ep')
-
-        _, _, _, d_back, g_back, grad_w_in, gwout_t = expert_exchange(n_dev, xs, dys, wr, w_in, w_out)
+        tok_slot, counts = route_slots(expert_idx, num_experts, capacity)
+        addr = row_address(tok_slot)
+        xs, dys = permute(n_dev, n_local, capacity, addr, x_tokens, grad_y)
+        w_hi, w_mid, w_low = split3(w_router)
+        lanes = ((0, 0), (0, LANES - num_experts))
+        wr = jnp.stack([jnp.pad(w, lanes) for w in (w_hi, w_mid, w_low)])
+        wr_back = jnp.pad(jnp.concatenate([w.T for w in (w_hi, w_hi, w_hi, w_mid, w_mid, w_low)]), ((0, LANES - 6 * num_experts), (0, 0)))
+        cnt = jnp.broadcast_to(jnp.pad(counts.astype(F32), (0, LANES - num_experts))[None], (8, LANES))
+
+        _, _, _, d_back, g_back, gwin, gwout_t, cnt_all = expert_exchange(n_dev, xs, dys, wr, cnt, w_in, w_out)
+        load_row = jnp.sum(cnt_all, axis=0) / total_tok
+        v_row = AUX_WEIGHT * num_experts * load_row / total_tok
+        grad_x, partial, _ = token_side(num_experts, 2.0 * Z_WEIGHT / total_tok, addr, x_tokens, expert_idx, wr, wr_back, v_row, d_back, g_back)
+        grad_wr_t, stats = total_over_devices(n_dev, num_experts, partial)
+        grad_w_router = grad_wr_t.T
+        mean_prob = stats[0, :num_experts] / total_tok
+        aux_loss = AUX_WEIGHT * num_experts * jnp.sum(load_row[0, :num_experts] * mean_prob)
+        z_loss = Z_WEIGHT * stats[0, LANES] / total_tok
         grad_w_out = jnp.swapaxes(gwout_t, 1, 2)
-        d_gate = gather_rows(g_back.reshape(-1), tok_slot)
-        dx_expert = gather_rows(d_back.reshape(num_experts * capacity, d_model), tok_slot)
-
-        load_frac = route_stats[:num_experts] / total_tok
-        mean_prob = route_stats[num_experts:2 * num_experts] / total_tok
-        aux_loss = AUX_WEIGHT * num_experts * jnp.sum(load_frac * mean_prob)
-        z_loss = Z_WEIGHT * route_stats[2 * num_experts] / total_tok
-        aux_vec = AUX_WEIGHT * num_experts * load_frac / total_tok
-        d_logits = router_grad(router_prob, onehot, gate_val, d_gate, log_norm, aux_vec, 2.0 * Z_WEIGHT / total_tok)
-        dx_router = jnp.einsum('se,de->sd', d_logits, w_router)
-        grad_x = (dx_expert.astype(jnp.float32) + dx_router).astype(jnp.bfloat16)
-        grad_w_router = lax.psum(jnp.einsum('sd,se->de', x_tokens, d_logits, preferred_element_type=jnp.float32), 'ep')
-        return grad_x, grad_w_in, grad_w_out, grad_w_router, aux_loss, z_loss
+        return grad_x, gwin, grad_w_out, grad_w_router, aux_loss, z_loss
 
     return jax.shard_map(expert_layer, mesh=mesh,
                          in_specs=(P('ep', None), P(None, None), P('ep'), P('ep', None, None), P('ep', None, None), P('ep', None)),

time: 878 us -> 711 us (0.81)
  local copies, waits for them, and re-layouts: 251 us -> 37.6 us
  Pallas kernels: 514 us -> 652 us
  blocking collectives: 45.5 us -> 0 us
  matrix products: 25.6 us -> 0 us
  other arithmetic: 34 us -> 14.8 us
    gather x4 -> x0, local copies, waits for them, and re-layouts: 187 us -> none  [gather_rows(): return jnp.take(source, row_index, axis=0, mode='fill', fill_value=0)]
    pallas_call x0 -> x3, Pallas kernels: none -> 138 us  [the longest x1 73.5 us: token_side(): pl.pallas_call(lambda *refs: token_kernel(num_experts, z_coef, *refs), ou...]
    psum x2 -> x0, blocking collectives: 45.5 us -> none  [the longest x1 24 us: expert_layer(): lax.psum(jnp.einsum('sd,se->de', x_tokens, d_logits, preferred_element_ty...]
    scatter x1 -> x0, local copies, waits for them, and re-layouts: 30.5 us -> none  [route_slots(): jnp.full((n_slots,), tokens, jnp.int32).at[tok_slot]]
    dot_general x3 -> x0, matrix products: 25.6 us -> none  [the longest x1 11.3 us: expert_layer(): dx_router = jnp.einsum('se,de->sd', d_logits, w_router)]
    select_n x2 -> x0, other arithmetic: 23.2 us -> none  [the longest x1 23.2 us: gather_rows(): return jnp.take(source, row_index, axis=0, mode='fill', fill_value=0)]
    unnamed x6 -> x8, local copies, waits for them, and re-layouts: 31.6 us -> 32.2 us
where the time goes in v2:
time: 711 us; the launch traced here: 709 us
  Pallas kernels  652 us (92%)
  local copies, waits for them, and re-layouts  37.6 us (5%)
  other arithmetic  14.8 us (2%)
    pallas_call x1, Pallas kernels, expert_exchange(): pl.pallas_call(lambda *refs: expert_kernel(n_dev, n_local, num_experts, b...  515 us
    pallas_call x1, Pallas kernels, token_side(): pl.pallas_call(lambda *refs: token_kernel(num_experts, z_coef, *refs), ou...  73.5 us
    pallas_call x1, Pallas kernels, permute(): pl.pallas_call(lambda *refs: permute_kernel(tb, *refs), out_shape=(out, o...  52.9 us
    unnamed x8, local copies, waits for them, and re-layouts  32.2 us

profile of v2, /device:TPU:1, one launch (start us, length us, event | category | flops | bytes accessed | tf_op | source)
XLA Modules:
  0.0 709.1 jit_solution(12279490635061834278)
XLA Ops:
  0.6 0.8 bitcast_dynamic-update-slice_fusion.4
  1.4 0.8 bitcast_dynamic-update-slice_fusion.1
  2.3 0.8 bitcast_dynamic-update-slice_fusion
  3.1 0.1 pad_maximum_fusion
  3.2 1.1 copy.16.refs_2_.refs_3_
  4.3 0.8 fusion.2
  5.1 4.8 reduce-window.6
  9.9 0.5 slice_reduce_fusion
  10.4 0.2 reduce-window.9
  10.6 0.2 broadcast_add_fusion
  10.8 1.3 convert_reduce_fusion
  12.1 1.5 fusion.11
  13.6 52.9 %permute_rows.1 = (bf16[8,2,640,768]{3,2,1,0:T(8,128)(2,1)}, bf16[8,2,640,768]{3,2,1,0:T(8,128)(2,1)}) custom-call(s32[8192]{0:T(1024)} %get-tuple-element.49.refs_0_, bf16[8192,768]{1,0:T(8,128)(2,1)} %refs_1_.3, bf16[8192,768]{1,0:T(8,128)(2,1)} %refs_2_.1), custom_call_target="tpu_custom_call" | custom-call | tf_op jit(solution)/shard_map/permute_rows/pallas_call | solution.py:352
  66.5 0.6 broadcast_in_dim.7.refs_3_
  67.1 514.7 %expert_exchange.1 = (bf16[8,2,640,768]{3,2,1,0:T(8,128)(2,1)}, bf16[8,2,640,768]{3,2,1,0:T(8,128)(2,1)}, bf16[8,2,640,768]{3,2,1,0:T(8,128)(2,1)}, bf16[8,2,640...) custom-call(bf16[8,2,640,768]{3,2,1,0:T(8,128)(2,1)} %get-tuple-elem, ...), custom_call_target="tpu_custom_call" | custom-call | tf_op jit(solution)/shard_map/expert_exchange/pallas_call | solution.py:257
  581.8 0.8 reduce_sum.38
  582.6 0.6 broadcast_multiply_fusion
  583.2 0.9 reduce.2
  584.1 0.6 reshape.42.refs_7_
  584.8 0.7 pad.21.refs_4_
  585.4 0.6 reshape.41.refs_2_
  586.0 73.5 %token_side.1 = (bf16[8192,768]{1,0:T(8,128)(2,1)}, f32[24,768]{1,0:T(8,128)}, f32[128,768]{1,0:T(8,128)}) custom-call(s32[8192]{0:T(1024)} %get-tuple-element.49.refs_0_, bf16[8192,768]{1,0:T(8,128)(2,1)} %refs_1_.3, f32[16,512]{1,0:T(8,128)} %reshape.41.refs_2_, bf16[3,768,128]{2,1,0:T(8,128)(2,1)} %copy.16.refs_2_.refs_3_, bf16[128,768]{1,0:T(8,128)(2,1)} %pad.21.refs_4_, ...), custom_call_target="tpu_custom_call" | custom-call | tf_op jit(solution)/shard_map/token_side/pallas_call | solution.py:461
  659.5 11.3 %device_total.1 = (f32[16,768]{1,0:T(8,128)}, f32[8,768]{1,0:T(8,128)}) custom-call(f32[24,768]{1,0:T(8,128)} %get-tuple-element.25.refs_0_), custom_call_target="tpu_custom_call" | custom-call | tf_op jit(solution)/shard_map/device_total/pallas_call | solution.py:504
  670.9 1.3 multiply_reduce_fusion
  672.8 1.2 slice.19
  674.7 18.6 %copy.17 = f32[2,3072,768]{2,1,0:T(8,128)} copy(f32[2,3072,768]{1,2,0:T(8,128)} %bitcast.33) | data formatting | bytes 37748736
  693.3 0.0 copy-start
  693.3 12.9 %copy.28 = f32[2,768,3072]{2,1,0:T(8,128)} copy(f32[2,768,3072]{2,1,0:T(8,128)} %get-tuple-element.61) | data formatting | bytes 37748736
  706.2 0.0 copy-done
  706.2 0.6 copy.29
  (7 shorter events, 0.1 us)
Async XLA Ops:
  693.3 12.9 %copy-start = (f32[16,768]{1,0:T(8,128)S(1)}, f32[16,768]{1,0:T(8,128)}, u32[]{:S(2)}) copy-start(f32[16,768]{1,0:T(8,128)} %get-tuple-element.26) | copy-start | bytes 147460

commit v3 on v2

--- a/solution.py
+++ b/solution.py
@@ -35,7 +35,7 @@
 
 
 def expert_kernel(n_dev, n_local, num_experts, blk, xs, dys, wr, cnt, w_in, w_out,
-                  xr, dyr, dsend, dback, gback, gwin, gwout_t, cnt_all,
+                  xr, dyr, dsend, dback, dlast, gback, gwin, gwout_t, cnt_all,
                   xv, dyv, gv, x_t, g_t, win_v, wout_v, acc_in, acc_out, o_acc, r_acc, r_out, g_all,
                   x_send, x_recv, dy_send, dy_recv, r_send, r_recv, s_send, s_recv, c_send, c_recv, ld_sem, st_sem, w_sem, flush_sem, own_sem):
     me = lax.axis_index('ep')
@@ -118,13 +118,19 @@
         k = offset_of(i)
         p = peer_of(k)
 
-        @pl.when(i == 0)
-        def _():
-            do(pltpu.make_async_copy(r_out.at[c % 2], dback.at[me, e], st_sem.at[c % 2]))
-
-        @pl.when(i > 0)
-        def _():
-            do(pltpu.make_async_copy(r_out.at[c % 2], dsend.at[p, e], st_sem.at[c % 2]))
+        @pl.when(e == n_local - 1)
+        def _():
+            do(pltpu.make_async_copy(r_out.at[c % 2], dlast.at[p], st_sem.at[c % 2]))
+
+        @pl.when(e < n_local - 1)
+        def _():
+            @pl.when(i == 0)
+            def _():
+                do(pltpu.make_async_copy(r_out.at[c % 2], dback.at[me, e], st_sem.at[c % 2]))
+
+            @pl.when(i > 0)
+            def _():
+                do(pltpu.make_async_copy(r_out.at[c % 2], dsend.at[p, e], st_sem.at[c % 2]))
 
     def own_g(e):
         return pltpu.make_async_copy(g_all.at[e, 0], gback.at[me, e], own_sem.at[e])
@@ -140,8 +146,11 @@
 
         @pl.when(i > 0)
         def _():
-            r_copy(k, e).start()
             s_copy(k, e).start()
+
+            @pl.when(e < n_local - 1)
+            def _():
+                r_copy(k, e).start()
 
     def weights(e):
         return (pltpu.make_async_copy(w_in.at[e], win_v, w_sem.at[0]), pltpu.make_async_copy(w_out.at[e], wout_v, w_sem.at[1]))
@@ -238,7 +247,8 @@
         for k in range(1, n_dev):
             x_copy(k, e).wait_send()
             dy_copy(k, e).wait_send()
-            r_copy(k, e).wait()
+            if e < n_local - 1:
+                r_copy(k, e).wait()
             s_copy(k, e).wait()
 
 
@@ -250,15 +260,17 @@
     hbm = pl.BlockSpec(memory_space=pl.ANY)
     vmem = pl.BlockSpec(memory_space=pltpu.VMEM)
     rows = jax.ShapeDtypeStruct(xs.shape, BF16)
+    early = jax.ShapeDtypeStruct((n_dev, n_local - 1, cap, d_model), BF16)
+    late = jax.ShapeDtypeStruct((n_dev, cap, d_model), BF16)
     g_shape = jax.ShapeDtypeStruct((n_dev, n_local, 1, cap), F32)
     w_shape = jax.ShapeDtypeStruct((n_local, d_model, d_ff), F32)
     dma = pltpu.SemaphoreType.DMA
     pair = (n_local, n_dev)
     return pl.pallas_call(
         lambda *refs: expert_kernel(n_dev, n_local, num_experts, blk, *refs),
-        out_shape=(rows, rows, rows, rows, g_shape, w_shape, w_shape, jax.ShapeDtypeStruct((n_dev,) + cnt.shape, F32)),
+        out_shape=(rows, rows, early, early, late, g_shape, w_shape, w_shape, jax.ShapeDtypeStruct((n_dev,) + cnt.shape, F32)),
         in_specs=[hbm, hbm, vmem, vmem, hbm, hbm],
-        out_specs=[hbm] * 8,
+        out_specs=[hbm] * 9,
         scratch_shapes=[
             pltpu.VMEM((2, cap, d_model), BF16), pltpu.VMEM((2, cap, d_model), BF16), pltpu.VMEM((cap, d_model), BF16),
             pltpu.VMEM((d_model, cap), BF16), pltpu.VMEM((d_model, cap), BF16),
@@ -274,7 +286,7 @@
     )(xs, dys, wr, cnt, w_in, w_out)
 
 
-PITCH = 7 * 8
+PITCH = 6 * 8
 ROW_TILES = 6
 
 
@@ -362,45 +374,27 @@
     )(addr, x, dy)
 
 
-def token_kernel(num_experts, z_coef, addr, x, idx, wr, wr_back, v_row, dback, gback, grad_x, partial, acc,
-                 stage, table, inb, pieces_t, p_acc, z_acc, in_sem):
+def router_kernel(num_experts, z_coef, slot, x, idx, wr, v_row, gback, pieces_out, partial, acc, gtab, g_rows, pieces_t, p_acc, z_acc):
     b = pl.program_id(0)
     tb = x.shape[0]
-    n_out, n_local, cap, d_model = dback.shape
-    groups = cap // 8
-    tiled = table.reshape(table.shape[0] // PITCH, PITCH, LANES)
-    stage3 = stage.reshape(tb // 8, PITCH, LANES)
-    n_chunk = n_out * n_local
+    n_chunk, cap = gback.shape
 
     @pl.when(b == 0)
     def _():
-        def fetch(c):
-            return pltpu.make_async_copy(dback.at[c // n_local, c % n_local], inb.at[c % 2], in_sem.at[c % 2])
-
-        fetch(0).start()
         acc[...] = jnp.zeros_like(acc)
         p_acc[...] = jnp.zeros_like(p_acc)
         z_acc[...] = jnp.zeros_like(z_acc)
-        tiled[n_chunk * groups] = jnp.zeros((PITCH, LANES), F32)
+        gtab[n_chunk * cap:, :] = jnp.zeros((8, LANES), F32)
 
         def fill(c, _):
-            @pl.when(c + 1 < n_chunk)
-            def _():
-                fetch(c + 1).start()
-            fetch(c).wait()
-            for j in range(ROW_TILES):
-                part = inb[c % 2, :, j * LANES:(j + 1) * LANES].astype(F32)
-                tiled[pl.ds(c * groups, groups), j * 8:(j + 1) * 8, :] = part.reshape(groups, 8, LANES)
-            g_col = jnp.broadcast_to(gback[pl.ds(c, 1), :], (LANES, cap)).T
-            tiled[pl.ds(c * groups, groups), 6 * 8:7 * 8, :] = g_col.reshape(groups, 8, LANES)
+            gtab[pl.ds(pl.multiple_of(c * cap, 8), cap), :] = jnp.broadcast_to(gback[pl.ds(c, 1), :], (LANES, cap)).T
             return 0
 
         lax.fori_loop(0, n_chunk, fill, 0)
 
     def move(i, _):
         for r in range(32):
-            at = addr[b * tb + i * 32 + r]
-            stage[row(i * (4 * PITCH) + (r // 8) * PITCH + r % 8, 7), :] = table[row(at, 7), :]
+            g_rows[pl.ds(i * 32 + r, 1), :] = gtab[pl.ds(slot[b * tb + i * 32 + r], 1), :]
         return 0
 
     lax.fori_loop(0, tb // 32, move, 0)
@@ -417,21 +411,19 @@
     mine = jnp.broadcast_to(idx[pl.ds(b, 1), :], (LANES, tb)).T == lane.astype(F32)
     onehot = jnp.where(mine, 1.0, 0.0)
     gate = jnp.sum(jnp.where(mine, prob, 0.0), axis=1, keepdims=True)
-    g = stage3[:, 6 * 8:7 * 8, :].reshape(tb, LANES)
     v = v_row[0:1, :]
     spread = jnp.sum(prob * v, axis=1, keepdims=True)
-    dlog = gate * g * (onehot - prob) + prob * (v - spread) + (z_coef * z) * prob
+    dlog = gate * g_rows[...] * (onehot - prob) + prob * (v - spread) + (z_coef * z) * prob
     hi = dlog.astype(BF16).astype(F32)
     mid = (dlog - hi).astype(BF16).astype(F32)
     low = dlog - hi - mid
+
     def at(piece, k):
         return piece if k == 0 else pltpu.roll(piece, k * num_experts, 1)
+
     pieces = at(hi, 0) + at(mid, 1) + at(low, 2) + at(hi, 3) + at(mid, 4) + at(hi, 5)
-    dx = nn(pieces.astype(BF16), wr_back[...])
+    pieces_out[...] = pieces.astype(BF16)
     pieces_t[...] = pieces.T.astype(BF16)
-    for j in range(ROW_TILES):
-        cols = slice(j * LANES, (j + 1) * LANES)
-        grad_x[:, cols] = (stage3[:, j * 8:(j + 1) * 8, :].reshape(tb, LANES) + dx[:, cols]).astype(BF16)
     acc[...] += nn(pieces_t[...], xv)
     p_acc[...] += jnp.sum(prob.reshape(tb // 8, 8, LANES), axis=0)
     z_acc[...] += jnp.sum(jnp.broadcast_to(z * z, (tb, LANES)).reshape(tb // 8, 8, LANES), axis=0)
@@ -445,36 +437,99 @@
         partial[n:n + 1, LANES:2 * LANES] = jnp.sum(z_acc[...], axis=0, keepdims=True)
 
 
-def token_side(num_experts, z_coef, addr, x, idx, wr, wr_back, v_row, dback, gback):
+def whole(a):
+    return pl.BlockSpec(a.shape, lambda b, addr: (0,) * a.ndim)
+
+
+def router_side(num_experts, z_coef, slot, x, idx, wr, v_row, gback):
     tokens, d_model = x.shape
-    n_dev, n_local, cap, _ = dback.shape
+    n_dev, n_local, _, cap = gback.shape
+    tb = 512
+    idx = idx.astype(F32).reshape(tokens // tb, tb)
+    gback = gback.reshape(n_dev * n_local, cap)
+    rows = num_experts + 8
+    return pl.pallas_call(
+        lambda *refs: router_kernel(num_experts, z_coef, *refs),
+        out_shape=(jax.ShapeDtypeStruct((tokens, LANES), BF16), jax.ShapeDtypeStruct((rows, d_model), F32), jax.ShapeDtypeStruct((LANES, d_model), F32)),
+        grid_spec=pltpu.PrefetchScalarGridSpec(
+            num_scalar_prefetch=1, grid=(tokens // tb,),
+            in_specs=[pl.BlockSpec((tb, d_model), lambda b, addr: (b, 0)), whole(idx), whole(wr), whole(v_row), whole(gback)],
+            out_specs=[pl.BlockSpec((tb, LANES), lambda b, addr: (b, 0)), pl.BlockSpec((rows, d_model), lambda b, addr: (0, 0)),
+                       pl.BlockSpec((LANES, d_model), lambda b, addr: (0, 0))],
+            scratch_shapes=[
+                pltpu.VMEM((n_dev * n_local * cap + 8, LANES), F32), pltpu.VMEM((tb, LANES), F32),
+                pltpu.VMEM((LANES, tb), BF16), pltpu.VMEM((8, LANES), F32), pltpu.VMEM((8, LANES), F32)]),
+        cost_estimate=pl.CostEstimate(flops=40 * 10 ** 9, bytes_accessed=16 * 2 ** 20, transcendentals=0),
+        compiler_params=pltpu.CompilerParams(vmem_limit_bytes=40 * 2 ** 20),
+        name='router_side',
+    )(slot, x, idx, wr, v_row, gback)
+
+
+def combine_kernel(addr, pieces, wr_back, dback, dlast, grad_x, stage, table, inb, in_sem):
+    b = pl.program_id(0)
+    tb = pieces.shape[0]
+    n_out, cap, d_model = dlast.shape
+    n_local = dback.shape[1] + 1
+    groups = cap // 8
+    tiled = table.reshape(table.shape[0] // PITCH, PITCH, LANES)
+    stage3 = stage.reshape(tb // 8, PITCH, LANES)
+
+    @pl.when(b == 0)
+    def _():
+        def fetch(d, e):
+            source = dback.at[d, e] if e < n_local - 1 else dlast.at[d]
+            return pltpu.make_async_copy(source, inb.at[e], in_sem.at[e])
+
+        for e in range(n_local):
+            fetch(0, e).start()
+        tiled[n_out * n_local * groups] = jnp.zeros((PITCH, LANES), F32)
+
+        def fill(d, _):
+            for e in range(n_local):
+                fetch(d, e).wait()
+                for j in range(ROW_TILES):
+                    part = inb[e, :, j * LANES:(j + 1) * LANES].astype(F32)
+                    tiled[pl.ds((d * n_local + e) * groups, groups), j * 8:(j + 1) * 8, :] = part.reshape(groups, 8, LANES)
+
+                @pl.when(d + 1 < n_out)
+                def _():
+                    fetch(d + 1, e).start()
+            return 0
+
+        lax.fori_loop(0, n_out, fill, 0)
+
+    def move(i, _):
+        for r in range(32):
+            at = addr[b * tb + i * 32 + r]
+            stage[row(i * (4 * PITCH) + (r // 8) * PITCH + r % 8, ROW_TILES), :] = table[row(at, ROW_TILES), :]
+        return 0
+
+    lax.fori_loop(0, tb // 32, move, 0)
+    for j in range(ROW_TILES):
+        cols = slice(j * LANES, (j + 1) * LANES)
+        grad_x[:, cols] = (stage3[:, j * 8:(j + 1) * 8, :].reshape(tb, LANES) + nn(pieces[...], wr_back[:, cols])).astype(BF16)
+
+
+def combine(addr, pieces, wr_back, dback, dlast):
+    tokens = pieces.shape[0]
+    n_dev, cap, d_model = dlast.shape
+    n_local = dback.shape[1] + 1
     tb = 512
     hbm = pl.BlockSpec(memory_space=pl.ANY)
-    idx = idx.astype(F32).reshape(tokens // tb, tb)
-    gback = gback.reshape(n_dev * n_local, cap)
-
-    def whole(a):
-        return pl.BlockSpec(a.shape, lambda b, addr: (0,) * a.ndim)
-
     n_groups = n_dev * n_local * cap // 8 + 1
-    rows = num_experts + 8
     return pl.pallas_call(
-        lambda *refs: token_kernel(num_experts, z_coef, *refs),
-        out_shape=(jax.ShapeDtypeStruct(x.shape, BF16), jax.ShapeDtypeStruct((rows, d_model), F32), jax.ShapeDtypeStruct((LANES, d_model), F32)),
+        combine_kernel,
+        out_shape=jax.ShapeDtypeStruct((tokens, d_model), BF16),
         grid_spec=pltpu.PrefetchScalarGridSpec(
             num_scalar_prefetch=1, grid=(tokens // tb,),
-            in_specs=[pl.BlockSpec((tb, d_model), lambda b, addr: (b, 0)), whole(idx),
-                      whole(wr), whole(wr_back), whole(v_row), hbm, whole(gback)],
-            out_specs=[pl.BlockSpec((tb, d_model), lambda b, addr: (b, 0)), pl.BlockSpec((rows, d_model), lambda b, addr: (0, 0)),
-                       pl.BlockSpec((LANES, d_model), lambda b, addr: (0, 0))],
+            in_specs=[pl.BlockSpec((tb, LANES), lambda b, addr: (b, 0)), whole(wr_back), hbm, hbm],
+            out_specs=pl.BlockSpec((tb, d_model), lambda b, addr: (b, 0)),
             scratch_shapes=[
                 pltpu.VMEM((tb // 8 * PITCH, LANES), F32), pltpu.VMEM((n_groups * PITCH, LANES), F32),
-                pltpu.VMEM((2, cap, d_model), BF16),
-                pltpu.VMEM((LANES, tb), BF16), pltpu.VMEM((8, LANES), F32), pltpu.VMEM((8, LANES), F32),
-                pltpu.SemaphoreType.DMA((2,))]),
-        compiler_params=pltpu.CompilerParams(vmem_limit_bytes=60 * 2 ** 20),
-        name='token_side',
-    )(addr, x, idx, wr, wr_back, v_row, dback, gback)
+                pltpu.VMEM((n_local, cap, d_model), BF16), pltpu.SemaphoreType.DMA((n_local,))]),
+        compiler_params=pltpu.CompilerParams(vmem_limit_bytes=56 * 2 ** 20),
+        name='combine_rows',
+    )(addr, pieces, wr_back, dback, dlast)
 
 
 def total_kernel(n_dev, part, out, stats, parts, send_sem, recv_sem):
@@ -511,6 +566,19 @@
     )(part)
 
 
+def copy_kernel(source, sink):
+    sink[...] = source[...]
+
+
+def own_copy(a):
+    n, rows, cols = a.shape
+    spec = pl.BlockSpec((1, rows // 6, cols), lambda e, r: (e, r, 0))
+    return pl.pallas_call(
+        copy_kernel, out_shape=jax.ShapeDtypeStruct(a.shape, a.dtype), grid=(n, 6), in_specs=[spec], out_specs=spec,
+        cost_estimate=pl.CostEstimate(flops=15 * 10 ** 9, bytes_accessed=2 * a.size * 4, transcendentals=0),
+        name='own_copy')(a)
+
+
 def solution(mesh):
     n_dev = mesh.shape['ep']
 
@@ -529,17 +597,21 @@
         wr_back = jnp.pad(jnp.concatenate([w.T for w in (w_hi, w_hi, w_hi, w_mid, w_mid, w_low)]), ((0, LANES - 6 * num_experts), (0, 0)))
         cnt = jnp.broadcast_to(jnp.pad(counts.astype(F32), (0, LANES - num_experts))[None], (8, LANES))
 
-        _, _, _, d_back, g_back, gwin, gwout_t, cnt_all = expert_exchange(n_dev, xs, dys, wr, cnt, w_in, w_out)
+        _, _, _, d_back, d_last, g_back, gwin, gwout_t, cnt_all = expert_exchange(n_dev, xs, dys, wr, cnt, w_in, w_out)
+        d_last = lax.all_to_all(d_last, 'ep', 0, 0, tiled=True)
         load_row = jnp.sum(cnt_all, axis=0) / total_tok
         v_row = AUX_WEIGHT * num_experts * load_row / total_tok
-        grad_x, partial, _ = token_side(num_experts, 2.0 * Z_WEIGHT / total_tok, addr, x_tokens, expert_idx, wr, wr_back, v_row, d_back, g_back)
+        pieces, partial, _ = router_side(num_experts, 2.0 * Z_WEIGHT / total_tok, tok_slot, x_tokens, expert_idx, wr, v_row, g_back)
+        grad_w_out = jnp.swapaxes(gwout_t, 1, 2)
+        grad_w_in = own_copy(gwin)
+        pieces, partial, grad_w_in, grad_w_out = lax.optimization_barrier((pieces, partial, grad_w_in, grad_w_out))
+        grad_x = combine(addr, pieces, wr_back, d_back, d_last)
         grad_wr_t, stats = total_over_devices(n_dev, num_experts, partial)
         grad_w_router = grad_wr_t.T
         mean_prob = stats[0, :num_experts] / total_tok
         aux_loss = AUX_WEIGHT * num_experts * jnp.sum(load_row[0, :num_experts] * mean_prob)
         z_loss = Z_WEIGHT * stats[0, LANES] / total_tok
-        grad_w_out = jnp.swapaxes(gwout_t, 1, 2)
-        return grad_x, gwin, grad_w_out, grad_w_router, aux_loss, z_loss
+        return grad_x, grad_w_in, grad_w_out, grad_w_router, aux_loss, z_loss
 
     return jax.shard_map(expert_layer, mesh=mesh,
                          in_specs=(P('ep', None), P(None, None), P('ep'), P('ep', None, None), P('ep', None, None), P('ep', None)),

time: 711 us -> 639 us (0.90)
  Pallas kernels: 652 us -> 591 us
  local copies, waits for them, and re-layouts: 37.6 us -> 25.3 us
    pallas_call x1, Pallas kernels: 515 us -> 431 us  [expert_exchange(): pl.pallas_call(lambda *refs: expert_kernel(n_dev, n_local, num_experts, b...]
    pallas_call x1 -> x3, Pallas kernels: 73.5 us -> 95.6 us  [the longest x1 45 us: router_side(): pl.pallas_call(lambda *refs: router_kernel(num_experts, z_coef, *refs), o...]
    unnamed x8 -> x17, local copies, waits for them, and re-layouts: 32.2 us -> 21.2 us
  transfers between devices with their start and end apart: 0 -> 1, of which waited for: 0 -> 0; matrix products, arithmetic and copies ran while one was open for 0% -> 3% of each run, Pallas kernels for 0% -> 12%
where the time goes in v3:
time: 639 us; the launch traced here: 637 us
  Pallas kernels  591 us (92%)
  local copies, waits for them, and re-layouts  25.3 us (4%)
  other arithmetic  12.7 us (2%)
    pallas_call x1, Pallas kernels, expert_exchange(): pl.pallas_call(lambda *refs: expert_kernel(n_dev, n_local, num_experts, b...  431 us
    pallas_call x1, Pallas kernels, permute(): pl.pallas_call(lambda *refs: permute_kernel(tb, *refs), out_shape=(out, o...  52.7 us
    pallas_call x1, Pallas kernels, router_side(): pl.pallas_call(lambda *refs: router_kernel(num_experts, z_coef, *refs), o...  45 us
    pallas_call x1, Pallas kernels, combine(): pl.pallas_call(combine_kernel, out_shape=jax.ShapeDtypeStruct((tokens, d_...  33.7 us
    unnamed x17, local copies, waits for them, and re-layouts  21.2 us
    pallas_call x1, Pallas kernels, own_copy(): pl.pallas_call(copy_kernel, out_shape=jax.ShapeDtypeStruct(a.shape, a.dty...  16.9 us
  transfers between devices with their start and end apart: 1, of which 0 were waited for; matrix products, arithmetic and copies ran while one was open for 3% of the time, Pallas kernels for 12%

profile of v3, /device:TPU:1, one launch (start us, length us, event | category | flops | bytes accessed | tf_op | source)
XLA Modules:
  0.0 637.3 jit_solution(11120912678489400626)
XLA Ops:
  0.6 0.8 fusion.2
  1.4 4.8 reduce-window.6
  6.2 0.5 slice_reduce_fusion
  6.7 0.2 reduce-window.9
  7.0 0.2 broadcast_add_fusion
  7.2 1.3 convert_reduce_fusion
  8.5 1.5 fusion.5
  10.0 0.8 bitcast_dynamic-update-slice_fusion.4
  10.8 0.8 bitcast_dynamic-update-slice_fusion.1
  11.6 0.8 bitcast_dynamic-update-slice_fusion
  12.5 0.1 pad_maximum_fusion
  12.6 1.1 copy.16.refs_2_.refs_3_
  13.6 52.7 %permute_rows.1 = (bf16[8,2,640,768]{3,2,1,0:T(8,128)(2,1)}, bf16[8,2,640,768]{3,2,1,0:T(8,128)(2,1)}) custom-call(s32[8192]{0:T(1024)} %get-tuple-element.58.refs_0_.addr, bf16[8192,768]{1,0:T(8,128)(2,1)} %refs_1_.3, bf16[8192,768]{1,0:T(8,128)(2,1)} %refs_2_.1), custom_call_target="tpu_custom_call" | custom-call | tf_op jit(solution)/shard_map/permute_rows/pallas_call | solution.py:364
  66.3 0.6 broadcast_in_dim.7.refs_3_
  66.9 430.6 %expert_exchange.1 = (bf16[8,2,640,768]{3,2,1,0:T(8,128)(2,1)}, bf16[8,2,640,768]{3,2,1,0:T(8,128)(2,1)}, bf16[8,1,640,768]{3,2,1,0:T(8,128)(2,1)}, bf16[8,1,640...) custom-call(bf16[8,2,640,768]{3,2,1,0:T(8,128)(2,1)} %get-tuple-elem, ...), custom_call_target="tpu_custom_call" | custom-call | tf_op jit(solution)/shard_map/expert_exchange/pallas_call | solution.py:269
  497.5 0.0 copy-start.5
  497.6 0.0 copy-start.4
  497.6 3.8 all-to-all-start
  501.4 0.1 reduce.2
  501.6 0.0 copy-start
  501.6 16.9 %own_copy.1 = f32[2,768,3072]{2,1,0:T(8,128)} custom-call(f32[2,768,3072]{2,1,0:T(8,128)} %get-tuple-element.28.source), custom_call_target="tpu_custom_call" | custom-call | flops 15000000512 | bytes 37748736 | tf_op jit(solution)/shard_map/own_copy/pallas_call | solution.py:576
  518.5 45.0 %router_side.1 = (bf16[8192,128]{1,0:T(8,128)(2,1)S(1)}, f32[24,768]{1,0:T(8,128)S(1)}, f32[128,768]{1,0:T(8,128)}) custom-call(s32[8192]{0:T(1024)S(1)} %get-tuple-element.59.refs_0_, bf16[8192,768]{1,0:T(8,128)(2,1)} %refs_1_.3, f32[16,512]{1,0:T(8,128)S(1)} %reshape.41.refs_2_, bf16[3,768,128]{2,1,0:T(8,128)(2,1)S(1)} %copy-done, ...), custom_call_target="tpu_custom_call" | custom-call | flops 40000000000 | bytes 16777216 | tf_op jit(solution)/shard_map/router_side/pallas_call | solution.py:451
  563.5 1.3 copy-done.1
  564.8 0.6 copy-done.2
  565.4 18.6 %copy.17 = f32[2,3072,768]{2,1,0:T(8,128)} copy(f32[2,3072,768]{1,2,0:T(8,128)} %bitcast.33) | data formatting | bytes 37748736
  584.0 12.2 %device_total.1 = (f32[16,768]{1,0:T(8,128)}, f32[8,768]{1,0:T(8,128)}) custom-call(f32[24,768]{1,0:T(8,128)} %copy-done.2), custom_call_target="tpu_custom_call" | custom-call | tf_op jit(solution)/shard_map/device_total/pallas_call | solution.py:559
  596.2 1.2 slice.19
  597.4 0.7 pad.22.wr_back
  598.1 1.3 multiply_reduce_fusion
  600.7 0.0 all-to-all-done.dlast
  600.7 33.7 %combine_rows.1 = bf16[8192,768]{1,0:T(8,128)(2,1)} custom-call(s32[8192]{0:T(1024)} %get-tuple-element.58.refs_0_.addr, bf16[8192,128]{1,0:T(8,128)(2,1)} %copy-done.1, bf16[128,768]{1,0:T(8,128)(2,1)} %pad.22.wr_back, bf16[8,1,640,768]{3,2,1,0:T(8,128)(2,1)} %get-tuple-element.31.dback, bf16[8,640,768]{2,1,0:T(8,128)(2,1)} %all-to-all-done.dlast), custom_call_target="tpu_custom_call" | custom-call | tf_op jit(solution)/shard_map/combine_rows/pallas_call | solution.py:520
  634.4 0.6 copy.27
  (18 shorter events, 0.1 us)
Async XLA Ops:
  497.5 3.8 copy-start.5
  497.6 3.8 copy-start.4
  497.6 103.1 %all-to-all-start = ((bf16[8,640,768]{2,1,0:T(8,128)(2,1)}), bf16[8,640,768]{2,1,0:T(8,128)(2,1)}, u32[]{:S(2)}, u32[]{:S(2)}) async-start(bf16[8,640,768]{2,1,0:T(8,128)(2,1)} %get-tuple-element.32), calls=%async_computation | async-start | bytes 15728640 | tf_op jit(solution)/shard_map/all_to_all | solution.py:601
  501.6 16.9 %copy-start = (bf16[3,768,128]{2,1,0:T(8,128)(2,1)S(1)}, bf16[3,768,128]{2,1,0:T(8,128)(2,1)}, u32[]{:S(2)}) copy-start(bf16[3,768,128]{2,1,0:T(8,128)(2,1)} %copy.16.refs_2_.refs_3_) | copy-start | bytes 1769476
  563.5 1.3 copy-start.1
  564.8 0.6 copy-start.2
  600.7 33.8 %copy-start.3 = (f32[16,768]{1,0:T(8,128)S(1)}, f32[16,768]{1,0:T(8,128)}, u32[]{:S(2)}) copy-start(f32[16,768]{1,0:T(8,128)} %get-tuple-element.36) | copy-start | bytes 147460

commit v4 on v3

--- a/solution.py
+++ b/solution.py
@@ -21,9 +21,15 @@
 
 
 def split3(w):
-    hi = lax.reduce_precision(w, 8, 7)
-    mid = lax.reduce_precision(w - hi, 8, 7)
-    return hi.astype(BF16), mid.astype(BF16), (w - hi - mid).astype(BF16)
+    hi = w.astype(BF16).astype(F32)
+    mid = (w - hi).astype(BF16).astype(F32)
+    return hi, mid, w - hi - mid
+
+
+def six_terms(w):
+    hi, mid, low = split3(w)
+    pad = jnp.zeros((LANES - 6 * w.shape[0], w.shape[1]), F32)
+    return jnp.concatenate([hi, hi, hi, mid, mid, low, pad], axis=0).astype(BF16)
 
 
 def nt(a, b):
@@ -34,9 +40,9 @@
     return jnp.dot(a, b, preferred_element_type=F32)
 
 
-def expert_kernel(n_dev, n_local, num_experts, blk, xs, dys, wr, cnt, w_in, w_out,
+def expert_kernel(n_dev, n_local, num_experts, blk, xs, dys, w_t, cnt, w_in, w_out,
                   xr, dyr, dsend, dback, dlast, gback, gwin, gwout_t, cnt_all,
-                  xv, dyv, gv, x_t, g_t, win_v, wout_v, acc_in, acc_out, o_acc, r_acc, r_out, g_all,
+                  xv, dyv, gv, x_t, g_t, wr, win_v, wout_v, acc_in, acc_out, o_acc, r_acc, r_out, g_all,
                   x_send, x_recv, dy_send, dy_recv, r_send, r_recv, s_send, s_recv, c_send, c_recv, ld_sem, st_sem, w_sem, flush_sem, own_sem):
     me = lax.axis_index('ep')
     n_blk = w_in.shape[2] // blk
@@ -161,6 +167,9 @@
     for cp in weights(0):
         cp.start()
     load(0, 0, 0, lambda cp: cp.start())
+    for at, piece in enumerate(split3(w_t[...])):
+        pad = jnp.zeros((LANES - num_experts, piece.shape[1]), F32)
+        wr[at] = jnp.concatenate([piece, pad], axis=0).T.astype(BF16)
 
     def chunk(c, _):
         e, i = c // n_dev, c % n_dev
@@ -252,7 +261,7 @@
             s_copy(k, e).wait()
 
 
-def expert_exchange(n_dev, xs, dys, wr, cnt, w_in, w_out):
+def expert_exchange(n_dev, xs, dys, w_t, cnt, w_in, w_out):
     n_local, d_model, d_ff = w_in.shape
     cap = xs.shape[2]
     num_experts = n_dev * n_local
@@ -273,7 +282,7 @@
         out_specs=[hbm] * 9,
         scratch_shapes=[
             pltpu.VMEM((2, cap, d_model), BF16), pltpu.VMEM((2, cap, d_model), BF16), pltpu.VMEM((cap, d_model), BF16),
-            pltpu.VMEM((d_model, cap), BF16), pltpu.VMEM((d_model, cap), BF16),
+            pltpu.VMEM((d_model, cap), BF16), pltpu.VMEM((d_model, cap), BF16), pltpu.VMEM((3, d_model, LANES), BF16),
             pltpu.VMEM((d_model, d_ff), BF16), pltpu.VMEM((d_ff, d_model), BF16),
             pltpu.VMEM((d_model, d_ff), F32), pltpu.VMEM((d_model, d_ff), F32),
             pltpu.VMEM((cap, d_model), F32), pltpu.VMEM((cap, d_model), F32),
@@ -283,7 +292,7 @@
         ],
         compiler_params=pltpu.CompilerParams(collective_id=0, has_side_effects=True, vmem_limit_bytes=63 * 2 ** 20),
         name='expert_exchange',
-    )(xs, dys, wr, cnt, w_in, w_out)
+    )(xs, dys, w_t, cnt, w_in, w_out)
 
 
 PITCH = 6 * 8
@@ -306,26 +315,32 @@
     stage3 = stage.reshape(tb // 8, PITCH, LANES)
     n_in = tokens // tb
 
+    n_buf = inb.shape[0]
+    n_chunk = n_out * n_local
+
     def fetch(source, b):
-        return pltpu.make_async_copy(source.at[pl.ds(pl.multiple_of(b * tb, tb), tb), :], inb.at[b % 2], in_sem.at[b % 2])
+        return pltpu.make_async_copy(source.at[pl.ds(pl.multiple_of(b * tb, tb), tb), :], inb.at[b % n_buf], in_sem.at[b % n_buf])
 
     def emit(sink, c):
-        return pltpu.make_async_copy(outb.at[c % 2], sink.at[c // n_local, c % n_local], out_sem.at[c % 2])
-
-    fetch(x_hbm, 0).start()
+        return pltpu.make_async_copy(outb.at[c], sink.at[c // n_local, c % n_local], out_sem.at[c])
+
+    for b in range(n_buf - 1):
+        fetch(x_hbm, b).start()
     table[...] = jnp.zeros_like(table)
-    for source, sink, follow in ((x_hbm, xs, dy_hbm), (dy_hbm, dys, None)):
+    for source, sink, follow, before in ((x_hbm, xs, dy_hbm, None), (dy_hbm, dys, None, xs)):
         def scatter(b, _):
-            @pl.when(b + 1 < n_in)
+            ahead = b + n_buf - 1
+
+            @pl.when(ahead < n_in)
             def _():
-                fetch(source, b + 1).start()
+                fetch(source, ahead).start()
             if follow is not None:
-                @pl.when(b + 1 == n_in)
+                @pl.when(ahead >= n_in)
                 def _():
-                    fetch(follow, 0).start()
+                    fetch(follow, ahead - n_in).start()
             fetch(source, b).wait()
             for j in range(ROW_TILES):
-                part = inb[b % 2, :, j * LANES:(j + 1) * LANES].astype(F32)
+                part = inb[b % n_buf, :, j * LANES:(j + 1) * LANES].astype(F32)
                 stage3[:, j * 8:(j + 1) * 8, :] = part.reshape(tb // 8, 8, LANES)
 
             def move(i, _):
@@ -340,19 +355,21 @@
         lax.fori_loop(0, n_in, scatter, 0)
 
         def drain(c, _):
-            @pl.when(c >= 2)
-            def _():
-                emit(sink, c - 2).wait()
+            if before is not None:
+                emit(before, c).wait()
             for j in range(ROW_TILES):
                 part = tiled[pl.ds(c * groups, groups), j * 8:(j + 1) * 8, :].reshape(cap, LANES)
-                outb[c % 2, :, j * LANES:(j + 1) * LANES] = part.astype(BF16)
+                outb[c, :, j * LANES:(j + 1) * LANES] = part.astype(BF16)
             emit(sink, c).start()
             return 0
 
-        n_chunk = n_out * n_local
         lax.fori_loop(0, n_chunk, drain, 0)
-        for c in (n_chunk - 2, n_chunk - 1):
-            emit(sink, c).wait()
+
+    def finish(c, _):
+        emit(dys, c).wait()
+        return 0
+
+    lax.fori_loop(0, n_chunk, finish, 0)
 
 
 def permute(n_dev, n_local, capacity, addr, x, dy):
@@ -367,23 +384,25 @@
         grid_spec=pltpu.PrefetchScalarGridSpec(
             num_scalar_prefetch=1, grid=(), in_specs=[hbm, hbm], out_specs=[hbm, hbm],
             scratch_shapes=[
-                pltpu.VMEM((2, tb, d_model), BF16), pltpu.VMEM((tb // 8 * PITCH, LANES), F32), pltpu.VMEM((n_groups * PITCH, LANES), F32),
-                pltpu.VMEM((2, capacity, d_model), BF16), pltpu.SemaphoreType.DMA((2,)), pltpu.SemaphoreType.DMA((2,))]),
+                pltpu.VMEM((4, tb, d_model), BF16), pltpu.VMEM((tb // 8 * PITCH, LANES), F32), pltpu.VMEM((n_groups * PITCH, LANES), F32),
+                pltpu.VMEM((n_dev * n_local, capacity, d_model), BF16), pltpu.SemaphoreType.DMA((4,)), pltpu.SemaphoreType.DMA((n_dev * n_local,))]),
         compiler_params=pltpu.CompilerParams(vmem_limit_bytes=60 * 2 ** 20),
         name='permute_rows',
     )(addr, x, dy)
 
 
-def router_kernel(num_experts, z_coef, slot, x, idx, wr, v_row, gback, pieces_out, partial, acc, gtab, g_rows, pieces_t, p_acc, z_acc):
+def router_kernel(z_coef, slot, x, idx, w_t, v_col, gback, pieces_out, partial, acc, gtab, g_rows, w_six, pieces_t, p_acc, z_acc):
     b = pl.program_id(0)
     tb = x.shape[0]
     n_chunk, cap = gback.shape
+    n = w_t.shape[0]
 
     @pl.when(b == 0)
     def _():
         acc[...] = jnp.zeros_like(acc)
         p_acc[...] = jnp.zeros_like(p_acc)
         z_acc[...] = jnp.zeros_like(z_acc)
+        w_six[...] = six_terms(w_t[...])
         gtab[n_chunk * cap:, :] = jnp.zeros((8, LANES), F32)
 
         def fill(c, _):
@@ -400,72 +419,70 @@
     lax.fori_loop(0, tb // 32, move, 0)
 
     xv = x[...]
-    logits = nn(xv, wr[0]) + nn(xv, wr[1]) + nn(xv, wr[2])
-    lane = lax.broadcasted_iota(jnp.int32, logits.shape, 1)
-    real = lane < num_experts
-    top = jnp.max(jnp.where(real, logits, -1e30), axis=1, keepdims=True)
-    expd = jnp.where(real, jnp.exp(jnp.minimum(logits - top, 0.0)), 0.0)
-    total = jnp.sum(expd, axis=1, keepdims=True)
+    terms = nt(w_six[...], xv)
+    logits = terms[0:n] + terms[3 * n:4 * n] + terms[5 * n:6 * n]
+    top = jnp.max(logits, axis=0, keepdims=True)
+    expd = jnp.exp(logits - top)
+    total = jnp.sum(expd, axis=0, keepdims=True)
     prob = expd / total
     z = top + jnp.log(total)
-    mine = jnp.broadcast_to(idx[pl.ds(b, 1), :], (LANES, tb)).T == lane.astype(F32)
+    mine = lax.broadcasted_iota(jnp.int32, logits.shape, 0).astype(F32) == idx[pl.ds(b, 1), :]
     onehot = jnp.where(mine, 1.0, 0.0)
-    gate = jnp.sum(jnp.where(mine, prob, 0.0), axis=1, keepdims=True)
-    v = v_row[0:1, :]
-    spread = jnp.sum(prob * v, axis=1, keepdims=True)
-    dlog = gate * g_rows[...] * (onehot - prob) + prob * (v - spread) + (z_coef * z) * prob
-    hi = dlog.astype(BF16).astype(F32)
-    mid = (dlog - hi).astype(BF16).astype(F32)
-    low = dlog - hi - mid
-
-    def at(piece, k):
-        return piece if k == 0 else pltpu.roll(piece, k * num_experts, 1)
-
-    pieces = at(hi, 0) + at(mid, 1) + at(low, 2) + at(hi, 3) + at(mid, 4) + at(hi, 5)
-    pieces_out[...] = pieces.astype(BF16)
-    pieces_t[...] = pieces.T.astype(BF16)
+    gate = jnp.sum(jnp.where(mine, prob, 0.0), axis=0, keepdims=True)
+    g = g_rows[...].T[0:1, :]
+    v = v_col[:, 0:1]
+    spread = jnp.sum(prob * v, axis=0, keepdims=True)
+    dlog = gate * g * (onehot - prob) + prob * (v - spread) + (z_coef * z) * prob
+    hi, mid, low = split3(dlog)
+    pieces = jnp.concatenate([hi, mid, low, hi, mid, hi, jnp.zeros((LANES - 6 * n, tb), F32)], axis=0)
+    pieces_out[...] = pieces.T.astype(BF16)
+    pieces_t[...] = pieces.astype(BF16)
     acc[...] += nn(pieces_t[...], xv)
-    p_acc[...] += jnp.sum(prob.reshape(tb // 8, 8, LANES), axis=0)
-    z_acc[...] += jnp.sum(jnp.broadcast_to(z * z, (tb, LANES)).reshape(tb // 8, 8, LANES), axis=0)
+    zz = z * z
+    for j in range(tb // LANES):
+        p_acc[...] += prob[:, j * LANES:(j + 1) * LANES]
+        z_acc[0:1, :] += zz[:, j * LANES:(j + 1) * LANES]
 
     @pl.when(b == pl.num_programs(0) - 1)
     def _():
-        n = num_experts
         partial[...] = jnp.zeros_like(partial)
         partial[0:n, :] = acc[0:n, :] + acc[n:2 * n, :] + acc[2 * n:3 * n, :]
-        partial[n:n + 1, 0:LANES] = jnp.sum(p_acc[...], axis=0, keepdims=True)
-        partial[n:n + 1, LANES:2 * LANES] = jnp.sum(z_acc[...], axis=0, keepdims=True)
+        p_sum = jnp.broadcast_to(jnp.sum(p_acc[...], axis=1, keepdims=True), p_acc.shape)
+        p_full = jnp.concatenate([p_sum, jnp.zeros((LANES - n, LANES), F32)], axis=0).T
+        partial[n:n + 1, 0:LANES] = p_full[0:1, :]
+        partial[n:n + 1, LANES:2 * LANES] = jnp.broadcast_to(jnp.sum(z_acc[0:1, :], axis=1, keepdims=True), (1, LANES))
 
 
 def whole(a):
     return pl.BlockSpec(a.shape, lambda b, addr: (0,) * a.ndim)
 
 
-def router_side(num_experts, z_coef, slot, x, idx, wr, v_row, gback):
+def router_side(z_coef, slot, x, idx, w_t, v_col, gback):
     tokens, d_model = x.shape
     n_dev, n_local, _, cap = gback.shape
     tb = 512
+    n = w_t.shape[0]
     idx = idx.astype(F32).reshape(tokens // tb, tb)
     gback = gback.reshape(n_dev * n_local, cap)
-    rows = num_experts + 8
+    rows = n + 8
     return pl.pallas_call(
-        lambda *refs: router_kernel(num_experts, z_coef, *refs),
+        lambda *refs: router_kernel(z_coef, *refs),
         out_shape=(jax.ShapeDtypeStruct((tokens, LANES), BF16), jax.ShapeDtypeStruct((rows, d_model), F32), jax.ShapeDtypeStruct((LANES, d_model), F32)),
         grid_spec=pltpu.PrefetchScalarGridSpec(
             num_scalar_prefetch=1, grid=(tokens // tb,),
-            in_specs=[pl.BlockSpec((tb, d_model), lambda b, addr: (b, 0)), whole(idx), whole(wr), whole(v_row), whole(gback)],
+            in_specs=[pl.BlockSpec((tb, d_model), lambda b, addr: (b, 0)), whole(idx), whole(w_t), whole(v_col), whole(gback)],
             out_specs=[pl.BlockSpec((tb, LANES), lambda b, addr: (b, 0)), pl.BlockSpec((rows, d_model), lambda b, addr: (0, 0)),
                        pl.BlockSpec((LANES, d_model), lambda b, addr: (0, 0))],
             scratch_shapes=[
-                pltpu.VMEM((n_dev * n_local * cap + 8, LANES), F32), pltpu.VMEM((tb, LANES), F32),
-                pltpu.VMEM((LANES, tb), BF16), pltpu.VMEM((8, LANES), F32), pltpu.VMEM((8, LANES), F32)]),
-        cost_estimate=pl.CostEstimate(flops=40 * 10 ** 9, bytes_accessed=16 * 2 ** 20, transcendentals=0),
+                pltpu.VMEM((n_dev * n_local * cap + 8, LANES), F32), pltpu.VMEM((tb, LANES), F32), pltpu.VMEM((LANES, d_model), BF16),
+                pltpu.VMEM((LANES, tb), BF16), pltpu.VMEM((n, LANES), F32), pltpu.VMEM((8, LANES), F32)]),
+        cost_estimate=pl.CostEstimate(flops=30 * 10 ** 9, bytes_accessed=16 * 2 ** 20, transcendentals=0),
         compiler_params=pltpu.CompilerParams(vmem_limit_bytes=40 * 2 ** 20),
         name='router_side',
-    )(slot, x, idx, wr, v_row, gback)
-
-
-def combine_kernel(addr, pieces, wr_back, dback, dlast, grad_x, stage, table, inb, in_sem):
+    )(slot, x, idx, w_t, v_col, gback)
+
+
+def combine_kernel(addr, pieces, w_t, dback, dlast, grad_x, stage, table, inb, w_six, in_sem):
     b = pl.program_id(0)
     tb = pieces.shape[0]
     n_out, cap, d_model = dlast.shape
@@ -476,24 +493,28 @@
 
     @pl.when(b == 0)
     def _():
+        n_buf = inb.shape[1]
+
         def fetch(d, e):
             source = dback.at[d, e] if e < n_local - 1 else dlast.at[d]
-            return pltpu.make_async_copy(source, inb.at[e], in_sem.at[e])
-
-        for e in range(n_local):
-            fetch(0, e).start()
+            return pltpu.make_async_copy(source, inb.at[e, d % n_buf], in_sem.at[e, d % n_buf])
+
+        for d in range(n_buf):
+            for e in range(n_local):
+                fetch(d, e).start()
+        w_six[...] = six_terms(w_t[...])
         tiled[n_out * n_local * groups] = jnp.zeros((PITCH, LANES), F32)
 
         def fill(d, _):
             for e in range(n_local):
                 fetch(d, e).wait()
                 for j in range(ROW_TILES):
-                    part = inb[e, :, j * LANES:(j + 1) * LANES].astype(F32)
+                    part = inb[e, d % n_buf, :, j * LANES:(j + 1) * LANES].astype(F32)
                     tiled[pl.ds((d * n_local + e) * groups, groups), j * 8:(j + 1) * 8, :] = part.reshape(groups, 8, LANES)
 
-                @pl.when(d + 1 < n_out)
+                @pl.when(d + n_buf < n_out)
                 def _():
-                    fetch(d + 1, e).start()
+                    fetch(d + n_buf, e).start()
             return 0
 
         lax.fori_loop(0, n_out, fill, 0)
@@ -507,10 +528,10 @@
     lax.fori_loop(0, tb // 32, move, 0)
     for j in range(ROW_TILES):
         cols = slice(j * LANES, (j + 1) * LANES)
-        grad_x[:, cols] = (stage3[:, j * 8:(j + 1) * 8, :].reshape(tb, LANES) + nn(pieces[...], wr_back[:, cols])).astype(BF16)
-
-
-def combine(addr, pieces, wr_back, dback, dlast):
+        grad_x[:, cols] = (stage3[:, j * 8:(j + 1) * 8, :].reshape(tb, LANES) + nn(pieces[...], w_six[:, cols])).astype(BF16)
+
+
+def combine(addr, pieces, w_t, dback, dlast):
     tokens = pieces.shape[0]
     n_dev, cap, d_model = dlast.shape
     n_local = dback.shape[1] + 1
@@ -522,17 +543,17 @@
         out_shape=jax.ShapeDtypeStruct((tokens, d_model), BF16),
         grid_spec=pltpu.PrefetchScalarGridSpec(
             num_scalar_prefetch=1, grid=(tokens // tb,),
-            in_specs=[pl.BlockSpec((tb, LANES), lambda b, addr: (b, 0)), whole(wr_back), hbm, hbm],
+            in_specs=[pl.BlockSpec((tb, LANES), lambda b, addr: (b, 0)), whole(w_t), hbm, hbm],
             out_specs=pl.BlockSpec((tb, d_model), lambda b, addr: (b, 0)),
             scratch_shapes=[
                 pltpu.VMEM((tb // 8 * PITCH, LANES), F32), pltpu.VMEM((n_groups * PITCH, LANES), F32),
-                pltpu.VMEM((n_local, cap, d_model), BF16), pltpu.SemaphoreType.DMA((n_local,))]),
+                pltpu.VMEM((n_local, 4, cap, d_model), BF16), pltpu.VMEM((LANES, d_model), BF16), pltpu.SemaphoreType.DMA((n_local, 4))]),
         compiler_params=pltpu.CompilerParams(vmem_limit_bytes=56 * 2 ** 20),
         name='combine_rows',
-    )(addr, pieces, wr_back, dback, dlast)
-
-
-def total_kernel(n_dev, part, out, stats, parts, send_sem, recv_sem):
+    )(addr, pieces, w_t, dback, dlast)
+
+
+def total_kernel(n_dev, part, _before_a, _before_b, out, stats, parts, send_sem, recv_sem):
     me = lax.axis_index('ep')
     barrier = pltpu.get_barrier_semaphore()
     peers = [(me + k) % n_dev for k in range(1, n_dev)]
@@ -554,16 +575,16 @@
     stats[...] = total[n:]
 
 
-def total_over_devices(n_dev, n_grad, part):
+def total_over_devices(n_dev, n_grad, part, before):
     vmem = pl.BlockSpec(memory_space=pltpu.VMEM)
     return pl.pallas_call(
         lambda *refs: total_kernel(n_dev, *refs),
         out_shape=(jax.ShapeDtypeStruct((n_grad, part.shape[1]), F32), jax.ShapeDtypeStruct((part.shape[0] - n_grad, part.shape[1]), F32)),
-        in_specs=[vmem], out_specs=[vmem, vmem],
+        in_specs=[vmem] + [pl.BlockSpec(memory_space=pl.ANY)] * 2, out_specs=[vmem, vmem],
         scratch_shapes=[pltpu.VMEM((n_dev,) + part.shape, F32), pltpu.SemaphoreType.DMA((n_dev - 1,)), pltpu.SemaphoreType.DMA((n_dev - 1,))],
         compiler_params=pltpu.CompilerParams(collective_id=1, has_side_effects=True),
         name='device_total',
-    )(part)
+    )(part, *before)
 
 
 def copy_kernel(source, sink):
@@ -591,22 +612,18 @@
         tok_slot, counts = route_slots(expert_idx, num_experts, capacity)
         addr = row_address(tok_slot)
         xs, dys = permute(n_dev, n_local, capacity, addr, x_tokens, grad_y)
-        w_hi, w_mid, w_low = split3(w_router)
-        lanes = ((0, 0), (0, LANES - num_experts))
-        wr = jnp.stack([jnp.pad(w, lanes) for w in (w_hi, w_mid, w_low)])
-        wr_back = jnp.pad(jnp.concatenate([w.T for w in (w_hi, w_hi, w_hi, w_mid, w_mid, w_low)]), ((0, LANES - 6 * num_experts), (0, 0)))
+        w_t = w_router.T
         cnt = jnp.broadcast_to(jnp.pad(counts.astype(F32), (0, LANES - num_experts))[None], (8, LANES))
 
-        _, _, _, d_back, d_last, g_back, gwin, gwout_t, cnt_all = expert_exchange(n_dev, xs, dys, wr, cnt, w_in, w_out)
+        _, _, _, d_back, d_last, g_back, gwin, gwout_t, cnt_all = expert_exchange(n_dev, xs, dys, w_t, cnt, w_in, w_out)
         d_last = lax.all_to_all(d_last, 'ep', 0, 0, tiled=True)
         load_row = jnp.sum(cnt_all, axis=0) / total_tok
-        v_row = AUX_WEIGHT * num_experts * load_row / total_tok
-        pieces, partial, _ = router_side(num_experts, 2.0 * Z_WEIGHT / total_tok, tok_slot, x_tokens, expert_idx, wr, v_row, g_back)
+        v_col = jnp.broadcast_to((AUX_WEIGHT * num_experts * load_row[0, :num_experts] / total_tok)[:, None], (num_experts, LANES))
+        pieces, partial, _ = router_side(2.0 * Z_WEIGHT / total_tok, tok_slot, x_tokens, expert_idx, w_t, v_col, g_back)
         grad_w_out = jnp.swapaxes(gwout_t, 1, 2)
         grad_w_in = own_copy(gwin)
-        pieces, partial, grad_w_in, grad_w_out = lax.optimization_barrier((pieces, partial, grad_w_in, grad_w_out))
-        grad_x = combine(addr, pieces, wr_back, d_back, d_last)
-        grad_wr_t, stats = total_over_devices(n_dev, num_experts, partial)
+        grad_x = combine(addr, pieces, w_t, d_back, d_last)
+        grad_wr_t, stats = total_over_devices(n_dev, num_experts, partial, (grad_w_in, grad_w_out))
         grad_w_router = grad_wr_t.T
         mean_prob = stats[0, :num_experts] / total_tok
         aux_loss = AUX_WEIGHT * num_experts * jnp.sum(load_row[0, :num_experts] * mean_prob)

time: 639 us -> 614 us (0.961)
  Pallas kernels: 591 us -> 570 us
    pallas_call x1, Pallas kernels: 45 us -> 25 us  [router_side(): pl.pallas_call(lambda *refs: router_kernel(z_coef, *refs), out_shape=(jax...]
    pallas_call x1, Pallas kernels: 12.2 us -> 31.9 us  [total_over_devices(): pl.pallas_call(lambda *refs: total_kernel(n_dev, *refs), out_shape=(jax.S...]
    pallas_call x0 -> x1, local copies, waits for them, and re-layouts: none -> 18.6 us  [expert_exchange(): pl.pallas_call(lambda *refs: expert_kernel(n_dev, n_local, num_experts, b...]
    unnamed x17 -> x13, local copies, waits for them, and re-layouts: 21.2 us -> 2.63 us
    pallas_call x1, Pallas kernels: 52.7 us -> 37.4 us  [permute(): pl.pallas_call(lambda *refs: permute_kernel(tb, *refs), out_shape=(out, o...]
where the time goes in v4:
time: 614 us; the launch traced here: 612 us
  Pallas kernels  570 us (93%)
  local copies, waits for them, and re-layouts  23.7 us (4%)
  other arithmetic  10.2 us (2%)
    pallas_call x1, Pallas kernels, expert_exchange(): pl.pallas_call(lambda *refs: expert_kernel(n_dev, n_local, num_experts, b...  430 us
    pallas_call x1, Pallas kernels, permute(): pl.pallas_call(lambda *refs: permute_kernel(tb, *refs), out_shape=(out, o...  37.4 us
    pallas_call x1, Pallas kernels, total_over_devices(): pl.pallas_call(lambda *refs: total_kernel(n_dev, *refs), out_shape=(jax.S...  31.9 us
    pallas_call x1, Pallas kernels, combine(): pl.pallas_call(combine_kernel, out_shape=jax.ShapeDtypeStruct((tokens, d_...  28.4 us
    pallas_call x1, Pallas kernels, router_side(): pl.pallas_call(lambda *refs: router_kernel(z_coef, *refs), out_shape=(jax...  25 us
    pallas_call x1, local copies, waits for them, and re-layouts, expert_exchange(): pl.pallas_call(lambda *refs: expert_kernel(n_dev, n_local, num_experts, b...  18.6 us
    pallas_call x1, Pallas kernels, own_copy(): pl.pallas_call(copy_kernel, out_shape=jax.ShapeDtypeStruct(a.shape, a.dty...  16.9 us
  transfers between devices with their start and end apart: 1, of which 0 were waited for; matrix products, arithmetic and copies ran while one was open for 3% of the time, Pallas kernels for 12%

profile of v4, /device:TPU:1, one launch (start us, length us, event | category | flops | bytes accessed | tf_op | source)
XLA Modules:
  0.0 612.1 jit_solution(399138422928357410)
XLA Ops:
  0.6 0.8 fusion.2
  1.4 4.8 reduce-window.6
  6.2 0.5 slice_reduce_fusion
  6.8 0.2 reduce-window.9
  7.0 0.2 broadcast_add_fusion
  7.2 1.3 convert_reduce_fusion
  8.5 1.5 fusion.4
  10.0 37.4 %permute_rows.1 = (bf16[8,2,640,768]{3,2,1,0:T(8,128)(2,1)}, bf16[8,2,640,768]{3,2,1,0:T(8,128)(2,1)}) custom-call(s32[8192]{0:T(1024)} %get-tuple-element.32.refs_0_.addr, bf16[8192,768]{1,0:T(8,128)(2,1)} %refs_1_.3, bf16[8192,768]{1,0:T(8,128)(2,1)} %refs_2_.1), custom_call_target="tpu_custom_call" | custom-call | tf_op jit(solution)/shard_map/permute_rows/pallas_call | solution.py:381
  47.4 0.6 broadcast_in_dim.9.refs_3_
  48.0 430.3 %expert_exchange.1 = (bf16[8,2,640,768]{3,2,1,0:T(8,128)(2,1)}, bf16[8,2,640,768]{3,2,1,0:T(8,128)(2,1)}, bf16[8,1,640,768]{3,2,1,0:T(8,128)(2,1)}, bf16[8,1,640...) custom-call(bf16[8,2,640,768]{3,2,1,0:T(8,128)(2,1)} %get-tuple-elem, ...), custom_call_target="tpu_custom_call" | custom-call | tf_op jit(solution)/shard_map/expert_exchange/pallas_call | solution.py:278
  478.3 0.0 copy-start.5
  478.3 0.0 copy-start.4
  478.3 4.0 all-to-all-start
  482.3 0.0 copy-done.5
  482.4 0.0 copy-done.4
  482.4 0.1 reduce.2
  482.5 18.6 %copy.13 = f32[2,768,3072]{1,2,0:T(8,128)} copy(f32[2,768,3072]{2,1,0:T(8,128)} %get-tuple-element.26) | data formatting | bytes 37748736 | tf_op jit(solution)/shard_map/expert_exchange/pallas_call | solution.py:278
  501.2 0.0 copy-start.1
  501.2 16.9 %own_copy.1.refs_1_ = f32[2,768,3072]{2,1,0:T(8,128)} custom-call(f32[2,768,3072]{2,1,0:T(8,128)} %get-tuple-element.25.source), custom_call_target="tpu_custom_call" | custom-call | flops 15000000512 | bytes 37748736 | tf_op jit(solution)/shard_map/own_copy/pallas_call | solution.py:597
  518.0 0.1 broadcast_in_dim.10.refs_4_
  518.1 0.0 copy-done.1
  518.1 25.0 %router_side.1 = (bf16[8192,128]{1,0:T(8,128)(2,1)S(1)}, f32[24,768]{1,0:T(8,128)S(1)}, f32[128,768]{1,0:T(8,128)}) custom-call(s32[8192]{0:T(1024)S(1)} %get-tuple-element.33.refs_0_, bf16[8192,768]{1,0:T(8,128)(2,1)} %refs_1_.3, f32[16,512]{1,0:T(8,128)S(1)} %reshape.48.refs_2_, f32[16,768]{1,0:T(8,128)S(1)} %bitcast.23, ...), custom_call_target="tpu_custom_call" | custom-call | flops 30000001024 | bytes 16777216 | tf_op jit(solution)/shard_map/router_side/pallas_call | solution.py:468
  543.1 1.4 copy-done
  544.4 0.6 copy-done.2
  545.1 31.9 %device_total.1 = (f32[16,768]{1,0:T(8,128)}, f32[8,768]{1,0:T(8,128)}) custom-call(f32[24,768]{1,0:T(8,128)} %copy-done.2, f32[2,768,3072]{2,1,0:T(8,128)} %own_copy.1.refs_1_, f32[2,3072,768]{2,1,0:T(8,128)} %bitcast.24), custom_call_target="tpu_custom_call" | custom-call | tf_op jit(solution)/shard_map/device_total/pallas_call | solution.py:580
  577.0 1.2 slice.20
  578.9 1.3 multiply_reduce_fusion
  580.8 0.0 all-to-all-done.dlast
  580.8 0.0 copy-start.3
  580.8 28.4 %combine_rows.1 = bf16[8192,768]{1,0:T(8,128)(2,1)} custom-call(s32[8192]{0:T(1024)} %get-tuple-element.32.refs_0_.addr, bf16[8192,128]{1,0:T(8,128)(2,1)} %copy-done, f32[16,768]{1,0:T(8,128)} %bitcast.22, bf16[8,1,640,768]{3,2,1,0:T(8,128)(2,1)} %get-tuple-element.23.dback, bf16[8,640,768]{2,1,0:T(8,128)(2,1)} %all-to-all-done.dlast), custom_call_target="tpu_custom_call" | custom-call | tf_op jit(solution)/shard_map/combine_rows/pallas_call | solution.py:541
  609.2 0.0 copy-done.3
  609.2 0.6 copy.18
  (9 shorter events, 0.1 us)
Async XLA Ops:
  478.3 4.0 copy-start.5
  478.3 4.0 copy-start.4
  478.3 102.5 %all-to-all-start = ((bf16[8,640,768]{2,1,0:T(8,128)(2,1)}), bf16[8,640,768]{2,1,0:T(8,128)(2,1)}, u32[]{:S(2)}, u32[]{:S(2)}) async-start(bf16[8,640,768]{2,1,0:T(8,128)(2,1)} %get-tuple-element.24), calls=%async_computation | async-start | bytes 15728640 | tf_op jit(solution)/shard_map/all_to_all | solution.py:619
  501.2 16.9 %copy-start.1 = (f32[768,16]{0,1:T(8,128)S(1)}, f32[768,16]{0,1:T(8,128)}, u32[]{:S(2)}) copy-start(f32[768,16]{0,1:T(8,128)} %param.7) | copy-start | bytes 147460
  543.1 1.4 copy-start
  544.4 0.6 copy-start.2
  580.8 28.4 %copy-start.3 = (f32[16,768]{1,0:T(8,128)S(1)}, f32[16,768]{1,0:T(8,128)}, u32[]{:S(2)}) copy-start(f32[16,768]{1,0:T(8,128)} %get-tuple-element.28) | copy-start | bytes 147460

commit v5 on v4

--- a/solution.py
+++ b/solution.py
@@ -13,13 +13,6 @@
 LANES = 128
 
 
-def route_slots(idx_group, num_experts, capacity):
-    onehot = (idx_group[:, None] == jnp.arange(num_experts, dtype=jnp.int32)[None, :]).astype(jnp.int32)
-    position = jnp.sum(jnp.cumsum(onehot, axis=0) * onehot, axis=1) - 1
-    tok_slot = jnp.where(position < capacity, idx_group * capacity + position, num_experts * capacity)
-    return tok_slot, jnp.sum(onehot, axis=0)
-
-
 def split3(w):
     hi = w.astype(BF16).astype(F32)
     mid = (w - hi).astype(BF16).astype(F32)
@@ -40,7 +33,10 @@
     return jnp.dot(a, b, preferred_element_type=F32)
 
 
-def expert_kernel(n_dev, n_local, num_experts, blk, xs, dys, w_t, cnt, w_in, w_out,
+EARLY = ((0, 2), (0, 4))
+
+
+def expert_kernel(n_dev, n_local, num_experts, blk, xs, dys, near_x, near_y, w_t, cnt, w_in, w_out,
                   xr, dyr, dsend, dback, dlast, gback, gwin, gwout_t, cnt_all,
                   xv, dyv, gv, x_t, g_t, wr, win_v, wout_v, acc_in, acc_out, o_acc, r_acc, r_out, g_all,
                   x_send, x_recv, dy_send, dy_recv, r_send, r_recv, s_send, s_recv, c_send, c_recv, ld_sem, st_sem, w_sem, flush_sem, own_sem):
@@ -87,7 +83,8 @@
         c_copy(k).start()
     for e in range(n_local):
         for k in (1, 2, 4, 6, 3, 5, 7):
-            x_copy(k, e).start()
+            if (e, k) not in EARLY:
+                x_copy(k, e).start()
             dy_copy(k, e).start()
 
     order = (0, 1, 2, 4, 6, 3, 5, 7)
@@ -102,21 +99,41 @@
         k = offset_of(i)
         p = peer_of(k)
 
+        early = (e == 0) & ((i == 2) | (i == 3))
+
+        def x_from(source):
+            do(pltpu.make_async_copy(source, xv.at[slot], ld_sem.at[slot, 0]))
+
         @pl.when(i == 0)
         def _():
-            do(pltpu.make_async_copy(xs.at[me, e], xv.at[slot], ld_sem.at[slot, 0]))
+            x_from(xs.at[me, e])
             do(pltpu.make_async_copy(dys.at[me, e], dyv.at[slot], ld_sem.at[slot, 1]))
 
+        @pl.when((e == 0) & (i == 2))
+        def _():
+            x_from(near_x)
+
+        @pl.when((e == 0) & (i == 3))
+        def _():
+            x_from(near_y)
+
+        @pl.when((i > 0) & jnp.logical_not(early))
+        def _():
+            x_from(xr.at[p, e])
+
         @pl.when(i > 0)
         def _():
-            do(pltpu.make_async_copy(xr.at[p, e], xv.at[slot], ld_sem.at[slot, 0]))
             do(pltpu.make_async_copy(dyr.at[p, e], dyv.at[slot], ld_sem.at[slot, 1]))
 
     def arrive(e, i):
+        k = offset_of(i)
+
+        @pl.when((i > 0) & jnp.logical_not((e == 0) & ((i == 2) | (i == 3))))
+        def _():
+            x_copy(k, e).wait_recv()
+
         @pl.when(i > 0)
         def _():
-            k = offset_of(i)
-            x_copy(k, e).wait_recv()
             dy_copy(k, e).wait_recv()
 
     def store(c, do):
@@ -166,7 +183,7 @@
 
     for cp in weights(0):
         cp.start()
-    load(0, 0, 0, lambda cp: cp.start())
+    load(0 * me, 0 * me, 0, lambda cp: cp.start())
     for at, piece in enumerate(split3(w_t[...])):
         pad = jnp.zeros((LANES - num_experts, piece.shape[1]), F32)
         wr[at] = jnp.concatenate([piece, pad], axis=0).T.astype(BF16)
@@ -254,14 +271,15 @@
     for e in range(n_local):
         own_g(e).wait()
         for k in range(1, n_dev):
-            x_copy(k, e).wait_send()
+            if (e, k) not in EARLY:
+                x_copy(k, e).wait_send()
             dy_copy(k, e).wait_send()
             if e < n_local - 1:
                 r_copy(k, e).wait()
             s_copy(k, e).wait()
 
 
-def expert_exchange(n_dev, xs, dys, w_t, cnt, w_in, w_out):
+def expert_exchange(n_dev, xs, dys, near_x, near_y, w_t, cnt, w_in, w_out):
     n_local, d_model, d_ff = w_in.shape
     cap = xs.shape[2]
     num_experts = n_dev * n_local
@@ -278,7 +296,7 @@
     return pl.pallas_call(
         lambda *refs: expert_kernel(n_dev, n_local, num_experts, blk, *refs),
         out_shape=(rows, rows, early, early, late, g_shape, w_shape, w_shape, jax.ShapeDtypeStruct((n_dev,) + cnt.shape, F32)),
-        in_specs=[hbm, hbm, vmem, vmem, hbm, hbm],
+        in_specs=[hbm, hbm, hbm, hbm, vmem, vmem, hbm, hbm],
         out_specs=[hbm] * 9,
         scratch_shapes=[
             pltpu.VMEM((2, cap, d_model), BF16), pltpu.VMEM((2, cap, d_model), BF16), pltpu.VMEM((cap, d_model), BF16),
@@ -292,103 +310,134 @@
         ],
         compiler_params=pltpu.CompilerParams(collective_id=0, has_side_effects=True, vmem_limit_bytes=63 * 2 ** 20),
         name='expert_exchange',
-    )(xs, dys, w_t, cnt, w_in, w_out)
+    )(xs, dys, near_x, near_y, w_t, cnt, w_in, w_out)
 
 
 PITCH = 6 * 8
 ROW_TILES = 6
 
 
-def row_address(slot):
-    return (slot // 8) * PITCH + slot % 8
-
-
 def row(addr, tiles):
     return pl.ds(addr, tiles, stride=8)
 
 
-def permute_kernel(tb, addr, x_hbm, dy_hbm, xs, dys, inb, stage, table, outb, in_sem, out_sem):
-    tokens = x_hbm.shape[0]
-    n_out, n_local, cap, d_model = xs.shape
+TB = 512
+IN_FLIGHT = 4
+
+
+def permute_rows(addr, source, sink, inb, stage, table, outb, in_sem, out_sem, meanwhile):
+    n_out, n_local, cap, d_model = sink.shape
     groups = cap // 8
     tiled = table.reshape(table.shape[0] // PITCH, PITCH, LANES)
-    stage3 = stage.reshape(tb // 8, PITCH, LANES)
-    n_in = tokens // tb
-
-    n_buf = inb.shape[0]
+    stage3 = stage.reshape(TB // 8, PITCH, LANES)
+    n_in = source.shape[0] // TB
     n_chunk = n_out * n_local
 
-    def fetch(source, b):
-        return pltpu.make_async_copy(source.at[pl.ds(pl.multiple_of(b * tb, tb), tb), :], inb.at[b % n_buf], in_sem.at[b % n_buf])
-
-    def emit(sink, c):
+    def fetch(b):
+        return pltpu.make_async_copy(source.at[pl.ds(pl.multiple_of(b * TB, TB), TB), :], inb.at[b % IN_FLIGHT], in_sem.at[b % IN_FLIGHT])
+
+    def emit(c):
         return pltpu.make_async_copy(outb.at[c], sink.at[c // n_local, c % n_local], out_sem.at[c])
 
-    for b in range(n_buf - 1):
-        fetch(x_hbm, b).start()
+    for b in range(IN_FLIGHT - 1):
+        fetch(b).start()
     table[...] = jnp.zeros_like(table)
-    for source, sink, follow, before in ((x_hbm, xs, dy_hbm, None), (dy_hbm, dys, None, xs)):
-        def scatter(b, _):
-            ahead = b + n_buf - 1
-
-            @pl.when(ahead < n_in)
-            def _():
-                fetch(source, ahead).start()
-            if follow is not None:
-                @pl.when(ahead >= n_in)
-                def _():
-                    fetch(follow, ahead - n_in).start()
-            fetch(source, b).wait()
-            for j in range(ROW_TILES):
-                part = inb[b % n_buf, :, j * LANES:(j + 1) * LANES].astype(F32)
-                stage3[:, j * 8:(j + 1) * 8, :] = part.reshape(tb // 8, 8, LANES)
-
-            def move(i, _):
-                for r in range(32):
-                    at = addr[b * tb + i * 32 + r]
-                    table[row(at, ROW_TILES), :] = stage[row(i * (4 * PITCH) + (r // 8) * PITCH + r % 8, ROW_TILES), :]
-                return 0
-
-            lax.fori_loop(0, tb // 32, move, 0)
+    meanwhile()
+
+    def scatter(b, _):
+        @pl.when(b + IN_FLIGHT - 1 < n_in)
+        def _():
+            fetch(b + IN_FLIGHT - 1).start()
+        fetch(b).wait()
+        for j in range(ROW_TILES):
+            part = inb[b % IN_FLIGHT, :, j * LANES:(j + 1) * LANES].astype(F32)
+            stage3[:, j * 8:(j + 1) * 8, :] = part.reshape(TB // 8, 8, LANES)
+
+        def move(i, _):
+            for r in range(32):
+                at = addr[b, i * 32 + r]
+                table[row(at, ROW_TILES), :] = stage[row(i * (4 * PITCH) + (r // 8) * PITCH + r % 8, ROW_TILES), :]
             return 0
 
-        lax.fori_loop(0, n_in, scatter, 0)
-
-        def drain(c, _):
-            if before is not None:
-                emit(before, c).wait()
-            for j in range(ROW_TILES):
-                part = tiled[pl.ds(c * groups, groups), j * 8:(j + 1) * 8, :].reshape(cap, LANES)
-                outb[c, :, j * LANES:(j + 1) * LANES] = part.astype(BF16)
-            emit(sink, c).start()
-            return 0
-
-        lax.fori_loop(0, n_chunk, drain, 0)
+        lax.fori_loop(0, TB // 32, move, 0)
+        return 0
+
+    lax.fori_loop(0, n_in, scatter, 0)
+
+    def drain(c, _):
+        for j in range(ROW_TILES):
+            part = tiled[pl.ds(c * groups, groups), j * 8:(j + 1) * 8, :].reshape(cap, LANES)
+            outb[c, :, j * LANES:(j + 1) * LANES] = part.astype(BF16)
+        emit(c).start()
+        return 0
 
     def finish(c, _):
-        emit(dys, c).wait()
+        emit(c).wait()
         return 0
 
+    lax.fori_loop(0, n_chunk, drain, 0)
     lax.fori_loop(0, n_chunk, finish, 0)
 
 
-def permute(n_dev, n_local, capacity, addr, x, dy):
-    tokens, d_model = x.shape
-    tb = 512
+def route_permute_kernel(idx, x, xs, slot_out, addr_out, count_out, addr, addr_sem, *scratch):
+    n_out, n_local, cap, _ = xs.shape
+    n = n_out * n_local
+
+    def route():
+        below = lax.broadcasted_iota(jnp.int32, (TB, TB), 0) <= lax.broadcasted_iota(jnp.int32, (TB, TB), 1)
+        upper = jnp.where(below, 1.0, 0.0).astype(BF16)
+        expert = lax.broadcasted_iota(jnp.int32, (n, TB), 0)
+        seen = jnp.zeros((n, 1), F32)
+        for b in range(idx.shape[0]):
+            mine = expert == idx[b:b + 1, :]
+            onehot = jnp.where(mine, 1.0, 0.0)
+            rank = nn(onehot.astype(BF16), upper)
+            pos = jnp.sum(jnp.where(mine, rank + (seen - 1.0), 0.0), axis=0, keepdims=True).astype(jnp.int32)
+            slot = jnp.where(pos < cap, idx[b:b + 1, :] * cap + pos, n * cap)
+            slot_out[b:b + 1, :] = slot
+            group = lax.shift_right_logical(slot, jnp.full_like(slot, 3))
+            addr_out[b:b + 1, :] = group * PITCH + (slot - group * 8)
+            seen = seen + rank[:, TB - 1:TB]
+        count_out[...] = jnp.broadcast_to(seen, count_out.shape)
+        copy = pltpu.make_async_copy(addr_out, addr, addr_sem)
+        copy.start()
+        copy.wait()
+
+    permute_rows(addr, x, xs, *scratch, route)
+
+
+def permute_scratch(n_slots, cap, d_model):
+    return [pltpu.VMEM((IN_FLIGHT, TB, d_model), BF16), pltpu.VMEM((TB // 8 * PITCH, LANES), F32), pltpu.VMEM(((n_slots // 8 + 1) * PITCH, LANES), F32),
+            pltpu.VMEM((n_slots // cap, cap, d_model), BF16), pltpu.SemaphoreType.DMA((IN_FLIGHT,)), pltpu.SemaphoreType.DMA((n_slots // cap,))]
+
+
+def route_permute(n_dev, n_local, cap, idx, x):
     hbm = pl.BlockSpec(memory_space=pl.ANY)
-    out = jax.ShapeDtypeStruct((n_dev, n_local, capacity, d_model), BF16)
-    n_groups = n_dev * n_local * capacity // 8 + 1
+    vmem = pl.BlockSpec(memory_space=pltpu.VMEM)
+    table = jax.ShapeDtypeStruct(idx.shape, jnp.int32)
+    n = n_dev * n_local
     return pl.pallas_call(
-        lambda *refs: permute_kernel(tb, *refs),
-        out_shape=(out, out),
+        route_permute_kernel,
+        out_shape=(jax.ShapeDtypeStruct((n_dev, n_local, cap, x.shape[1]), BF16), table, table, jax.ShapeDtypeStruct((n, LANES), F32)),
+        in_specs=[vmem, hbm], out_specs=[hbm, vmem, vmem, vmem],
+        scratch_shapes=[pltpu.SMEM(idx.shape, jnp.int32), pltpu.SemaphoreType.DMA] + permute_scratch(n * cap, cap, x.shape[1]),
+        compiler_params=pltpu.CompilerParams(vmem_limit_bytes=60 * 2 ** 20),
+        name='route_permute',
+    )(idx, x)
+
+
+def permute(n_dev, n_local, cap, addr, x):
+    hbm = pl.BlockSpec(memory_space=pl.ANY)
+    return pl.pallas_call(
+        lambda *refs: permute_rows(*refs, lambda: None),
+        out_shape=jax.ShapeDtypeStruct((n_dev, n_local, cap, x.shape[1]), BF16),
         grid_spec=pltpu.PrefetchScalarGridSpec(
-            num_scalar_prefetch=1, grid=(), in_specs=[hbm, hbm], out_specs=[hbm, hbm],
-            scratch_shapes=[
-                pltpu.VMEM((4, tb, d_model), BF16), pltpu.VMEM((tb // 8 * PITCH, LANES), F32), pltpu.VMEM((n_groups * PITCH, LANES), F32),
-                pltpu.VMEM((n_dev * n_local, capacity, d_model), BF16), pltpu.SemaphoreType.DMA((4,)), pltpu.SemaphoreType.DMA((n_dev * n_local,))]),
+            num_scalar_prefetch=1, grid=(), in_specs=[hbm], out_specs=hbm,
+            scratch_shapes=permute_scratch(n_dev * n_local * cap, cap, x.shape[1])),
+        cost_estimate=pl.CostEstimate(flops=20 * 10 ** 9, bytes_accessed=28 * 2 ** 20, transcendentals=0),
         compiler_params=pltpu.CompilerParams(vmem_limit_bytes=60 * 2 ** 20),
         name='permute_rows',
-    )(addr, x, dy)
+    )(addr, x)
 
 
 def router_kernel(z_coef, slot, x, idx, w_t, v_col, gback, pieces_out, partial, acc, gtab, g_rows, w_six, pieces_t, p_acc, z_acc):
@@ -413,7 +462,7 @@
 
     def move(i, _):
         for r in range(32):
-            g_rows[pl.ds(i * 32 + r, 1), :] = gtab[pl.ds(slot[b * tb + i * 32 + r], 1), :]
+            g_rows[pl.ds(i * 32 + r, 1), :] = gtab[pl.ds(slot[b, i * 32 + r], 1), :]
         return 0
 
     lax.fori_loop(0, tb // 32, move, 0)
@@ -426,7 +475,7 @@
     total = jnp.sum(expd, axis=0, keepdims=True)
     prob = expd / total
     z = top + jnp.log(total)
-    mine = lax.broadcasted_iota(jnp.int32, logits.shape, 0).astype(F32) == idx[pl.ds(b, 1), :]
+    mine = lax.broadcasted_iota(jnp.int32, logits.shape, 0) == idx[pl.ds(b, 1), :]
     onehot = jnp.where(mine, 1.0, 0.0)
     gate = jnp.sum(jnp.where(mine, prob, 0.0), axis=0, keepdims=True)
     g = g_rows[...].T[0:1, :]
@@ -460,9 +509,8 @@
 def router_side(z_coef, slot, x, idx, w_t, v_col, gback):
     tokens, d_model = x.shape
     n_dev, n_local, _, cap = gback.shape
-    tb = 512
+    tb = TB
     n = w_t.shape[0]
-    idx = idx.astype(F32).reshape(tokens // tb, tb)
     gback = gback.reshape(n_dev * n_local, cap)
     rows = n + 8
     return pl.pallas_call(
@@ -521,7 +569,7 @@
 
     def move(i, _):
         for r in range(32):
-            at = addr[b * tb + i * 32 + r]
+            at = addr[b, i * 32 + r]
             stage[row(i * (4 * PITCH) + (r // 8) * PITCH + r % 8, ROW_TILES), :] = table[row(at, ROW_TILES), :]
         return 0
 
@@ -535,7 +583,7 @@
     tokens = pieces.shape[0]
     n_dev, cap, d_model = dlast.shape
     n_local = dback.shape[1] + 1
-    tb = 512
+    tb = TB
     hbm = pl.BlockSpec(memory_space=pl.ANY)
     n_groups = n_dev * n_local * cap // 8 + 1
     return pl.pallas_call(
@@ -609,24 +657,26 @@
         num_experts = n_local * n_dev
         capacity = (5 * tokens + 4 * num_experts - 1) // (4 * num_experts)
         total_tok = tokens * n_dev
-        tok_slot, counts = route_slots(expert_idx, num_experts, capacity)
-        addr = row_address(tok_slot)
-        xs, dys = permute(n_dev, n_local, capacity, addr, x_tokens, grad_y)
         w_t = w_router.T
-        cnt = jnp.broadcast_to(jnp.pad(counts.astype(F32), (0, LANES - num_experts))[None], (8, LANES))
-
-        _, _, _, d_back, d_last, g_back, gwin, gwout_t, cnt_all = expert_exchange(n_dev, xs, dys, w_t, cnt, w_in, w_out)
+        idx = expert_idx.reshape(tokens // TB, TB)
+        xs, slot, addr, cnt = route_permute(n_dev, n_local, capacity, idx, x_tokens)
+        me = lax.axis_index('ep')
+        near_x, near_y = [lax.ppermute(lax.dynamic_slice(xs, (me ^ k, e, 0, 0), (1, 1, capacity, d_model)).reshape(capacity, d_model), 'ep',
+                                       [(d, d ^ k) for d in range(n_dev)]) for e, k in EARLY]
+        dys = permute(n_dev, n_local, capacity, addr, grad_y)
+
+        _, _, _, d_back, d_last, g_back, gwin, gwout_t, cnt_all = expert_exchange(n_dev, xs, dys, near_x, near_y, w_t, cnt, w_in, w_out)
         d_last = lax.all_to_all(d_last, 'ep', 0, 0, tiled=True)
-        load_row = jnp.sum(cnt_all, axis=0) / total_tok
-        v_col = jnp.broadcast_to((AUX_WEIGHT * num_experts * load_row[0, :num_experts] / total_tok)[:, None], (num_experts, LANES))
-        pieces, partial, _ = router_side(2.0 * Z_WEIGHT / total_tok, tok_slot, x_tokens, expert_idx, w_t, v_col, g_back)
+        load_frac = jnp.sum(cnt_all, axis=0) / total_tok
+        v_col = AUX_WEIGHT * num_experts * load_frac / total_tok
+        pieces, partial, _ = router_side(2.0 * Z_WEIGHT / total_tok, slot, x_tokens, idx, w_t, v_col, g_back)
         grad_w_out = jnp.swapaxes(gwout_t, 1, 2)
         grad_w_in = own_copy(gwin)
         grad_x = combine(addr, pieces, w_t, d_back, d_last)
         grad_wr_t, stats = total_over_devices(n_dev, num_experts, partial, (grad_w_in, grad_w_out))
         grad_w_router = grad_wr_t.T
         mean_prob = stats[0, :num_experts] / total_tok
-        aux_loss = AUX_WEIGHT * num_experts * jnp.sum(load_row[0, :num_experts] * mean_prob)
+        aux_loss = AUX_WEIGHT * num_experts * jnp.sum(load_frac[:, 0] * mean_prob)
         z_loss = Z_WEIGHT * stats[0, LANES] / total_tok
         return grad_x, grad_w_in, grad_w_out, grad_w_router, aux_loss, z_loss
 

time: 614 us -> 630 us (1.026)
  Pallas kernels: 570 us -> 590 us
  other arithmetic: 10.2 us -> 1.53 us
    pallas_call x1 -> x2, Pallas kernels: 37.4 us -> 66.4 us  [the longest x1 34.5 us: route_permute(): pl.pallas_call(route_permute_kernel, out_shape=(jax.ShapeDtypeStruct((n_d...]
    pallas_call x1, Pallas kernels: 430 us -> 409 us  [expert_exchange(): pl.pallas_call(lambda *refs: expert_kernel(n_dev, n_local, num_experts, b...]
    pallas_call x1, Pallas kernels: 25 us -> 38.2 us  [router_side(): pl.pallas_call(lambda *refs: router_kernel(z_coef, *refs), out_shape=(jax...]
    pallas_call x1, Pallas kernels: 31.9 us -> 18.7 us  [total_over_devices(): pl.pallas_call(lambda *refs: total_kernel(n_dev, *refs), out_shape=(jax.S...]
    pallas_call x1, Pallas kernels: 28.4 us -> 40.4 us  [combine(): pl.pallas_call(combine_kernel, out_shape=jax.ShapeDtypeStruct((tokens, d_...]
  transfers between devices with their start and end apart: 1 -> 3, of which waited for: 0 -> 0; matrix products, arithmetic and copies ran while one was open for 3% -> 3% of each run, Pallas kernels for 12% -> 17%
where the time goes in v5:
time: 630 us; the launch traced here: 629 us
  Pallas kernels  590 us (94%)
  local copies, waits for them, and re-layouts  26.5 us (4%)
  starting transfers between devices  7.1 us (1%)
    pallas_call x1, Pallas kernels, expert_exchange(): pl.pallas_call(lambda *refs: expert_kernel(n_dev, n_local, num_experts, b...  409 us
    pallas_call x1, Pallas kernels, combine(): pl.pallas_call(combine_kernel, out_shape=jax.ShapeDtypeStruct((tokens, d_...  40.4 us
    pallas_call x1, Pallas kernels, router_side(): pl.pallas_call(lambda *refs: router_kernel(z_coef, *refs), out_shape=(jax...  38.2 us
    pallas_call x1, Pallas kernels, route_permute(): pl.pallas_call(route_permute_kernel, out_shape=(jax.ShapeDtypeStruct((n_d...  34.5 us
    pallas_call x1, Pallas kernels, permute(): pl.pallas_call(lambda *refs: permute_rows(*refs, lambda: None), out_shape...  31.9 us
    pallas_call x1, local copies, waits for them, and re-layouts, expert_exchange(): pl.pallas_call(lambda *refs: expert_kernel(n_dev, n_local, num_experts, b...  18.7 us
    pallas_call x1, Pallas kernels, total_over_devices(): pl.pallas_call(lambda *refs: total_kernel(n_dev, *refs), out_shape=(jax.S...  18.7 us
    pallas_call x1, Pallas kernels, own_copy(): pl.pallas_call(copy_kernel, out_shape=jax.ShapeDtypeStruct(a.shape, a.dty...  16.9 us
  transfers between devices with their start and end apart: 3, of which 0 were waited for; matrix products, arithmetic and copies ran while one was open for 3% of the time, Pallas kernels for 17%

profile of v5, /device:TPU:1, one launch (start us, length us, event | category | flops | bytes accessed | tf_op | source)
XLA Modules:
  0.0 629.3 jit_solution(2681381642029877828)
XLA Ops:
  0.6 1.4 reshape.28.idx.refs_2_
  2.0 34.5 %route_permute.1 = (bf16[8,2,640,768]{3,2,1,0:T(8,128)(2,1)}, s32[16,512]{1,0:T(8,128)}, s32[16,512]{1,0:T(8,128)}, f32[16,128]{1,0:T(8,128)}) custom-call(s32[16,512]{1,0:T(8,128)} %reshape.28.idx.refs_2_, bf16[8192,768]{1,0:T(8,128)(2,1)} %refs_1_.3), custom_call_target="tpu_custom_call" | custom-call | tf_op jit(solution)/shard_map/route_permute/pallas_call | solution.py:419
  36.5 1.6 dynamic-slice_bitcast_fusion
  38.2 2.1 collective-permute-start.1
  40.2 1.2 collective-permute-start
  41.5 31.9 %permute_rows.1.refs_1_ = bf16[8,2,640,768]{3,2,1,0:T(8,128)(2,1)} custom-call(s32[16,512]{1,0:T(8,128)} %get-tuple-element.20.refs_0_.addr, bf16[8192,768]{1,0:T(8,128)(2,1)} %refs_1_.2), custom_call_target="tpu_custom_call" | custom-call | flops 20000000000 | bytes 29360128 | tf_op jit(solution)/shard_map/permute_rows/pallas_call | solution.py:431
  73.4 0.0 collective-permute-done.1.refs_3_
  73.4 0.0 copy-start.5
  73.4 0.0 collective-permute-done.refs_2_
  73.4 0.9 copy-done.5
  74.3 409.3 %expert_exchange.1 = (bf16[8,2,640,768]{3,2,1,0:T(8,128)(2,1)}, bf16[8,2,640,768]{3,2,1,0:T(8,128)(2,1)}, bf16[8,1,640,768]{3,2,1,0:T(8,128)(2,1)}, bf16[8,1,640...) custom-call(bf16[8,2,640,768]{3,2,1,0:T(8,128)(2,1)} %get-tuple-elem, ...), custom_call_target="tpu_custom_call" | custom-call | tf_op jit(solution)/shard_map/expert_exchange/pallas_call | solution.py:296
  483.6 0.0 copy-start.8
  483.6 3.8 all-to-all-start
  487.4 0.0 copy-done.8
  487.4 0.1 reduce
  487.6 0.0 copy-start.6
  487.6 18.7 %copy.13 = f32[2,768,3072]{1,2,0:T(8,128)} copy(f32[2,768,3072]{2,1,0:T(8,128)} %get-tuple-element.30) | data formatting | bytes 37748736 | tf_op jit(solution)/shard_map/expert_exchange/pallas_call | solution.py:296
  506.3 0.0 copy-done.6
  506.3 0.0 copy-start.1
  506.3 0.0 copy-start.2
  506.4 16.9 %own_copy.1.refs_1_ = f32[2,768,3072]{2,1,0:T(8,128)} custom-call(f32[2,768,3072]{2,1,0:T(8,128)} %get-tuple-element.29.source), custom_call_target="tpu_custom_call" | custom-call | flops 15000000512 | bytes 37748736 | tf_op jit(solution)/shard_map/own_copy/pallas_call | solution.py:645
  523.2 0.0 copy-done.1
  523.2 38.2 %router_side.1 = (bf16[8192,128]{1,0:T(8,128)(2,1)S(1)}, f32[24,768]{1,0:T(8,128)S(1)}, f32[128,768]{1,0:T(8,128)}) custom-call(s32[16,512]{1,0:T(8,128)S(1)} %copy-done.4, bf16[8192,768]{1,0:T(8,128)(2,1)} %refs_1_.3, s32[16,512]{1,0:T(8,128)S(1)} %copy-done.2, f32[16,768]{1,0:T(8,128)S(1)} %bitcast.14, f32[16,128]{1,0:T(8,128)S(1)} %broadcast_multiply_fusion.refs_4_, ...), custom_call_target="tpu_custom_call" | custom-call | flops 30000001024 | bytes 16777216 | tf_op jit(solution)/shard_map/router_side/pallas_call | solution.py:516
  561.5 1.4 copy-done
  562.8 0.6 copy-done.3
  563.5 18.7 %device_total.1 = (f32[16,768]{1,0:T(8,128)}, f32[8,768]{1,0:T(8,128)}) custom-call(f32[24,768]{1,0:T(8,128)} %copy-done.3, f32[2,768,3072]{2,1,0:T(8,128)} %own_copy.1.refs_1_, f32[2,3072,768]{2,1,0:T(8,128)} %bitcast.15), custom_call_target="tpu_custom_call" | custom-call | tf_op jit(solution)/shard_map/device_total/pallas_call | solution.py:628
  582.1 1.2 slice.11
  584.0 0.1 fusion
  584.1 1.3 fusion.1
  586.0 0.0 all-to-all-done.dlast
  586.0 40.4 %combine_rows.1 = bf16[8192,768]{1,0:T(8,128)(2,1)} custom-call(s32[16,512]{1,0:T(8,128)} %get-tuple-element.20.refs_0_.addr, bf16[8192,128]{1,0:T(8,128)(2,1)} %copy-done, f32[16,768]{1,0:T(8,128)} %bitcast.13, bf16[8,1,640,768]{3,2,1,0:T(8,128)(2,1)} %get-tuple-element.27.dback, bf16[8,640,768]{2,1,0:T(8,128)(2,1)} %all-to-all-done.dlast), custom_call_target="tpu_custom_call" | custom-call | tf_op jit(solution)/shard_map/combine_rows/pallas_call | solution.py:589
  626.5 0.6 copy.16
  (10 shorter events, 0.1 us)
Async XLA Ops:
  38.2 35.2 %collective-permute-start.1 = (bf16[640,768]{1,0:T(8,128)(2,1)S(1)}, bf16[640,768]{1,0:T(8,128)(2,1)S(1)}, u32[]{:S(2)}, u32[]{:S(2)}) collective-permute-start(bf16[640,768]{1,0:T(8,128)(2,1)S(1)} %get-tuple-element.34), channel_id=1, source_target_pairs={{0,4},{1,5},{2,6},{3,7},{4,0},{5,1},{6,2},{7,3}} | collective-permute-start | bytes 2949128 | tf_op jit(solution)/shard_map/ppermute | solution.py:664
  40.2 33.2 %collective-permute-start = (bf16[640,768]{1,0:T(8,128)(2,1)S(1)}, bf16[640,768]{1,0:T(8,128)(2,1)}, u32[]{:S(2)}, u32[]{:S(2)}) collective-permute-start(bf16[640,768]{1,0:T(8,128)(2,1)S(1)} %get-tuple-element.35), channel_id=1, source_target_pairs={{0,2},{1,3},{2,0},{3,1},{4,6},{5,7},{6,4},{7,5}} | collective-permute-start | bytes 2949128 | tf_op jit(solution)/shard_map/ppermute | solution.py:664
  73.4 0.9 copy-start.5
  483.6 3.8 copy-start.8
  483.6 102.4 %all-to-all-start = ((bf16[8,640,768]{2,1,0:T(8,128)(2,1)}), bf16[8,640,768]{2,1,0:T(8,128)(2,1)}, u32[]{:S(2)}, u32[]{:S(2)}) async-start(bf16[8,640,768]{2,1,0:T(8,128)(2,1)} %get-tuple-element.28), calls=%async_computation | async-start | bytes 15728640 | tf_op jit(solution)/shard_map/all_to_all | solution.py:669
  487.6 18.7 %copy-start.6 = (f32[8,16,128]{2,1,0:T(8,128)S(1)}, f32[8,16,128]{2,1,0:T(8,128)}, u32[]{:S(2)}) copy-start(f32[8,16,128]{2,1,0:T(8,128)} %get-tuple-element.24) | copy-start | bytes 196612
  506.3 16.9 %copy-start.1 = (f32[768,16]{0,1:T(8,128)S(1)}, f32[768,16]{0,1:T(8,128)}, u32[]{:S(2)}) copy-start(f32[768,16]{0,1:T(8,128)} %param.7) | copy-start | bytes 147460
  506.3 16.9 %copy-start.2 = (s32[16,512]{1,0:T(8,128)S(1)}, s32[16,512]{1,0:T(8,128)}, u32[]{:S(2)}) copy-start(s32[16,512]{1,0:T(8,128)} %reshape.28.idx.refs_2_) | copy-start | bytes 98308
  506.3 16.9 %copy-start.4 = (s32[16,512]{1,0:T(8,128)S(1)}, s32[16,512]{1,0:T(8,128)}, u32[]{:S(2)}) copy-start(s32[16,512]{1,0:T(8,128)} %get-tuple-element.21.refs_0_) | copy-start | bytes 98308
  561.5 1.4 copy-start
  562.8 0.6 copy-start.3
  586.0 40.4 %copy-start.7 = (f32[16,768]{1,0:T(8,128)S(1)}, f32[16,768]{1,0:T(8,128)}, u32[]{:S(2)}) copy-start(f32[16,768]{1,0:T(8,128)} %get-tuple-element.32) | copy-start | bytes 147460

commit v6 on v5

--- a/solution.py
+++ b/solution.py
@@ -355,7 +355,7 @@
 
         def move(i, _):
             for r in range(32):
-                at = addr[b, i * 32 + r]
+                at = addr[b * TB + i * 32 + r]
                 table[row(at, ROW_TILES), :] = stage[row(i * (4 * PITCH) + (r // 8) * PITCH + r % 8, ROW_TILES), :]
             return 0
 
@@ -399,9 +399,11 @@
             addr_out[b:b + 1, :] = group * PITCH + (slot - group * 8)
             seen = seen + rank[:, TB - 1:TB]
         count_out[...] = jnp.broadcast_to(seen, count_out.shape)
-        copy = pltpu.make_async_copy(addr_out, addr, addr_sem)
-        copy.start()
-        copy.wait()
+        copies = [pltpu.make_async_copy(addr_out.at[b], addr.at[pl.ds(b * TB, TB)], addr_sem.at[b]) for b in range(idx.shape[0])]
+        for copy in copies:
+            copy.start()
+        for copy in copies:
+            copy.wait()
 
     permute_rows(addr, x, xs, *scratch, route)
 
@@ -420,7 +422,7 @@
         route_permute_kernel,
         out_shape=(jax.ShapeDtypeStruct((n_dev, n_local, cap, x.shape[1]), BF16), table, table, jax.ShapeDtypeStruct((n, LANES), F32)),
         in_specs=[vmem, hbm], out_specs=[hbm, vmem, vmem, vmem],
-        scratch_shapes=[pltpu.SMEM(idx.shape, jnp.int32), pltpu.SemaphoreType.DMA] + permute_scratch(n * cap, cap, x.shape[1]),
+        scratch_shapes=[pltpu.SMEM((idx.size,), jnp.int32), pltpu.SemaphoreType.DMA((idx.shape[0],))] + permute_scratch(n * cap, cap, x.shape[1]),
         compiler_params=pltpu.CompilerParams(vmem_limit_bytes=60 * 2 ** 20),
         name='route_permute',
     )(idx, x)
@@ -462,7 +464,7 @@
 
     def move(i, _):
         for r in range(32):
-            g_rows[pl.ds(i * 32 + r, 1), :] = gtab[pl.ds(slot[b, i * 32 + r], 1), :]
+            g_rows[pl.ds(i * 32 + r, 1), :] = gtab[pl.ds(slot[b * tb + i * 32 + r], 1), :]
         return 0
 
     lax.fori_loop(0, tb // 32, move, 0)
@@ -569,7 +571,7 @@
 
     def move(i, _):
         for r in range(32):
-            at = addr[b, i * 32 + r]
+            at = addr[b * tb + i * 32 + r]
             stage[row(i * (4 * PITCH) + (r // 8) * PITCH + r % 8, ROW_TILES), :] = table[row(at, ROW_TILES), :]
         return 0
 
@@ -660,6 +662,7 @@
         w_t = w_router.T
         idx = expert_idx.reshape(tokens // TB, TB)
         xs, slot, addr, cnt = route_permute(n_dev, n_local, capacity, idx, x_tokens)
+        slot, addr = slot.reshape(tokens), addr.reshape(tokens)
         me = lax.axis_index('ep')
         near_x, near_y = [lax.ppermute(lax.dynamic_slice(xs, (me ^ k, e, 0, 0), (1, 1, capacity, d_model)).reshape(capacity, d_model), 'ep',
                                        [(d, d ^ k) for d in range(n_dev)]) for e, k in EARLY]

time: 630 us -> 601 us (0.954)
  Pallas kernels: 590 us -> 558 us
    pallas_call x1, Pallas kernels: 38.2 us -> 25 us  [router_side(): pl.pallas_call(lambda *refs: router_kernel(z_coef, *refs), out_shape=(jax...]
    pallas_call x1, Pallas kernels: 18.7 us -> 31.8 us  [total_over_devices(): pl.pallas_call(lambda *refs: total_kernel(n_dev, *refs), out_shape=(jax.S...]
    pallas_call x1, Pallas kernels: 40.4 us -> 28.4 us  [combine(): pl.pallas_call(combine_kernel, out_shape=jax.ShapeDtypeStruct((tokens, d_...]
    pallas_call x1, Pallas kernels: 31.9 us -> 22.1 us  [permute(): pl.pallas_call(lambda *refs: permute_rows(*refs, lambda: None), out_shape...]
    pallas_call x1, Pallas kernels: 34.5 us -> 24.8 us  [route_permute(): pl.pallas_call(route_permute_kernel, out_shape=(jax.ShapeDtypeStruct((n_d...]
  transfers between devices with their start and end apart: 3 -> 3, of which waited for: 0 -> 0; matrix products, arithmetic and copies ran while one was open for 3% -> 4% of each run, Pallas kernels for 17% -> 16%
where the time goes in v6:
time: 601 us; the launch traced here: 599 us
  Pallas kernels  558 us (93%)
  local copies, waits for them, and re-layouts  27.9 us (5%)
  starting transfers between devices  7.22 us (1%)
    pallas_call x1, Pallas kernels, expert_exchange(): pl.pallas_call(lambda *refs: expert_kernel(n_dev, n_local, num_experts, b...  409 us
    pallas_call x1, Pallas kernels, total_over_devices(): pl.pallas_call(lambda *refs: total_kernel(n_dev, *refs), out_shape=(jax.S...  31.8 us
    pallas_call x1, Pallas kernels, combine(): pl.pallas_call(combine_kernel, out_shape=jax.ShapeDtypeStruct((tokens, d_...  28.4 us
    pallas_call x1, Pallas kernels, router_side(): pl.pallas_call(lambda *refs: router_kernel(z_coef, *refs), out_shape=(jax...  25 us
    pallas_call x1, Pallas kernels, route_permute(): pl.pallas_call(route_permute_kernel, out_shape=(jax.ShapeDtypeStruct((n_d...  24.8 us
    pallas_call x1, Pallas kernels, permute(): pl.pallas_call(lambda *refs: permute_rows(*refs, lambda: None), out_shape...  22.1 us
    pallas_call x1, local copies, waits for them, and re-layouts, expert_exchange(): pl.pallas_call(lambda *refs: expert_kernel(n_dev, n_local, num_experts, b...  18.7 us
    pallas_call x1, Pallas kernels, own_copy(): pl.pallas_call(copy_kernel, out_shape=jax.ShapeDtypeStruct(a.shape, a.dty...  16.8 us
  transfers between devices with their start and end apart: 3, of which 0 were waited for; matrix products, arithmetic and copies ran while one was open for 4% of the time, Pallas kernels for 16%

profile of v6, /device:TPU:1, one launch (start us, length us, event | category | flops | bytes accessed | tf_op | source)
XLA Modules:
  0.0 599.1 jit_solution(11839542473639258752)
XLA Ops:
  0.6 1.4 reshape.34.idx.refs_2_
  2.0 24.8 %route_permute.1 = (bf16[8,2,640,768]{3,2,1,0:T(8,128)(2,1)}, s32[16,512]{1,0:T(8,128)}, s32[16,512]{1,0:T(8,128)}, f32[16,128]{1,0:T(8,128)}) custom-call(s32[16,512]{1,0:T(8,128)} %reshape.34.idx.refs_2_, bf16[8192,768]{1,0:T(8,128)(2,1)} %refs_1_.3), custom_call_target="tpu_custom_call" | custom-call | tf_op jit(solution)/shard_map/route_permute/pallas_call | solution.py:421
  26.8 1.6 dynamic-slice_bitcast_fusion
  28.4 2.1 collective-permute-start.1
  30.5 1.2 collective-permute-start
  31.7 1.4 copy.15
  33.1 22.1 %permute_rows.1.refs_1_ = bf16[8,2,640,768]{3,2,1,0:T(8,128)(2,1)} custom-call(s32[8192]{0:T(1024)} %bitcast.22, bf16[8192,768]{1,0:T(8,128)(2,1)} %refs_1_.2), custom_call_target="tpu_custom_call" | custom-call | flops 20000000000 | bytes 29360128 | tf_op jit(solution)/shard_map/permute_rows/pallas_call | solution.py:433
  55.2 0.0 collective-permute-done.1.refs_3_
  55.2 0.0 copy-start.4
  55.2 0.0 collective-permute-done.refs_2_
  55.2 0.9 copy-done.4
  56.1 409.3 %expert_exchange.1 = (bf16[8,2,640,768]{3,2,1,0:T(8,128)(2,1)}, bf16[8,2,640,768]{3,2,1,0:T(8,128)(2,1)}, bf16[8,1,640,768]{3,2,1,0:T(8,128)(2,1)}, bf16[8,1,640...) custom-call(bf16[8,2,640,768]{3,2,1,0:T(8,128)(2,1)} %get-tuple-elem, ...), custom_call_target="tpu_custom_call" | custom-call | tf_op jit(solution)/shard_map/expert_exchange/pallas_call | solution.py:296
  465.4 0.0 copy-start.8
  465.4 0.0 copy-start.7
  465.4 3.9 all-to-all-start
  469.4 0.1 reduce
  469.5 0.0 copy-start.5
  469.5 18.7 %copy.13 = f32[2,768,3072]{1,2,0:T(8,128)} copy(f32[2,768,3072]{2,1,0:T(8,128)} %get-tuple-element.30) | data formatting | bytes 37748736 | tf_op jit(solution)/shard_map/expert_exchange/pallas_call | solution.py:296
  488.2 0.0 copy-done.5
  488.3 0.0 copy-start.1
  488.3 0.0 copy-start.2
  488.3 16.8 %own_copy.1.refs_1_ = f32[2,768,3072]{2,1,0:T(8,128)} custom-call(f32[2,768,3072]{2,1,0:T(8,128)} %get-tuple-element.29.source), custom_call_target="tpu_custom_call" | custom-call | flops 15000000512 | bytes 37748736 | tf_op jit(solution)/shard_map/own_copy/pallas_call | solution.py:647
  505.1 25.0 %router_side.1 = (bf16[8192,128]{1,0:T(8,128)(2,1)S(1)}, f32[24,768]{1,0:T(8,128)S(1)}, f32[128,768]{1,0:T(8,128)}) custom-call(s32[8192]{0:T(1024)S(1)} %bitcast.19, bf16[8192,768]{1,0:T(8,128)(2,1)} %refs_1_.3, s32[16,512]{1,0:T(8,128)S(1)} %copy-done.2, f32[16,768]{1,0:T(8,128)S(1)} %bitcast.18, f32[16,128]{1,0:T(8,128)S(1)} %broadcast_multiply_fusion.refs_4_, ...), custom_call_target="tpu_custom_call" | custom-call | flops 30000001024 | bytes 16777216 | tf_op jit(solution)/shard_map/router_side/pallas_call | solution.py:518
  530.1 1.4 copy-done
  531.5 0.6 copy-done.3
  532.1 31.8 %device_total.1 = (f32[16,768]{1,0:T(8,128)}, f32[8,768]{1,0:T(8,128)}) custom-call(f32[24,768]{1,0:T(8,128)} %copy-done.3, f32[2,768,3072]{2,1,0:T(8,128)} %own_copy.1.refs_1_, f32[2,3072,768]{2,1,0:T(8,128)} %bitcast.20), custom_call_target="tpu_custom_call" | custom-call | tf_op jit(solution)/shard_map/device_total/pallas_call | solution.py:630
  563.9 1.2 slice.11
  565.8 0.1 fusion
  565.9 1.3 fusion.1
  567.8 0.0 all-to-all-done.dlast
  567.8 28.4 %combine_rows.1 = bf16[8192,768]{1,0:T(8,128)(2,1)} custom-call(s32[8192]{0:T(1024)} %bitcast.23, bf16[8192,128]{1,0:T(8,128)(2,1)} %copy-done, f32[16,768]{1,0:T(8,128)} %bitcast.17, bf16[8,1,640,768]{3,2,1,0:T(8,128)(2,1)} %get-tuple-element.27.dback, bf16[8,640,768]{2,1,0:T(8,128)(2,1)} %all-to-all-done.dlast), custom_call_target="tpu_custom_call" | custom-call | tf_op jit(solution)/shard_map/combine_rows/pallas_call | solution.py:591
  596.2 0.6 copy.18
  (12 shorter events, 0.1 us)
Async XLA Ops:
  28.4 26.7 %collective-permute-start.1 = (bf16[640,768]{1,0:T(8,128)(2,1)S(1)}, bf16[640,768]{1,0:T(8,128)(2,1)S(1)}, u32[]{:S(2)}, u32[]{:S(2)}) collective-permute-start(bf16[640,768]{1,0:T(8,128)(2,1)S(1)} %get-tuple-element.34), channel_id=1, source_target_pairs={{0,4},{1,5},{2,6},{3,7},{4,0},{5,1},{6,2},{7,3}} | collective-permute-start | bytes 2949128 | tf_op jit(solution)/shard_map/ppermute | solution.py:667
  30.5 24.7 %collective-permute-start = (bf16[640,768]{1,0:T(8,128)(2,1)S(1)}, bf16[640,768]{1,0:T(8,128)(2,1)}, u32[]{:S(2)}, u32[]{:S(2)}) collective-permute-start(bf16[640,768]{1,0:T(8,128)(2,1)S(1)} %get-tuple-element.35), channel_id=1, source_target_pairs={{0,2},{1,3},{2,0},{3,1},{4,6},{5,7},{6,4},{7,5}} | collective-permute-start | bytes 2949128 | tf_op jit(solution)/shard_map/ppermute | solution.py:667
  55.2 0.9 copy-start.4
  465.4 4.0 copy-start.8
  465.4 4.0 copy-start.7
  465.4 102.4 %all-to-all-start = ((bf16[8,640,768]{2,1,0:T(8,128)(2,1)}), bf16[8,640,768]{2,1,0:T(8,128)(2,1)}, u32[]{:S(2)}, u32[]{:S(2)}) async-start(bf16[8,640,768]{2,1,0:T(8,128)(2,1)} %get-tuple-element.28), calls=%async_computation | async-start | bytes 15728640 | tf_op jit(solution)/shard_map/all_to_all | solution.py:672
  469.5 18.7 %copy-start.5 = (f32[8,16,128]{2,1,0:T(8,128)S(1)}, f32[8,16,128]{2,1,0:T(8,128)}, u32[]{:S(2)}) copy-start(f32[8,16,128]{2,1,0:T(8,128)} %get-tuple-element.24) | copy-start | bytes 196612
  488.3 16.9 %copy-start.1 = (f32[768,16]{0,1:T(8,128)S(1)}, f32[768,16]{0,1:T(8,128)}, u32[]{:S(2)}) copy-start(f32[768,16]{0,1:T(8,128)} %param.7) | copy-start | bytes 147460
  488.3 16.9 %copy-start.2 = (s32[16,512]{1,0:T(8,128)S(1)}, s32[16,512]{1,0:T(8,128)}, u32[]{:S(2)}) copy-start(s32[16,512]{1,0:T(8,128)} %reshape.34.idx.refs_2_) | copy-start | bytes 98308
  530.1 1.4 copy-start
  531.5 0.6 copy-start.3
  567.8 28.4 %copy-start.6 = (f32[16,768]{1,0:T(8,128)S(1)}, f32[16,768]{1,0:T(8,128)}, u32[]{:S(2)}) copy-start(f32[16,768]{1,0:T(8,128)} %get-tuple-element.32) | copy-start | bytes 147460

commit v7 on v6

--- a/solution.py
+++ b/solution.py
@@ -325,7 +325,7 @@
 IN_FLIGHT = 4
 
 
-def permute_rows(addr, source, sink, inb, stage, table, outb, in_sem, out_sem, meanwhile):
+def permute_rows(addr, source, sink, inb, stage, table, outb, in_sem, out_sem, meanwhile, extra):
     n_out, n_local, cap, d_model = sink.shape
     groups = cap // 8
     tiled = table.reshape(table.shape[0] // PITCH, PITCH, LANES)
@@ -376,10 +376,11 @@
         return 0
 
     lax.fori_loop(0, n_chunk, drain, 0)
+    extra(outb)
     lax.fori_loop(0, n_chunk, finish, 0)
 
 
-def route_permute_kernel(idx, x, xs, slot_out, addr_out, count_out, addr, addr_sem, *scratch):
+def route_permute_kernel(idx, x, xs, near_x, near_y, slot_out, addr_out, count_out, addr, addr_sem, near_sem, *scratch):
     n_out, n_local, cap, _ = xs.shape
     n = n_out * n_local
 
@@ -399,13 +400,20 @@
             addr_out[b:b + 1, :] = group * PITCH + (slot - group * 8)
             seen = seen + rank[:, TB - 1:TB]
         count_out[...] = jnp.broadcast_to(seen, count_out.shape)
-        copies = [pltpu.make_async_copy(addr_out.at[b], addr.at[pl.ds(b * TB, TB)], addr_sem.at[b]) for b in range(idx.shape[0])]
+        load_table(addr_out, addr, addr_sem)
+
+    def near(outb):
+        me = lax.axis_index('ep')
+        copies = []
+        for at, ((e, k), sink) in enumerate(zip(EARLY, (near_x, near_y))):
+            p = me + k - 2 * k * ((me // k) % 2)
+            copies.append(pltpu.make_async_copy(outb.at[p * n_local + e], sink, near_sem.at[at]))
         for copy in copies:
             copy.start()
         for copy in copies:
             copy.wait()
 
-    permute_rows(addr, x, xs, *scratch, route)
+    permute_rows(addr, x, xs, *scratch, route, near)
 
 
 def permute_scratch(n_slots, cap, d_model):
@@ -418,24 +426,37 @@
     vmem = pl.BlockSpec(memory_space=pltpu.VMEM)
     table = jax.ShapeDtypeStruct(idx.shape, jnp.int32)
     n = n_dev * n_local
+    block = jax.ShapeDtypeStruct((cap, x.shape[1]), BF16)
     return pl.pallas_call(
         route_permute_kernel,
-        out_shape=(jax.ShapeDtypeStruct((n_dev, n_local, cap, x.shape[1]), BF16), table, table, jax.ShapeDtypeStruct((n, LANES), F32)),
-        in_specs=[vmem, hbm], out_specs=[hbm, vmem, vmem, vmem],
-        scratch_shapes=[pltpu.SMEM((idx.size,), jnp.int32), pltpu.SemaphoreType.DMA((idx.shape[0],))] + permute_scratch(n * cap, cap, x.shape[1]),
+        out_shape=(jax.ShapeDtypeStruct((n_dev, n_local, cap, x.shape[1]), BF16), block, block, table, table, jax.ShapeDtypeStruct((n, LANES), F32)),
+        in_specs=[vmem, hbm], out_specs=[hbm, hbm, hbm, vmem, vmem, vmem],
+        scratch_shapes=[pltpu.SMEM((idx.size,), jnp.int32), pltpu.SemaphoreType.DMA((idx.shape[0],)), pltpu.SemaphoreType.DMA((2,))] + permute_scratch(n * cap, cap, x.shape[1]),
         compiler_params=pltpu.CompilerParams(vmem_limit_bytes=60 * 2 ** 20),
         name='route_permute',
     )(idx, x)
 
 
+def load_table(table, addr, sem):
+    copies = [pltpu.make_async_copy(table.at[b], addr.at[pl.ds(b * TB, TB)], sem.at[b]) for b in range(table.shape[0])]
+    for copy in copies:
+        copy.start()
+    for copy in copies:
+        copy.wait()
+
+
+def permute_kernel(table, x, xs, addr, addr_sem, *scratch):
+    permute_rows(addr, x, xs, *scratch, lambda: load_table(table, addr, addr_sem), lambda outb: None)
+
+
 def permute(n_dev, n_local, cap, addr, x):
     hbm = pl.BlockSpec(memory_space=pl.ANY)
     return pl.pallas_call(
-        lambda *refs: permute_rows(*refs, lambda: None),
+        permute_kernel,
         out_shape=jax.ShapeDtypeStruct((n_dev, n_local, cap, x.shape[1]), BF16),
-        grid_spec=pltpu.PrefetchScalarGridSpec(
-            num_scalar_prefetch=1, grid=(), in_specs=[hbm], out_specs=hbm,
-            scratch_shapes=permute_scratch(n_dev * n_local * cap, cap, x.shape[1])),
+        in_specs=[pl.BlockSpec(memory_space=pltpu.VMEM), hbm], out_specs=hbm,
+        scratch_shapes=[pltpu.SMEM((addr.size,), jnp.int32), pltpu.SemaphoreType.DMA((addr.shape[0],))]
+        + permute_scratch(n_dev * n_local * cap, cap, x.shape[1]),
         cost_estimate=pl.CostEstimate(flops=20 * 10 ** 9, bytes_accessed=28 * 2 ** 20, transcendentals=0),
         compiler_params=pltpu.CompilerParams(vmem_limit_bytes=60 * 2 ** 20),
         name='permute_rows',
@@ -585,7 +606,7 @@
     tokens = pieces.shape[0]
     n_dev, cap, d_model = dlast.shape
     n_local = dback.shape[1] + 1
-    tb = TB
+    tb = 2 * TB
     hbm = pl.BlockSpec(memory_space=pl.ANY)
     n_groups = n_dev * n_local * cap // 8 + 1
     return pl.pallas_call(
@@ -603,7 +624,7 @@
     )(addr, pieces, w_t, dback, dlast)
 
 
-def total_kernel(n_dev, part, _before_a, _before_b, out, stats, parts, send_sem, recv_sem):
+def total_kernel(n_dev, total_tok, part, load, _before_a, _before_b, out, aux, zl, parts, send_sem, recv_sem):
     me = lax.axis_index('ep')
     barrier = pltpu.get_barrier_semaphore()
     peers = [(me + k) % n_dev for k in range(1, n_dev)]
@@ -622,19 +643,23 @@
         total = total + parts[d]
     n = out.shape[0]
     out[...] = total[0:n]
-    stats[...] = total[n:]
-
-
-def total_over_devices(n_dev, n_grad, part, before):
+    load_row = jnp.concatenate([load[...], jnp.zeros((LANES - n, LANES), F32)], axis=0).T[0:1, :]
+    aux[0, 0] = AUX_WEIGHT * n * jnp.sum(load_row * (total[n:n + 1, 0:LANES] / total_tok))
+    zl[0, 0] = Z_WEIGHT * jnp.max(total[n:n + 1, LANES:2 * LANES]) / total_tok
+
+
+def total_over_devices(n_dev, total_tok, part, load, before):
     vmem = pl.BlockSpec(memory_space=pltpu.VMEM)
+    smem = pl.BlockSpec(memory_space=pltpu.SMEM)
+    one = jax.ShapeDtypeStruct((1, 1), F32)
     return pl.pallas_call(
-        lambda *refs: total_kernel(n_dev, *refs),
-        out_shape=(jax.ShapeDtypeStruct((n_grad, part.shape[1]), F32), jax.ShapeDtypeStruct((part.shape[0] - n_grad, part.shape[1]), F32)),
-        in_specs=[vmem] + [pl.BlockSpec(memory_space=pl.ANY)] * 2, out_specs=[vmem, vmem],
+        lambda *refs: total_kernel(n_dev, total_tok, *refs),
+        out_shape=(jax.ShapeDtypeStruct((load.shape[0], part.shape[1]), F32), one, one),
+        in_specs=[vmem, vmem] + [pl.BlockSpec(memory_space=pl.ANY)] * 2, out_specs=[vmem, smem, smem],
         scratch_shapes=[pltpu.VMEM((n_dev,) + part.shape, F32), pltpu.SemaphoreType.DMA((n_dev - 1,)), pltpu.SemaphoreType.DMA((n_dev - 1,))],
         compiler_params=pltpu.CompilerParams(collective_id=1, has_side_effects=True),
         name='device_total',
-    )(part, *before)
+    )(part, load, *before)
 
 
 def copy_kernel(source, sink):
@@ -661,12 +686,10 @@
         total_tok = tokens * n_dev
         w_t = w_router.T
         idx = expert_idx.reshape(tokens // TB, TB)
-        xs, slot, addr, cnt = route_permute(n_dev, n_local, capacity, idx, x_tokens)
+        xs, near_x, near_y, slot, addr, cnt = route_permute(n_dev, n_local, capacity, idx, x_tokens)
+        near_x, near_y = [lax.ppermute(block, 'ep', [(d, d ^ k) for d in range(n_dev)]) for block, (_, k) in zip((near_x, near_y), EARLY)]
+        dys = permute(n_dev, n_local, capacity, addr, grad_y)
         slot, addr = slot.reshape(tokens), addr.reshape(tokens)
-        me = lax.axis_index('ep')
-        near_x, near_y = [lax.ppermute(lax.dynamic_slice(xs, (me ^ k, e, 0, 0), (1, 1, capacity, d_model)).reshape(capacity, d_model), 'ep',
-                                       [(d, d ^ k) for d in range(n_dev)]) for e, k in EARLY]
-        dys = permute(n_dev, n_local, capacity, addr, grad_y)
 
         _, _, _, d_back, d_last, g_back, gwin, gwout_t, cnt_all = expert_exchange(n_dev, xs, dys, near_x, near_y, w_t, cnt, w_in, w_out)
         d_last = lax.all_to_all(d_last, 'ep', 0, 0, tiled=True)
@@ -676,11 +699,8 @@
         grad_w_out = jnp.swapaxes(gwout_t, 1, 2)
         grad_w_in = own_copy(gwin)
         grad_x = combine(addr, pieces, w_t, d_back, d_last)
-        grad_wr_t, stats = total_over_devices(n_dev, num_experts, partial, (grad_w_in, grad_w_out))
-        grad_w_router = grad_wr_t.T
-        mean_prob = stats[0, :num_experts] / total_tok
-        aux_loss = AUX_WEIGHT * num_experts * jnp.sum(load_frac[:, 0] * mean_prob)
-        z_loss = Z_WEIGHT * stats[0, LANES] / total_tok
+        grad_wr_t, aux_loss, z_loss = total_over_devices(n_dev, total_tok, partial, load_frac, (grad_w_in, grad_w_out))
+        grad_w_router, aux_loss, z_loss = grad_wr_t.T, aux_loss.reshape(()), z_loss.reshape(())
         return grad_x, grad_w_in, grad_w_out, grad_w_router, aux_loss, z_loss
 
     return jax.shard_map(expert_layer, mesh=mesh,

time: 601 us -> 594 us (0.988)
  transfers between devices with their start and end apart: 3 -> 3, of which waited for: 0 -> 0; matrix products, arithmetic and copies ran while one was open for 4% -> 3% of each run, Pallas kernels for 16% -> 16%
where the time goes in v7:
time: 594 us; the launch traced here: 593 us
  Pallas kernels  557 us (94%)
  local copies, waits for them, and re-layouts  24.3 us (4%)
  starting transfers between devices  7.25 us (1%)
    pallas_call x1, Pallas kernels, expert_exchange(): pl.pallas_call(lambda *refs: expert_kernel(n_dev, n_local, num_experts, b...  409 us
    pallas_call x1, Pallas kernels, total_over_devices(): pl.pallas_call(lambda *refs: total_kernel(n_dev, total_tok, *refs), out_s...  30.9 us
    pallas_call x1, Pallas kernels, combine(): pl.pallas_call(combine_kernel, out_shape=jax.ShapeDtypeStruct((tokens, d_...  27.3 us
    pallas_call x1, Pallas kernels, route_permute(): pl.pallas_call(route_permute_kernel, out_shape=(jax.ShapeDtypeStruct((n_d...  25.4 us
    pallas_call x1, Pallas kernels, router_side(): pl.pallas_call(lambda *refs: router_kernel(z_coef, *refs), out_shape=(jax...  25 us
    pallas_call x1, Pallas kernels, permute(): pl.pallas_call(permute_kernel, out_shape=jax.ShapeDtypeStruct((n_dev, n_l...  21.9 us
    pallas_call x1, local copies, waits for them, and re-layouts, expert_exchange(): pl.pallas_call(lambda *refs: expert_kernel(n_dev, n_local, num_experts, b...  18.7 us
    pallas_call x1, Pallas kernels, own_copy(): pl.pallas_call(copy_kernel, out_shape=jax.ShapeDtypeStruct(a.shape, a.dty...  16.8 us
  transfers between devices with their start and end apart: 3, of which 0 were waited for; matrix products, arithmetic and copies ran while one was open for 3% of the time, Pallas kernels for 16%

profile of v7, /device:TPU:1, one launch (start us, length us, event | category | flops | bytes accessed | tf_op | source)
XLA Modules:
  0.0 593.1 jit_solution(15556863609110972168)
XLA Ops:
  0.6 1.4 reshape.30.idx.refs_2_
  2.0 25.4 %route_permute.1 = (bf16[8,2,640,768]{3,2,1,0:T(8,128)(2,1)}, bf16[640,768]{1,0:T(8,128)(2,1)}, bf16[640,768]{1,0:T(8,128)(2,1)}, s32[16,512]{1,0:T(8,128)}, s32[16,512]{1,0:T(8,128)}, /*index=5*/f32[16,128]{1,0:T(8,128)}) custom-call(s32[16,512]{1,0:T(8,128)} %reshape.30.idx.refs_2_, bf16[8192,768]{1,0:T(8,128)(2,1)} %refs_1_.1), custom_call_target="tpu_custom_call" | custom-call | tf_op jit(solution)/shard_map/route_permute/pallas_call | solution.py:430
  27.4 2.1 collective-permute-start
  29.5 1.2 collective-permute-start.1
  30.7 21.9 %permute_rows.1.refs_1_ = bf16[8,2,640,768]{3,2,1,0:T(8,128)(2,1)} custom-call(s32[16,512]{1,0:T(8,128)} %get-tuple-element.23.table, bf16[8192,768]{1,0:T(8,128)(2,1)} %x.3), custom_call_target="tpu_custom_call" | custom-call | flops 20000000000 | bytes 29360128 | tf_op jit(solution)/shard_map/permute_rows/pallas_call | solution.py:454
  52.7 0.0 collective-permute-done.refs_2_
  52.7 0.0 copy-start.4
  52.7 0.0 collective-permute-done.1.refs_3_
  52.7 0.9 copy-done.4
  53.6 409.3 %expert_exchange.1 = (bf16[8,2,640,768]{3,2,1,0:T(8,128)(2,1)}, bf16[8,2,640,768]{3,2,1,0:T(8,128)(2,1)}, bf16[8,1,640,768]{3,2,1,0:T(8,128)(2,1)}, bf16[8,1,640...) custom-call(bf16[8,2,640,768]{3,2,1,0:T(8,128)(2,1)} %get-tuple-elem, ...), custom_call_target="tpu_custom_call" | custom-call | tf_op jit(solution)/shard_map/expert_exchange/pallas_call | solution.py:296
  462.9 0.0 copy-start.9
  462.9 0.0 copy-start.8
  462.9 0.0 copy-start.7
  462.9 4.0 all-to-all-start
  466.9 0.0 copy-done.9
  466.9 0.0 copy-done.8
  466.9 0.6 copy.14
  467.5 0.0 copy-done.7
  467.5 0.1 reduce
  467.7 0.0 copy-start.5
  467.7 18.7 %copy.12 = f32[2,768,3072]{1,2,0:T(8,128)} copy(f32[2,768,3072]{2,1,0:T(8,128)} %get-tuple-element.35) | data formatting | bytes 37748736 | tf_op jit(solution)/shard_map/expert_exchange/pallas_call | solution.py:296
  486.4 0.0 copy-done.5
  486.4 0.6 broadcast_multiply_fusion
  487.0 16.8 %own_copy.1.refs_2_ = f32[2,768,3072]{2,1,0:T(8,128)} custom-call(f32[2,768,3072]{2,1,0:T(8,128)} %get-tuple-element.34.source), custom_call_target="tpu_custom_call" | custom-call | flops 15000000512 | bytes 37748736 | tf_op jit(solution)/shard_map/own_copy/pallas_call | solution.py:672
  503.8 0.0 copy-done.1
  503.8 25.0 %router_side.1 = (bf16[8192,128]{1,0:T(8,128)(2,1)S(1)}, f32[24,768]{1,0:T(8,128)S(1)}, f32[128,768]{1,0:T(8,128)}) custom-call(s32[8192]{0:T(1024)S(1)} %bitcast.12, bf16[8192,768]{1,0:T(8,128)(2,1)} %refs_1_.1, s32[16,512]{1,0:T(8,128)S(1)} %copy-done.2, f32[16,768]{1,0:T(8,128)S(1)} %bitcast.11, f32[16,128]{1,0:T(8,128)S(1)} %get-tuple-element.41.refs_4_, ...), custom_call_target="tpu_custom_call" | custom-call | flops 30000001024 | bytes 16777216 | tf_op jit(solution)/shard_map/router_side/pallas_call | solution.py:539
  528.8 1.3 copy-done
  530.1 0.6 copy-done.3
  530.8 30.9 %device_total.1 = (f32[16,768]{1,0:T(8,128)}, f32[1,1]{1,0:T(1,128)}, f32[1,1]{1,0:T(1,128)}) custom-call(f32[24,768]{1,0:T(8,128)} %copy-done.3, f32[16,128]{1,0:T(8,128)} %get-tuple-element.40.refs_1_, f32[2,768,3072]{2,1,0:T(8,128)} %own_copy.1.refs_2_, f32[2,3072,768]{2,1,0:T(8,128)} %bitcast.13), custom_call_target="tpu_custom_call" | custom-call | tf_op jit(solution)/shard_map/device_total/pallas_call | solution.py:655
  561.6 0.0 all-to-all-done.dlast
  561.7 27.3 %combine_rows.1 = bf16[8192,768]{1,0:T(8,128)(2,1)} custom-call(s32[8192]{0:T(1024)} %bitcast.15, bf16[8192,128]{1,0:T(8,128)(2,1)} %copy-done, f32[16,768]{1,0:T(8,128)} %bitcast.10, bf16[8,1,640,768]{3,2,1,0:T(8,128)(2,1)} %get-tuple-element.32.dback, bf16[8,640,768]{2,1,0:T(8,128)(2,1)} %all-to-all-done.dlast), custom_call_target="tpu_custom_call" | custom-call | tf_op jit(solution)/shard_map/combine_rows/pallas_call | solution.py:612
  588.9 0.6 copy.19
  (10 shorter events, 0.1 us)
Async XLA Ops:
  27.4 25.2 %collective-permute-start = (bf16[640,768]{1,0:T(8,128)(2,1)}, bf16[640,768]{1,0:T(8,128)(2,1)S(1)}, u32[]{:S(2)}, u32[]{:S(2)}) collective-permute-start(bf16[640,768]{1,0:T(8,128)(2,1)} %get-tuple-element.26), channel_id=1, source_target_pairs={{0,2},{1,3},{2,0},{3,1},{4,6},{5,7},{6,4},{7,5}} | collective-permute-start | bytes 2949128 | tf_op jit(solution)/shard_map/ppermute | solution.py:690
  29.5 23.2 %collective-permute-start.1 = (bf16[640,768]{1,0:T(8,128)(2,1)}, bf16[640,768]{1,0:T(8,128)(2,1)}, u32[]{:S(2)}, u32[]{:S(2)}) collective-permute-start(bf16[640,768]{1,0:T(8,128)(2,1)} %get-tuple-element.27), channel_id=1, source_target_pairs={{0,4},{1,5},{2,6},{3,7},{4,0},{5,1},{6,2},{7,3}} | collective-permute-start | bytes 2949128 | tf_op jit(solution)/shard_map/ppermute | solution.py:690
  52.7 0.9 copy-start.4
  462.9 4.0 copy-start.9
  462.9 4.0 copy-start.8
  462.9 4.6 copy-start.7
  462.9 98.7 %all-to-all-start = ((bf16[8,640,768]{2,1,0:T(8,128)(2,1)}), bf16[8,640,768]{2,1,0:T(8,128)(2,1)}, u32[]{:S(2)}, u32[]{:S(2)}) async-start(bf16[8,640,768]{2,1,0:T(8,128)(2,1)} %get-tuple-element.33), calls=%async_computation | async-start | bytes 15728640 | tf_op jit(solution)/shard_map/all_to_all | solution.py:695
  467.7 18.7 %copy-start.5 = (f32[8,16,128]{2,1,0:T(8,128)S(1)}, f32[8,16,128]{2,1,0:T(8,128)}, u32[]{:S(2)}) copy-start(f32[8,16,128]{2,1,0:T(8,128)} %get-tuple-element.29) | copy-start | bytes 196612
  487.0 16.8 %copy-start.1 = (f32[768,16]{0,1:T(8,128)S(1)}, f32[768,16]{0,1:T(8,128)}, u32[]{:S(2)}) copy-start(f32[768,16]{0,1:T(8,128)} %param.7) | copy-start | bytes 147460
  487.0 16.8 %copy-start.2 = (s32[16,512]{1,0:T(8,128)S(1)}, s32[16,512]{1,0:T(8,128)}, u32[]{:S(2)}) copy-start(s32[16,512]{1,0:T(8,128)} %reshape.30.idx.refs_2_) | copy-start | bytes 98308
  528.8 1.3 copy-start
  530.1 0.6 copy-start.3
  561.6 27.3 %copy-start.6 = (f32[16,768]{1,0:T(8,128)S(1)}, f32[16,768]{1,0:T(8,128)}, u32[]{:S(2)}) copy-start(f32[16,768]{1,0:T(8,128)} %get-tuple-element.37) | copy-start | bytes 147460

commit v8 on v7

--- a/solution.py
+++ b/solution.py
@@ -313,12 +313,14 @@
     )(xs, dys, near_x, near_y, w_t, cnt, w_in, w_out)
 
 
-PITCH = 6 * 8
+PITCH = 7 * 8
+STEP = 9
+UNROLL = 128
 ROW_TILES = 6
 
 
 def row(addr, tiles):
-    return pl.ds(addr, tiles, stride=8)
+    return pl.ds(addr, tiles, stride=STEP)
 
 
 TB = 512
@@ -351,22 +353,22 @@
         fetch(b).wait()
         for j in range(ROW_TILES):
             part = inb[b % IN_FLIGHT, :, j * LANES:(j + 1) * LANES].astype(F32)
-            stage3[:, j * 8:(j + 1) * 8, :] = part.reshape(TB // 8, 8, LANES)
+            stage3[:, j * STEP:j * STEP + 8, :] = part.reshape(TB // 8, 8, LANES)
 
         def move(i, _):
-            for r in range(32):
-                at = addr[b * TB + i * 32 + r]
-                table[row(at, ROW_TILES), :] = stage[row(i * (4 * PITCH) + (r // 8) * PITCH + r % 8, ROW_TILES), :]
+            for r in range(UNROLL):
+                at = addr[b * TB + i * UNROLL + r]
+                table[row(at, ROW_TILES), :] = stage[row(i * (UNROLL // 8 * PITCH) + (r // 8) * PITCH + r % 8, ROW_TILES), :]
             return 0
 
-        lax.fori_loop(0, TB // 32, move, 0)
+        lax.fori_loop(0, TB // UNROLL, move, 0)
         return 0
 
     lax.fori_loop(0, n_in, scatter, 0)
 
     def drain(c, _):
         for j in range(ROW_TILES):
-            part = tiled[pl.ds(c * groups, groups), j * 8:(j + 1) * 8, :].reshape(cap, LANES)
+            part = tiled[pl.ds(c * groups, groups), j * STEP:j * STEP + 8, :].reshape(cap, LANES)
             outb[c, :, j * LANES:(j + 1) * LANES] = part.astype(BF16)
         emit(c).start()
         return 0
@@ -484,11 +486,11 @@
         lax.fori_loop(0, n_chunk, fill, 0)
 
     def move(i, _):
-        for r in range(32):
-            g_rows[pl.ds(i * 32 + r, 1), :] = gtab[pl.ds(slot[b * tb + i * 32 + r], 1), :]
+        for r in range(UNROLL):
+            g_rows[pl.ds(i * UNROLL + r, 1), :] = gtab[pl.ds(slot[b * tb + i * UNROLL + r], 1), :]
         return 0
 
-    lax.fori_loop(0, tb // 32, move, 0)
+    lax.fori_loop(0, tb // UNROLL, move, 0)
 
     xv = x[...]
     terms = nt(w_six[...], xv)
@@ -581,7 +583,7 @@
                 fetch(d, e).wait()
                 for j in range(ROW_TILES):
                     part = inb[e, d % n_buf, :, j * LANES:(j + 1) * LANES].astype(F32)
-                    tiled[pl.ds((d * n_local + e) * groups, groups), j * 8:(j + 1) * 8, :] = part.reshape(groups, 8, LANES)
+                    tiled[pl.ds((d * n_local + e) * groups, groups), j * STEP:j * STEP + 8, :] = part.reshape(groups, 8, LANES)
 
                 @pl.when(d + n_buf < n_out)
                 def _():
@@ -591,15 +593,15 @@
         lax.fori_loop(0, n_out, fill, 0)
 
     def move(i, _):
-        for r in range(32):
-            at = addr[b * tb + i * 32 + r]
-            stage[row(i * (4 * PITCH) + (r // 8) * PITCH + r % 8, ROW_TILES), :] = table[row(at, ROW_TILES), :]
+        for r in range(UNROLL):
+            at = addr[b * tb + i * UNROLL + r]
+            stage[row(i * (UNROLL // 8 * PITCH) + (r // 8) * PITCH + r % 8, ROW_TILES), :] = table[row(at, ROW_TILES), :]
         return 0
 
-    lax.fori_loop(0, tb // 32, move, 0)
+    lax.fori_loop(0, tb // UNROLL, move, 0)
     for j in range(ROW_TILES):
         cols = slice(j * LANES, (j + 1) * LANES)
-        grad_x[:, cols] = (stage3[:, j * 8:(j + 1) * 8, :].reshape(tb, LANES) + nn(pieces[...], w_six[:, cols])).astype(BF16)
+        grad_x[:, cols] = (stage3[:, j * STEP:j * STEP + 8, :].reshape(tb, LANES) + nn(pieces[...], w_six[:, cols])).astype(BF16)
 
 
 def combine(addr, pieces, w_t, dback, dlast):

time: 594 us -> 586 us (0.987)
  Pallas kernels: 557 us -> 546 us
  transfers between devices with their start and end apart: 3 -> 3, of which waited for: 0 -> 2; matrix products, arithmetic and copies ran while one was open for 3% -> 3% of each run, Pallas kernels for 16% -> 16%
where the time goes in v8:
time: 586 us; the launch traced here: 584 us
  Pallas kernels  546 us (93%)
  local copies, waits for them, and re-layouts  23.4 us (4%)
  starting transfers between devices  7.23 us (1%)
    pallas_call x1, Pallas kernels, expert_exchange(): pl.pallas_call(lambda *refs: expert_kernel(n_dev, n_local, num_experts, b...  410 us
    pallas_call x1, Pallas kernels, total_over_devices(): pl.pallas_call(lambda *refs: total_kernel(n_dev, total_tok, *refs), out_s...  31.7 us
    pallas_call x1, Pallas kernels, router_side(): pl.pallas_call(lambda *refs: router_kernel(z_coef, *refs), out_shape=(jax...  24.1 us
    pallas_call x1, Pallas kernels, combine(): pl.pallas_call(combine_kernel, out_shape=jax.ShapeDtypeStruct((tokens, d_...  22.9 us
    pallas_call x1, Pallas kernels, route_permute(): pl.pallas_call(route_permute_kernel, out_shape=(jax.ShapeDtypeStruct((n_d...  22.2 us
    pallas_call x1, local copies, waits for them, and re-layouts, expert_exchange(): pl.pallas_call(lambda *refs: expert_kernel(n_dev, n_local, num_experts, b...  18.7 us
    pallas_call x1, Pallas kernels, permute(): pl.pallas_call(permute_kernel, out_shape=jax.ShapeDtypeStruct((n_dev, n_l...  18.6 us
    pallas_call x1, Pallas kernels, own_copy(): pl.pallas_call(copy_kernel, out_shape=jax.ShapeDtypeStruct(a.shape, a.dty...  16.8 us
  transfers between devices with their start and end apart: 3, of which 2 were waited for; matrix products, arithmetic and copies ran while one was open for 3% of the time, Pallas kernels for 16%

profile of v8, /device:TPU:1, one launch (start us, length us, event | category | flops | bytes accessed | tf_op | source)
XLA Modules:
  0.0 584.3 jit_solution(15071938235844059409)
XLA Ops:
  0.6 1.4 reshape.30.idx.refs_2_
  2.0 22.2 %route_permute.1 = (bf16[8,2,640,768]{3,2,1,0:T(8,128)(2,1)}, bf16[640,768]{1,0:T(8,128)(2,1)}, bf16[640,768]{1,0:T(8,128)(2,1)}, s32[16,512]{1,0:T(8,128)}, s32[16,512]{1,0:T(8,128)}, /*index=5*/f32[16,128]{1,0:T(8,128)}) custom-call(s32[16,512]{1,0:T(8,128)} %reshape.30.idx.refs_2_, bf16[8192,768]{1,0:T(8,128)(2,1)} %refs_1_.1), custom_call_target="tpu_custom_call" | custom-call | tf_op jit(solution)/shard_map/route_permute/pallas_call | solution.py:432
  24.2 2.1 collective-permute-start
  26.2 1.2 collective-permute-start.1
  27.5 18.6 %permute_rows.1.refs_1_ = bf16[8,2,640,768]{3,2,1,0:T(8,128)(2,1)} custom-call(s32[16,512]{1,0:T(8,128)} %get-tuple-element.23.table, bf16[8192,768]{1,0:T(8,128)(2,1)} %x.3), custom_call_target="tpu_custom_call" | custom-call | flops 20000000000 | bytes 29360128 | tf_op jit(solution)/shard_map/permute_rows/pallas_call | solution.py:456
  46.1 1.7 collective-permute-done.refs_2_
  47.8 0.9 collective-permute-done.1.refs_3_
  48.7 0.0 copy-done.4
  48.7 409.8 %expert_exchange.1 = (bf16[8,2,640,768]{3,2,1,0:T(8,128)(2,1)}, bf16[8,2,640,768]{3,2,1,0:T(8,128)(2,1)}, bf16[8,1,640,768]{3,2,1,0:T(8,128)(2,1)}, bf16[8,1,640...) custom-call(bf16[8,2,640,768]{3,2,1,0:T(8,128)(2,1)} %get-tuple-elem, ...), custom_call_target="tpu_custom_call" | custom-call | tf_op jit(solution)/shard_map/expert_exchange/pallas_call | solution.py:296
  458.5 0.0 copy-start.9
  458.5 0.0 copy-start.8
  458.5 0.0 copy-start.7
  458.6 3.9 all-to-all-start
  462.5 0.0 copy-done.9
  462.5 0.0 copy-done.8
  462.5 0.6 copy.14
  463.1 0.0 copy-done.7
  463.1 0.1 reduce
  463.3 0.0 copy-start.5
  463.3 18.7 %copy.12 = f32[2,768,3072]{1,2,0:T(8,128)} copy(f32[2,768,3072]{2,1,0:T(8,128)} %get-tuple-element.35) | data formatting | bytes 37748736 | tf_op jit(solution)/shard_map/expert_exchange/pallas_call | solution.py:296
  482.0 0.0 copy-done.5
  482.0 0.6 broadcast_multiply_fusion
  482.6 16.8 %own_copy.1.refs_2_ = f32[2,768,3072]{2,1,0:T(8,128)} custom-call(f32[2,768,3072]{2,1,0:T(8,128)} %get-tuple-element.34.source), custom_call_target="tpu_custom_call" | custom-call | flops 15000000512 | bytes 37748736 | tf_op jit(solution)/shard_map/own_copy/pallas_call | solution.py:674
  499.4 24.1 %router_side.1 = (bf16[8192,128]{1,0:T(8,128)(2,1)S(1)}, f32[24,768]{1,0:T(8,128)S(1)}, f32[128,768]{1,0:T(8,128)}) custom-call(s32[8192]{0:T(1024)S(1)} %bitcast.12, bf16[8192,768]{1,0:T(8,128)(2,1)} %refs_1_.1, s32[16,512]{1,0:T(8,128)S(1)} %copy-done.2, f32[16,768]{1,0:T(8,128)S(1)} %bitcast.11, f32[16,128]{1,0:T(8,128)S(1)} %get-tuple-element.41.refs_4_, ...), custom_call_target="tpu_custom_call" | custom-call | flops 30000001024 | bytes 16777216 | tf_op jit(solution)/shard_map/router_side/pallas_call | solution.py:541
  523.5 1.3 copy-done
  524.9 0.6 copy-done.3
  525.5 31.7 %device_total.1 = (f32[16,768]{1,0:T(8,128)}, f32[1,1]{1,0:T(1,128)}, f32[1,1]{1,0:T(1,128)}) custom-call(f32[24,768]{1,0:T(8,128)} %copy-done.3, f32[16,128]{1,0:T(8,128)} %get-tuple-element.40.refs_1_, f32[2,768,3072]{2,1,0:T(8,128)} %own_copy.1.refs_2_, f32[2,3072,768]{2,1,0:T(8,128)} %bitcast.13), custom_call_target="tpu_custom_call" | custom-call | tf_op jit(solution)/shard_map/device_total/pallas_call | solution.py:657
  557.2 0.0 all-to-all-done.dlast
  557.3 0.0 copy-start.6
  557.3 22.9 %combine_rows.1 = bf16[8192,768]{1,0:T(8,128)(2,1)} custom-call(s32[8192]{0:T(1024)} %bitcast.15, bf16[8192,128]{1,0:T(8,128)(2,1)} %copy-done, f32[16,768]{1,0:T(8,128)} %bitcast.10, bf16[8,1,640,768]{3,2,1,0:T(8,128)(2,1)} %get-tuple-element.32.dback, bf16[8,640,768]{2,1,0:T(8,128)(2,1)} %all-to-all-done.dlast), custom_call_target="tpu_custom_call" | custom-call | tf_op jit(solution)/shard_map/combine_rows/pallas_call | solution.py:614
  580.2 0.0 copy-done.6
  580.2 0.6 copy.19
  (10 shorter events, 0.1 us)
Async XLA Ops:
  24.2 23.6 %collective-permute-start = (bf16[640,768]{1,0:T(8,128)(2,1)}, bf16[640,768]{1,0:T(8,128)(2,1)S(1)}, u32[]{:S(2)}, u32[]{:S(2)}) collective-permute-start(bf16[640,768]{1,0:T(8,128)(2,1)} %get-tuple-element.26), channel_id=1, source_target_pairs={{0,2},{1,3},{2,0},{3,1},{4,6},{5,7},{6,4},{7,5}} | collective-permute-start | bytes 2949128 | tf_op jit(solution)/shard_map/ppermute | solution.py:692
  26.2 22.5 %collective-permute-start.1 = (bf16[640,768]{1,0:T(8,128)(2,1)}, bf16[640,768]{1,0:T(8,128)(2,1)}, u32[]{:S(2)}, u32[]{:S(2)}) collective-permute-start(bf16[640,768]{1,0:T(8,128)(2,1)} %get-tuple-element.27), channel_id=1, source_target_pairs={{0,4},{1,5},{2,6},{3,7},{4,0},{5,1},{6,2},{7,3}} | collective-permute-start | bytes 2949128 | tf_op jit(solution)/shard_map/ppermute | solution.py:692
  47.8 0.9 copy-start.4
  458.5 4.0 copy-start.9
  458.5 4.0 copy-start.8
  458.5 4.6 copy-start.7
  458.6 98.7 %all-to-all-start = ((bf16[8,640,768]{2,1,0:T(8,128)(2,1)}), bf16[8,640,768]{2,1,0:T(8,128)(2,1)}, u32[]{:S(2)}, u32[]{:S(2)}) async-start(bf16[8,640,768]{2,1,0:T(8,128)(2,1)} %get-tuple-element.33), calls=%async_computation | async-start | bytes 15728640 | tf_op jit(solution)/shard_map/all_to_all | solution.py:697
  463.3 18.7 %copy-start.5 = (f32[8,16,128]{2,1,0:T(8,128)S(1)}, f32[8,16,128]{2,1,0:T(8,128)}, u32[]{:S(2)}) copy-start(f32[8,16,128]{2,1,0:T(8,128)} %get-tuple-element.29) | copy-start | bytes 196612
  482.6 16.8 %copy-start.1 = (f32[768,16]{0,1:T(8,128)S(1)}, f32[768,16]{0,1:T(8,128)}, u32[]{:S(2)}) copy-start(f32[768,16]{0,1:T(8,128)} %param.7) | copy-start | bytes 147460
  482.6 16.8 %copy-start.2 = (s32[16,512]{1,0:T(8,128)S(1)}, s32[16,512]{1,0:T(8,128)}, u32[]{:S(2)}) copy-start(s32[16,512]{1,0:T(8,128)} %reshape.30.idx.refs_2_) | copy-start | bytes 98308
  523.5 1.3 copy-start
  524.9 0.6 copy-start.3
  557.3 22.9 %copy-start.6 = (f32[16,768]{1,0:T(8,128)S(1)}, f32[16,768]{1,0:T(8,128)}, u32[]{:S(2)}) copy-start(f32[16,768]{1,0:T(8,128)} %get-tuple-element.37) | copy-start | bytes 147460
